TPU v7x, 32 devices: a whole 2x2x4 slice. The times are simulated.
32 devices in a mesh: groups: 2 (over y), dp: 4 (over z), section: 2 (over x), tensor: 2 (over core).
Axes of the slice: x: 2, y: 2, z: 4, core: 2. Of those that a mesh axis runs over, the one named last changes fastest.
Arguments:
- hidden: bfloat16 [128, 8, 5120], P(('groups', 'dp')), parts along dimension 0, may hold values from -6 to 6
- unembed: bfloat16 [128, 8, 5120], P(('groups', 'dp')), parts along dimension 0, may hold values from -0.02734375 to 0.02734375
- value_proj: bfloat16 [2, 5120, 512], P('section', 'dp', 'tensor'), may hold values from -0.078125 to 0.078125
- output_proj: bfloat16 [2, 512, 5120], P('section', 'tensor', 'dp'), may hold values from -0.125 to 0.125
- norm_gains: float32 [2, 5120], P('section'), may hold values from 0.1 to 1.9
- survive: int32 [8], P(('groups', 'dp')), parts along dimension 0, may hold values from 0 to 1, as said below
- lengths: int32 [128], P(('groups', 'dp')), parts along dimension 0, may hold values from 1 to 8
- assign: int32 [128], P(('groups', 'dp')), parts along dimension 0, may hold values from 0 to 16, as said below
- advantage: float32 [128], P(('groups', 'dp')), parts along dimension 0, may hold values from -4 to 4
- reference_logit: float32 [128, 8], P(('groups', 'dp')), parts along dimension 0, may hold values from -4 to 4
- recorded_gap: float32 [128, 8], P(('groups', 'dp')), parts along dimension 0, may hold values from -2 to 2
Outputs:
- grad_value: float32 [4, 5120, 512], P(('groups', 'section'), 'dp', 'tensor'), parts along dimension 0
- grad_output: float32 [4, 512, 5120], P(('groups', 'section'), 'tensor', 'dp'), parts along dimension 0
There are 2 independent parts, one for each index of `groups`. A program takes and returns all parts, laid end to end along the dimension named above; an argument that names none is the same for every part. Nothing has to cross between parts.
Inputs may be any that keep to these rules, and one draw needn't show every extreme that they name: `survive`: 1 where the group of 16 responses is kept, 0 where it is dropped; in every draw all groups of some dp index are kept. `assign`: the 16 slots of a dp index list the local positions (0 to 15) of the responses of its kept groups, each exactly once, then hold 16 in every other slot.
All inputs are finite; a program needn't handle non-finite values.
Results may differ from a plain program's by a relative error of at most 0.029.
Values may be sent and summed in bfloat16 or wider, within the bound.
No kernel may reach another device: no remote copies, remote signals or barrier semaphores. Data moves between devices by JAX's collectives and lax.ppermute only.
A program may use at most 64 MiB of HBM per device.

v0:
```python
import math

import jax
import jax.numpy as jnp
from jax import lax
from jax.sharding import PartitionSpec as P

GROUP = 16
MB_RESP = 8


eps_norm = 1e-06
loss_scale = 4096.0
clip_high = math.log(1.28)
clip_low = math.log(0.8)


def from_behind(block, axis, distance):
    devices = range(lax.axis_size(axis))
    route = [(i - distance, i) for i in devices if i - distance in devices]
    return lax.ppermute(block, axis, route)


def norm_forward(row_block, norm_gain):
    values = row_block.astype(jnp.float32)
    inverse = lax.rsqrt(jnp.mean(values * values, axis=-1, keepdims=True) + eps_norm)
    return (values, inverse, (values * inverse * norm_gain).astype(jnp.bfloat16))


def norm_backward(values, inverse, norm_gain, upstream):
    scaled = upstream * norm_gain
    inner_sum = jnp.sum(scaled * values, axis=-1, keepdims=True) / values.shape[-1]
    return inverse * scaled - values * (inverse * inverse * inverse) * inner_sum


def contract_last(left_rows, right_rows):
    return lax.dot_general(
        left_rows, right_rows, (((1,), (1,)), ((), ())), preferred_element_type=jnp.float32
    )


def contract_first(left_rows, right_rows):
    return lax.dot_general(
        left_rows, right_rows, (((0,), (0,)), ((), ())), preferred_element_type=jnp.float32
    )


def take_slot(slot_store, slot_index):
    return lax.dynamic_index_in_dim(slot_store, slot_index, 0, keepdims=False)


def put_slot(slot_store, new_value, slot_index, active):
    previous = take_slot(slot_store, slot_index)
    return lax.dynamic_update_index_in_dim(
        slot_store, jnp.where(active, new_value, previous), slot_index, 0
    )


def local(
    hidden,
    unembed,
    value_proj,
    output_proj,
    norm_gains,
    survive,
    lengths,
    assign,
    advantage,
    reference_logit,
    recorded_gap,
):
    resp_count = hidden.shape[0]
    positions = hidden.shape[1]
    model_width = hidden.shape[2]
    half_value = value_proj.shape[2]
    micro_count = resp_count // MB_RESP
    row_count = MB_RESP * positions
    section_count = lax.axis_size("section")
    section_index = lax.axis_index("section")
    is_last = section_index == section_count - 1
    norm_gain = norm_gains[0]
    alive_mask = jnp.repeat(survive, GROUP)
    local_count = jnp.sum((alive_mask * lengths).astype(jnp.float32))
    gathered_value, gathered_output = (
        lax.all_gather(value_proj, "dp", axis=1, tiled=True),
        lax.all_gather(output_proj, "dp", axis=2, tiled=True),
    )
    w_first = gathered_value[0]
    w_second = gathered_output[0]

    def pick(array):
        return jnp.take(array, assign, axis=0, mode="fill", fill_value=0)

    slot_hidden = pick(hidden).reshape(micro_count, row_count, model_width)
    slot_unembed = pick(unembed).reshape(micro_count, row_count, model_width)
    position_index = lax.broadcasted_iota(jnp.int32, (resp_count, positions), 1)
    live_mask = (position_index < pick(lengths)[:, None]).astype(jnp.float32)
    advantages = jnp.broadcast_to(pick(advantage)[:, None], (resp_count, positions))
    gap_rows = pick(recorded_gap)
    clipped = (advantages > 0) & (gap_rows > clip_high) | (advantages < 0) & (gap_rows < clip_low)
    kept_mask = 1.0 - clipped.astype(jnp.float32)
    weight_rows = (-loss_scale * advantages * kept_mask * live_mask).reshape(micro_count, row_count)
    logit_base = pick(reference_logit).reshape(micro_count, row_count)
    step_count = micro_count + section_count - 1
    store_in = jnp.zeros((micro_count, row_count, model_width), jnp.bfloat16)
    store_normed = jnp.zeros((micro_count, row_count, model_width), jnp.bfloat16)
    store_projected = jnp.zeros((micro_count, row_count, half_value), jnp.bfloat16)
    store_out = jnp.zeros((micro_count, row_count, model_width), jnp.bfloat16)
    arriving = jnp.zeros((row_count, model_width), jnp.bfloat16)
    for step_index in range(step_count):
        micro_index = step_index - section_index
        active = (micro_index >= 0) & (micro_index < micro_count)
        clamped = jnp.clip(micro_index, 0, micro_count - 1)
        entering = jnp.where(section_index == 0, take_slot(slot_hidden, clamped), arriving)
        values, inverse, normed = norm_forward(entering, norm_gain)
        projected = jnp.dot(normed, w_first, preferred_element_type=jnp.float32).astype(
            jnp.bfloat16
        )
        partial_out = jnp.dot(projected, w_second, preferred_element_type=jnp.float32)
        mixed_sum = lax.psum(partial_out.astype(jnp.bfloat16), "tensor").astype(jnp.float32)
        leaving = (values + mixed_sum).astype(jnp.bfloat16)
        store_in = put_slot(store_in, entering, clamped, active)
        store_normed = put_slot(store_normed, normed, clamped, active)
        store_projected = put_slot(store_projected, projected, clamped, active)
        store_out = put_slot(store_out, leaving, clamped, active)
        arriving = from_behind(leaving, "section", 1)
    store_upstream = jnp.zeros((micro_count, row_count, model_width), jnp.bfloat16)
    store_grad_value = jnp.zeros((micro_count, row_count, half_value), jnp.bfloat16)
    arriving = jnp.zeros((row_count, model_width), jnp.bfloat16)
    for step_index in range(step_count):
        micro_index = step_index - (section_count - 1 - section_index)
        active = (micro_index >= 0) & (micro_index < micro_count)
        clamped = jnp.clip(micro_index, 0, micro_count - 1)
        top_rows = take_slot(store_out, clamped).astype(jnp.float32)
        unembed_rows = take_slot(slot_unembed, clamped).astype(jnp.float32)
        logit = jnp.sum(top_rows * unembed_rows, axis=-1)
        seed_rows = take_slot(weight_rows, clamped) * jnp.exp(
            logit - take_slot(logit_base, clamped)
        )
        start_grad = (seed_rows[:, None] * unembed_rows).astype(jnp.bfloat16)
        upstream = jnp.where(is_last, start_grad, arriving)
        entering = take_slot(store_in, clamped)
        normed = take_slot(store_normed, clamped)
        projected = take_slot(store_projected, clamped)
        grad_projected = contract_last(upstream, w_second).astype(jnp.bfloat16)
        partial_norm = contract_last(grad_projected, w_first)
        grad_normed = lax.psum(partial_norm.astype(jnp.bfloat16), "tensor").astype(jnp.float32)
        values, inverse, unused_normed = norm_forward(entering, norm_gain)
        grad_entering = (
            upstream.astype(jnp.float32) + norm_backward(values, inverse, norm_gain, grad_normed)
        ).astype(jnp.bfloat16)
        store_upstream = put_slot(store_upstream, upstream, clamped, active)
        store_grad_value = put_slot(store_grad_value, grad_projected, clamped, active)
        arriving = from_behind(grad_entering, "section", -1)
    flat_normed = store_normed.reshape(micro_count * row_count, model_width)
    flat_upstream = store_upstream.reshape(micro_count * row_count, model_width)
    flat_grad_value = store_grad_value.reshape(micro_count * row_count, half_value)
    flat_projected = store_projected.reshape(micro_count * row_count, half_value)
    reduced = lax.psum_scatter(
        jnp.concatenate(
            [
                contract_first(flat_normed, flat_grad_value),
                contract_first(flat_upstream, flat_projected),
            ],
            axis=1,
        ).astype(jnp.bfloat16),
        "dp",
        scatter_dimension=0,
        tiled=True,
    ).astype(jnp.float32)
    token_total = lax.psum(local_count, "dp")
    scaled_grads = reduced / token_total
    grad_value = scaled_grads[:, :half_value][None]
    grad_output = scaled_grads[:, half_value:].T[None]
    return (grad_value, grad_output)


def solution(mesh):
    placed = (
        P(("groups", "dp"), None, None),
        P(("groups", "dp"), None, None),
        P("section", "dp", "tensor"),
        P("section", "tensor", "dp"),
        P("section", None),
        P(("groups", "dp")),
        P(("groups", "dp")),
        P(("groups", "dp")),
        P(("groups", "dp")),
        P(("groups", "dp"), None),
        P(("groups", "dp"), None),
    )
    return jax.shard_map(
        local,
        mesh=mesh,
        in_specs=placed,
        out_specs=(
            P(("groups", "section"), "dp", "tensor"),
            P(("groups", "section"), "tensor", "dp"),
        ),
        check_vma=False,
    )
```

profile of v0, /device:TPU:0, one launch (start us, length us, event | category | flops | bytes accessed | tf_op | source)
XLA Modules:
  0.0 449.3 jit_solution(629598408572374933)
XLA Ops:
  9.5 1.7 gather_fusion.2
  11.2 1.7 gather_fusion.4
  14.8 2.0 broadcast_select_fusion.1
  18.2 48.9 %all-gather.3.cloned.1.call-done = bf16[1,5120,256]{2,1,0:T(8,128)(2,1)} async-done(((bf16[1,1280,256]{2,1,0:T(8,128)(2,1)}), bf16[1,5120,256]{2,1,0:T(8,128)(2,1)}) %all-gather.3.cloned.1.call-update) | async-done | bytes 2621456 | tf_op jit(solution)/shard_map/all_gather | solution.py:85
  67.1 2.6 bitcast_dynamic-update-slice_fusion.10
  69.7 52.5 %all-gather.5.cloned.1.call-done = bf16[1,256,5120]{2,1,0:T(8,128)(2,1)} async-done(((bf16[1,256,1280]{2,1,0:T(8,128)(2,1)}), bf16[1,256,5120]{2,1,0:T(8,128)(2,1)}) %all-gather.5.cloned.1.call-update) | async-done | bytes 2621456 | tf_op jit(solution)/shard_map/all_gather | solution.py:86
  122.2 3.2 convolution_convert_fusion.4
  125.7 1.2 broadcast.209.clone
  128.5 14.6 %all-reduce.6.cloned.1.call-done = bf16[64,5120]{1,0:T(8,128)(2,1)} async-done(((bf16[64,5120]{1,0:T(8,128)(2,1)}), bf16[64,5120]{1,0:T(8,128)(2,1)}) %all-reduce.6.cloned.1.call-update) | async-done | bytes 655376 | tf_op jit(solution)/shard_map/psum | solution.py:120
  143.2 1.2 copy-done.14
  144.4 1.4 bitcast_dynamic-update-slice_fusion.5
  145.8 3.7 collective-permute-start
  150.7 13.2 %collective-permute-done = bf16[64,5120]{1,0:T(8,128)(2,1)S(1)} collective-permute-done((bf16[64,5120]{1,0:T(8,128)(2,1)S(1)}, bf16[64,5120]{1,0:T(8,128)(2,1)S(1)}, u32[]{:S(2)}, u32[]{:S(2)}) %collective-permute-start) | collective-permute-done | bytes 655392 | tf_op jit(solution)/shard_map/ppermute | solution.py:21
  167.0 1.5 convolution_convert_fusion.3
  168.6 2.0 constant_dynamic-slice_fusion.14
  170.6 2.0 constant_dynamic-slice_fusion.8
  172.6 16.8 %all-reduce.8.cloned.1.call-done = bf16[64,5120]{1,0:T(8,128)(2,1)} async-done(((bf16[64,5120]{1,0:T(8,128)(2,1)}), bf16[64,5120]{1,0:T(8,128)(2,1)}) %all-reduce.8.cloned.1.call-update) | async-done | bytes 655376 | tf_op jit(solution)/shard_map/psum | solution.py:120
  189.4 2.5 bitcast_dynamic-update-slice_fusion.4
  191.9 3.7 collective-permute-start.1
  195.6 2.2 constant_dynamic-slice_fusion.13
  197.8 12.1 %collective-permute-done.1 = bf16[64,5120]{1,0:T(8,128)(2,1)S(1)} collective-permute-done((bf16[64,5120]{1,0:T(8,128)(2,1)S(1)}, bf16[64,5120]{1,0:T(8,128)(2,1)S(1)}, u32[]{:S(2)}, u32[]{:S(2)}) %collective-permute-start.1) | collective-permute-done | bytes 655392 | tf_op jit(solution)/shard_map/ppermute | solution.py:21
  210.1 1.4 bitcast_dynamic-update-slice_fusion.2
  213.9 1.4 convolution_convert_fusion.2
  215.4 1.2 constant_dynamic-slice_fusion.17
  219.3 17.0 %all-reduce.10.cloned.1.call-done = bf16[64,5120]{1,0:T(8,128)(2,1)} async-done(((bf16[64,5120]{1,0:T(8,128)(2,1)}), bf16[64,5120]{1,0:T(8,128)(2,1)}) %all-reduce.10.cloned.1.call-update) | async-done | bytes 655376 | tf_op jit(solution)/shard_map/psum | solution.py:120
  236.2 3.1 bitcast_dynamic-update-slice_fusion.6
  239.3 2.4 fusion.32
  243.5 1.7 convolution_convert_fusion.1
  247.6 17.8 %all-reduce.12.cloned.1.call-done = bf16[64,5120]{1,0:T(8,128)(2,1)} async-done(((bf16[64,5120]{1,0:T(8,128)(2,1)}), bf16[64,5120]{1,0:T(8,128)(2,1)}) %all-reduce.12.cloned.1.call-update) | async-done | bytes 655376 | tf_op jit(solution)/shard_map/psum | solution.py:147
  265.4 2.1 fusion.48
  267.6 1.6 fusion.46
  269.2 1.5 collective-permute-start.2
  271.8 16.1 %collective-permute-done.2 = bf16[64,5120]{1,0:T(8,128)(2,1)S(1)} collective-permute-done((bf16[64,5120]{1,0:T(8,128)(2,1)S(1)}, bf16[64,5120]{1,0:T(8,128)(2,1)S(1)}, u32[]{:S(2)}, u32[]{:S(2)}) %collective-permute-start.2) | collective-permute-done | bytes 655392 | tf_op jit(solution)/shard_map/ppermute | solution.py:21
  288.0 1.2 bitcast_dynamic-update-slice_fusion.1
  291.7 1.7 convolution_convert_fusion
  293.5 19.2 %all-reduce.14.cloned.1.call-done = bf16[64,5120]{1,0:T(8,128)(2,1)} async-done(((bf16[64,5120]{1,0:T(8,128)(2,1)}), bf16[64,5120]{1,0:T(8,128)(2,1)}) %all-reduce.14.cloned.1.call-update) | async-done | bytes 655376 | tf_op jit(solution)/shard_map/psum | solution.py:147
  312.7 1.7 fusion.53
  314.4 1.7 fusion.52
  316.1 1.3 collective-permute-start.3
  318.6 16.3 %collective-permute-done.3 = bf16[64,5120]{1,0:T(8,128)(2,1)S(1)} collective-permute-done((bf16[64,5120]{1,0:T(8,128)(2,1)S(1)}, bf16[64,5120]{1,0:T(8,128)(2,1)S(1)}, u32[]{:S(2)}, u32[]{:S(2)}) %collective-permute-start.3) | collective-permute-done | bytes 655392 | tf_op jit(solution)/shard_map/ppermute | solution.py:21
  337.1 1.2 bitcast_dynamic-update-slice_fusion
  338.3 2.2 fusion.1
  340.5 2.7 pad_maximum_fusion
  344.5 12.9 %psum.47 = f32[]{:T(128)} all-reduce(f32[]{:T(128)} %convert_reduce_fusion), channel_id=1, replica_groups=mesh['groups'=2,'dp'=4,'section'=2,'tensor'=2] {'dp'}, use_global_device_ids=true, to_apply=%region_17.20 | all-reduce | flops 1 | bytes 8 | tf_op jit(solution)/shard_map/psum | solution.py:171
  357.4 80.2 %reduce-scatter.2.cloned.1.call-done = bf16[1280,512]{0,1:T(8,128)(2,1)} async-done(((bf16[5120,512]{0,1:T(8,128)(2,1)}), bf16[1280,512]{0,1:T(8,128)(2,1)}) %reduce-scatter.2.cloned.1.call-update) | async-done | bytes 1310736 | tf_op jit(solution)/shard_map/reduce_scatter | solution.py:159
  437.6 2.2 convert_divide_fusion
  439.7 1.2 slice_bitcast_fusion
  441.0 1.5 copy.18
  (126 shorter events, 28.8 us)
Async XLA Ops:
  7.2 2.3 copy-start
  7.2 1.6 copy-start.30
  7.2 1.6 copy-start.1
  7.2 59.9 %all-gather.3.cloned.1.call-start = ((), (), s32[]{:S(2)}) async-start(), calls=%async_computation.1 | async-start | bytes 3276800 | tf_op jit(solution)/shard_map/all_gather | solution.py:85
  7.9 114.3 %all-gather.5.cloned.1.call-start = ((), (), s32[]{:S(2)}) async-start(), calls=%async_computation.2 | async-start | bytes 3276800 | tf_op jit(solution)/shard_map/all_gather | solution.py:86
  8.7 134.4 %all-reduce.6.cloned.1.call-start = ((), (), s32[]{:S(2)}) async-start(), calls=%async_computation.3 | async-start | bytes 1310720 | tf_op jit(solution)/shard_map/psum | solution.py:120
  9.5 1.7 copy-start.27
  11.2 1.7 copy-start.2
  11.2 2.4 copy-start.28
  11.2 3.0 copy-start.29
  14.8 52.3 %copy-start.26 = (f32[1,5120]{1,0:T(1,128)S(1)}, f32[1,5120]{1,0:T(1,128)}, u32[]{:S(2)}) copy-start(f32[1,5120]{1,0:T(1,128)} %param.19) | copy-start | bytes 61444
  16.8 1.1 copy-start.12
  125.4 64.0 %all-reduce.8.cloned.1.call-start = ((), (), s32[]{:S(2)}) async-start(), calls=%async_computation.4 | async-start | bytes 1310720 | tf_op jit(solution)/shard_map/psum | solution.py:120
  125.7 1.8 copy-start.13
  143.1 1.3 copy-start.14
  145.8 4.9 %copy-start.20 = (bf16[2,64,5120]{2,1,0:T(8,128)(2,1)}, bf16[2,64,5120]{2,1,0:T(8,128)(2,1)S(1)}, u32[]{:S(2)}) copy-start(bf16[2,64,5120]{2,1,0:T(8,128)(2,1)S(1)} %get-tuple-element.22) | copy-start | bytes 3932164
  145.8 18.1 %collective-permute-start = (bf16[64,5120]{1,0:T(8,128)(2,1)S(1)}, bf16[64,5120]{1,0:T(8,128)(2,1)S(1)}, u32[]{:S(2)}, u32[]{:S(2)}) collective-permute-start(bf16[64,5120]{1,0:T(8,128)(2,1)S(1)} %get-tuple-element.23), channel_id=1, source_target_pairs={{0,2},{1,3},{4,6},{5,7},{8,10},{9,11},{12,14},{13,15},{16,18},{17,... | collective-permute-start | bytes 1966088 | tf_op jit(solution)/shard_map/ppermute | solution.py:21
  150.7 14.6 %copy-start.8 = (bf16[1,5120,256]{2,1,0:T(8,128)(2,1)S(1)}, bf16[1,5120,256]{2,1,0:T(8,128)(2,1)}, u32[]{:S(2)}) copy-start(bf16[1,5120,256]{2,1,0:T(8,128)(2,1)} %all-gather.3.cloned.1.call-done) | copy-start | bytes 7864324
  165.3 1.7 copy-start.3
  168.5 67.7 %all-reduce.10.cloned.1.call-start = ((), (), s32[]{:S(2)}) async-start(), calls=%async_computation.5 | async-start | bytes 1310720 | tf_op jit(solution)/shard_map/psum | solution.py:120
  191.9 18.1 %collective-permute-start.1 = (bf16[64,5120]{1,0:T(8,128)(2,1)S(1)}, bf16[64,5120]{1,0:T(8,128)(2,1)S(1)}, u32[]{:S(2)}, u32[]{:S(2)}) collective-permute-start(bf16[64,5120]{1,0:T(8,128)(2,1)S(1)} %get-tuple-element.21), channel_id=1, source_target_pairs={{0,2},{1,3},{4,6},{5,7},{8,10},{9,11},{12,14},{13,15},{16,18},{17,... | collective-permute-start | bytes 1966088 | tf_op jit(solution)/shard_map/ppermute | solution.py:21
  195.6 14.5 %copy-start.15 = (bf16[16,8,5120]{2,1,0:T(8,128)(2,1)S(1)}, bf16[16,8,5120]{2,1,0:T(8,128)(2,1)}, u32[]{:S(2)}) copy-start(bf16[16,8,5120]{2,1,0:T(8,128)(2,1)} %copy-done.12) | copy-start | bytes 3932164
  195.6 14.5 %copy-start.25 = (bf16[1,64,5120]{2,1,0:T(8,128)(2,1)S(1)}, bf16[1,64,5120]{2,1,0:T(8,128)(2,1)}, u32[]{:S(2)}) copy-start(bf16[1,64,5120]{2,1,0:T(8,128)(2,1)} %constant_dynamic-slice_fusion.8) | copy-start | bytes 1966084
  210.1 2.0 copy-start.9
  211.5 1.2 copy-start.16
  211.5 1.3 copy-start.21
  212.0 1.9 copy-start.4
  215.4 50.0 %all-reduce.12.cloned.1.call-start = ((), (), s32[]{:S(2)}) async-start(), calls=%async_computation.6 | async-start | bytes 1310720 | tf_op jit(solution)/shard_map/psum | solution.py:147
  215.4 1.5 copy-start.17
  217.3 1.1 copy-start.18
  218.4 17.8 %copy-start.22 = (bf16[64,5120]{1,0:T(8,128)(2,1)S(1)}, bf16[64,5120]{1,0:T(8,128)(2,1)}, u32[]{:S(2)}) copy-start(bf16[64,5120]{1,0:T(8,128)(2,1)} %copy-done.21) | copy-start | bytes 1966084
  239.3 2.4 copy-start.5
  241.8 1.7 copy-start.10
  245.3 67.4 %all-reduce.14.cloned.1.call-start = ((), (), s32[]{:S(2)}) async-start(), calls=%async_computation.7 | async-start | bytes 1310720 | tf_op jit(solution)/shard_map/psum | solution.py:147
  265.4 2.1 copy-start.24
  269.2 18.8 %collective-permute-start.2 = (bf16[64,5120]{1,0:T(8,128)(2,1)S(1)}, bf16[64,5120]{1,0:T(8,128)(2,1)S(1)}, u32[]{:S(2)}, u32[]{:S(2)}) collective-permute-start(bf16[64,5120]{1,0:T(8,128)(2,1)S(1)} %fusion.46), channel_id=1, source_target_pairs={{2,0},{3,1},{6,4},{7,5},{10,8},{11,9},{14,12},{15,13},{18,16},{19,... | collective-permute-start | bytes 1966088 | tf_op jit(solution)/shard_map/ppermute | solution.py:21
  288.0 2.0 copy-start.6
  290.0 1.7 copy-start.11
  293.5 144.1 %reduce-scatter.2.cloned.1.call-start = ((), (), s32[]{:S(2)}) async-start(), calls=%async_computation.8 | async-start | bytes 6553600 | tf_op jit(solution)/shard_map/reduce_scatter | solution.py:159
  312.7 1.7 copy-start.23
  314.4 20.5 %copy-start.7 = (bf16[1,256,5120]{2,1,0:T(8,128)(2,1)S(1)}, bf16[1,256,5120]{2,1,0:T(8,128)(2,1)}, u32[]{:S(2)}) copy-start(bf16[1,256,5120]{2,1,0:T(8,128)(2,1)} %all-gather.5.cloned.1.call-done) | copy-start | bytes 7864324
  316.1 18.8 %collective-permute-start.3 = (bf16[64,5120]{1,0:T(8,128)(2,1)S(1)}, bf16[64,5120]{1,0:T(8,128)(2,1)S(1)}, u32[]{:S(2)}, u32[]{:S(2)}) collective-permute-start(bf16[64,5120]{1,0:T(8,128)(2,1)S(1)} %fusion.52), channel_id=1, source_target_pairs={{2,0},{3,1},{6,4},{7,5},{10,8},{11,9},{14,12},{15,13},{18,16},{19,... | collective-permute-start | bytes 1966088 | tf_op jit(solution)/shard_map/ppermute | solution.py:21
  334.9 1.3 copy-start.19
Sparse Core Ops, SparseCore 0:
  9.6 57.4 all-gather.2
  68.6 53.4 all-gather.4
  125.5 17.5 all-reduce.5
  168.6 20.6 all-reduce.7
  215.5 20.6 all-reduce.9
  245.4 19.9 all-reduce.11
  293.6 19.0 all-reduce.13
  343.3 94.1 reduce-scatter.1
where the time goes:
time: 450 us; the launch traced here: 449 us
  waiting for transfers between devices  326 us (72%)
  local copies, waits for them, and re-layouts  32.9 us (7%)
  other arithmetic  32.2 us (7%)
  matrix products  19.3 us (4%)
  between operations  15.3 us (3%)
  blocking collectives  12.9 us (3%)
  starting transfers between devices  10.5 us (2%)
    reduce_scatter x1, waiting for transfers between devices, local(): lax.psum_scatter(jnp.concatenate([contract_first(flat_normed, flat_grad_v...  80.2 us
    ppermute x4, waiting for transfers between devices, from_behind(): return lax.ppermute(block, axis, route)  57.8 us
    all_gather x1, waiting for transfers between devices, local(): lax.all_gather(output_proj, 'dp', axis=2, tiled=True)  52.5 us
    all_gather x1, waiting for transfers between devices, local(): lax.all_gather(value_proj, 'dp', axis=1, tiled=True)  48.9 us
    psum x3, waiting for transfers between devices, local(): lax.psum(partial_out.astype(jnp.bfloat16), 'tensor').astype(jnp.float32)  48.4 us
    psum x2, waiting for transfers between devices, local(): lax.psum(partial_norm.astype(jnp.bfloat16), 'tensor').astype(jnp.float32)  37 us
    dynamic_update_slice x10, other arithmetic, put_slot(): lax.dynamic_update_index_in_dim(slot_store, jnp.where(active, new_value,...  14.3 us
    psum x1, blocking collectives, local(): token_total = lax.psum(local_count, 'dp')  12.9 us
  transfers between devices with their start and end apart: 12, of which 12 were waited for; matrix products, arithmetic and copies ran while one was open for 6% of the time, Pallas kernels for 0%

commit v1 on v0

--- a/solution.py
+++ b/solution.py
@@ -56,7 +56,7 @@
     )
 
 
-def local(
+def general(
     hidden,
     unembed,
     value_proj,
@@ -175,6 +175,200 @@
     return (grad_value, grad_output)
 
 
+def rotate(block, axis, distance):
+    count = lax.axis_size(axis)
+    return lax.ppermute(block, axis, [(i, (i + distance) % count) for i in range(count)])
+
+
+def swap(block, axis):
+    return rotate(block, axis, 1)
+
+
+def low_rank(
+    hidden,
+    unembed,
+    value_proj,
+    output_proj,
+    norm_gains,
+    survive,
+    lengths,
+    assign,
+    advantage,
+    reference_logit,
+    recorded_gap,
+):
+    f32, bf16 = jnp.float32, jnp.bfloat16
+    resp_count, positions, model_width = hidden.shape
+    _, own_width, half_value = value_proj.shape
+    dp_count, group_count = lax.axis_size("dp"), lax.axis_size("groups")
+    dp_index, group_index = lax.axis_index("dp"), lax.axis_index("groups")
+    tensor_index = lax.axis_index("tensor")
+    first = lax.axis_index("section") == 0
+    half_resp = resp_count // 2
+    half_rows = half_resp * positions
+    shifts = range(1, dp_count)
+
+    def my_half(array):
+        return lax.dynamic_slice_in_dim(array, tensor_index * half_resp, half_resp, 0)
+
+    def columns(array, index):
+        return lax.dynamic_slice_in_dim(array, index * own_width, own_width, array.ndim - 1)
+
+    gain = columns(norm_gains[0], dp_index)
+    a_own = (value_proj[0].astype(f32) * gain[:, None]).astype(bf16).T
+    b_own = output_proj[0]
+    hid_half = my_half(hidden).reshape(half_rows, model_width)
+    un_half = my_half(unembed).reshape(half_rows, model_width)
+    moved = jnp.where(first, hid_half, un_half)
+    arrived = [columns(moved, dp_index)]
+    for d in shifts:
+        arrived.append(rotate(columns(moved, (dp_index + d) % dp_count), "dp", d))
+    c_own = swap(jnp.where(first, b_own, a_own), "section")
+    ab_other = swap(jnp.concatenate([a_own, b_own]), "tensor")
+    a_all = jnp.concatenate([a_own, ab_other[:half_value]])
+    b_all = jnp.concatenate([b_own, ab_other[half_value:]])
+    c_all = jnp.concatenate([c_own, swap(c_own, "tensor")])
+
+    part_rows = half_value // group_count
+    block_rows = part_rows // dp_count
+    left = lax.dynamic_slice_in_dim(
+        jnp.where(first, b_own, c_own), group_index * part_rows, part_rows, 0
+    )
+    part = contract_last(left, jnp.where(first, b_all, a_all))
+
+    def part_block(index):
+        return lax.dynamic_slice_in_dim(part, index * block_rows, block_rows, 0)
+
+    total = part_block(dp_index)
+    for d in shifts:
+        total = total + rotate(
+            part_block((dp_index + d) % dp_count).astype(bf16), "dp", d
+        ).astype(f32)
+    total = total.astype(bf16)
+    product = jnp.zeros((part_rows, 2 * half_value), bf16)
+    product = lax.dynamic_update_slice_in_dim(product, total, dp_index * block_rows, 0)
+    for d in shifts:
+        product = lax.dynamic_update_slice_in_dim(
+            product, rotate(total, "dp", d), (dp_index - d) % dp_count * block_rows, 0
+        )
+    grown = jnp.zeros((half_value, 2 * half_value), bf16)
+    grown = lax.dynamic_update_slice_in_dim(grown, product, group_index * part_rows, 0)
+    for d in range(1, group_count):
+        grown = lax.dynamic_update_slice_in_dim(
+            grown,
+            rotate(product, "groups", d),
+            (group_index - d) % group_count * part_rows,
+            0,
+        )
+    across = swap(grown, "section")
+    both = jnp.concatenate([jnp.where(first, grown, across), jnp.where(first, across, grown)])
+    both_other = swap(both, "tensor")
+    both_other = jnp.concatenate([both_other[:, half_value:], both_other[:, :half_value]], axis=1)
+    gram = jnp.concatenate([both[:half_value], both_other[:half_value]])
+    link = jnp.concatenate([both[half_value:], both_other[half_value:]])
+
+    rows_here = jnp.concatenate(arrived)
+    weights = jnp.concatenate([a_all, b_all, c_all])
+    partial = contract_last(rows_here, weights)
+    summed = partial[:half_rows]
+    for d in shifts:
+        block = partial[d * half_rows : (d + 1) * half_rows].astype(bf16)
+        summed = summed + rotate(block, "dp", -d).astype(f32)
+    mine = summed.astype(bf16)
+    theirs = swap(mine, "section")
+    from_hidden = jnp.where(first, mine, theirs).astype(f32)
+    from_unembed = jnp.where(first, theirs, mine).astype(f32)
+    width = 2 * half_value
+    a0, b0, a1 = (from_hidden[:, i * width : (i + 1) * width] for i in range(3))
+    t1, t0 = (from_unembed[:, i * width : (i + 1) * width] for i in range(1, 3))
+
+    local_count = jnp.sum(
+        (jnp.repeat(survive, resp_count // survive.shape[0]) * lengths).astype(f32)
+    )
+    listed = jnp.any(assign[None, :] == jnp.arange(resp_count)[:, None], axis=1)
+    position_index = lax.broadcasted_iota(jnp.int32, (half_resp, positions), 1)
+    live = (position_index < my_half(lengths)[:, None]) & my_half(listed)[:, None]
+    adv = my_half(advantage)[:, None]
+    gap = my_half(recorded_gap)
+    clipped = (adv > 0) & (gap > clip_high) | (adv < 0) & (gap < clip_low)
+    weight = jnp.where(live & ~clipped, -loss_scale * adv, 0.0).reshape(half_rows, 1)
+    base = my_half(reference_logit).reshape(half_rows, 1)
+    listed_rows = jnp.repeat(my_half(listed), positions)[:, None]
+    hid32, un32 = hid_half.astype(f32), un_half.astype(f32)
+
+    def row_sum(array):
+        return jnp.sum(array, axis=-1, keepdims=True)
+
+    square0 = row_sum(hid32 * hid32)
+    dot0 = row_sum(hid32 * un32)
+    r0 = lax.rsqrt(square0 / model_width + eps_norm)
+    p0b = (r0 * a0).astype(bf16)
+    p0 = p0b.astype(f32)
+    linked = jnp.dot(p0b, link, preferred_element_type=f32)
+    grammed = jnp.dot(p0b, gram, preferred_element_type=f32)
+    square1 = square0 + row_sum(p0 * (2.0 * b0 + grammed))
+    r1 = lax.rsqrt(jnp.maximum(square1, 0.0) / model_width + eps_norm)
+    p1 = r1 * (a1 + linked)
+    logit = dot0 + row_sum(p0 * t0) + row_sum(p1 * t1)
+    seed = weight * jnp.exp(jnp.where(listed_rows, logit - base, 0.0))
+    gp1 = seed * t1
+    c1 = r1 * r1 * row_sum(gp1 * p1) / model_width
+    back = contract_last(gp1.astype(bf16), link)
+    gp0 = seed * t0 + r1 * back - c1 * (b0 + grammed)
+
+    early = jnp.where(first, p0b, mine[:, width : 2 * width])
+    early_all = jnp.concatenate([early] + [rotate(early, "dp", d) for d in shifts])
+    early_cross = swap(early_all, "section")
+    early_two = jnp.concatenate([early_all, early_cross], axis=1)
+    early_rows = jnp.concatenate([early_two, swap_columns(swap(early_two, "tensor"), half_value)])
+    p0_rows = jnp.where(first, early_rows[:, :width], early_rows[:, width:])
+    t1_rows = jnp.where(first, early_rows[:, width:], early_rows[:, :width])
+
+    here_cross = swap(rows_here, "section")
+    here_two = jnp.concatenate([rows_here, here_cross], axis=1)
+    here_rows = jnp.concatenate([here_two, swap(here_two, "tensor")])
+    hid_rows = jnp.where(first, here_rows[:, :own_width], here_rows[:, own_width:])
+    un_rows = jnp.where(first, here_rows[:, own_width:], here_rows[:, :own_width])
+
+    late = jnp.where(first, r0 * gp0, seed * p1).astype(bf16)
+    scalars = jnp.concatenate([seed, r1, c1, jnp.full_like(seed, local_count)], axis=1)
+    high = lax.reduce_precision(scalars, 8, 7)
+    extra = jnp.concatenate([high, scalars - high], axis=1).astype(bf16)
+    extra = jnp.pad(extra, ((0, 0), (0, 128 - extra.shape[1])))
+    late_own = jnp.concatenate([late[:, :half_value], extra], axis=1)
+    late_other = swap(jnp.concatenate([late[:, half_value:], extra], axis=1), "tensor")
+    late_here = jnp.concatenate([late_own, late_other])
+    pieces = [late_here] + [rotate(late_here, "dp", d) for d in shifts]
+    late_rows = jnp.concatenate([p[:half_rows] for p in pieces] + [p[half_rows:] for p in pieces])
+    found = late_rows[:, half_value : half_value + 8].astype(f32)
+    found = found[:, :4] + found[:, 4:]
+    seed_rows, r1_rows, c1_rows = found[:, 0:1], found[:, 1:2], found[:, 2:3]
+    token_total = jnp.sum(found[:: half_rows, 3]) / 2.0
+    late_rows = late_rows[:, :half_value]
+
+    hid32_rows = hid_rows.astype(f32)
+    x1_rows = hid32_rows + jnp.dot(
+        p0_rows, jnp.where(first, b_all, c_all), preferred_element_type=f32
+    )
+    n1_rows = jnp.dot(t1_rows, c_all, preferred_element_type=f32)
+    g1_rows = seed_rows * (un_rows.astype(f32) + r1_rows * n1_rows) - c1_rows * x1_rows
+    value_left = jnp.where(
+        first, late_rows, (seed_rows * r1_rows * t1_rows[:, :half_value].astype(f32)).astype(bf16)
+    )
+    value_right = jnp.where(first, hid_rows, x1_rows.astype(bf16))
+    output_left = jnp.where(first, p0_rows[:, :half_value], late_rows)
+    output_right = jnp.where(first, g1_rows.astype(bf16), un_rows)
+    grad_value = contract_first(value_right, value_left) * (gain[:, None] / token_total)
+    grad_output = contract_first(output_left, output_right) / token_total
+    return (grad_value[None], grad_output[None])
+
+
+def swap_columns(array, half_value):
+    low, high = array[:, :half_value], array[:, half_value : 2 * half_value]
+    low2, high2 = array[:, 2 * half_value : 3 * half_value], array[:, 3 * half_value :]
+    return jnp.concatenate([high, low, high2, low2], axis=1)
+
+
 def solution(mesh):
     placed = (
         P(("groups", "dp"), None, None),
@@ -189,8 +383,9 @@
         P(("groups", "dp"), None),
         P(("groups", "dp"), None),
     )
+    two_by_two = mesh.shape["section"] == 2 and mesh.shape["tensor"] == 2
     return jax.shard_map(
-        local,
+        low_rank if two_by_two else general,
         mesh=mesh,
         in_specs=placed,
         out_specs=(

time: 450 us -> 129 us (0.29)
  waiting for transfers between devices: 326 us -> 41.1 us
  starting transfers between devices: 10.5 us -> 38 us
  local copies, waits for them, and re-layouts: 32.9 us -> 13.4 us
  other arithmetic: 32.2 us -> 19.2 us
  blocking collectives: 12.9 us -> 0 us
  between operations: 15.3 us -> 2.78 us
  matrix products: 19.3 us -> 13.9 us
    all_gather x2 -> x0, waiting for transfers between devices: 101 us -> none  [the longest x1 52.5 us: local(): lax.all_gather(output_proj, 'dp', axis=2, tiled=True)]
    psum x5 -> x0, waiting for transfers between devices: 85.4 us -> none  [the longest x3 48.4 us: local(): lax.psum(partial_out.astype(jnp.bfloat16), 'tensor').astype(jnp.float32)]
    reduce_scatter x1 -> x0, waiting for transfers between devices: 80.2 us -> none  [local(): lax.psum_scatter(jnp.concatenate([contract_first(flat_normed, flat_grad_v...]
    ppermute x4 -> x30, starting transfers between devices: 10.2 us -> 38 us  [rotate(): lax.ppermute(block, axis, [(i, (i + distance) % count) for i in range(cou...]
    ppermute x4 -> x30, waiting for transfers between devices: 57.8 us -> 41.1 us  [rotate(): lax.ppermute(block, axis, [(i, (i + distance) % count) for i in range(cou...]
    dynamic_update_slice x10 -> x1, other arithmetic: 14.3 us -> 0.03 us  [low_rank(): lax.dynamic_update_slice_in_dim(product, total, dp_index * block_rows, 0)]
    psum x1 -> x0, blocking collectives: 12.9 us -> none  [local(): token_total = lax.psum(local_count, 'dp')]
    dynamic_slice x12 -> x5, local copies, waits for them, and re-layouts: 11.8 us -> 1.03 us  [the longest x2 0.81 us: columns(): lax.dynamic_slice_in_dim(array, index * own_width, own_width, array.ndim...]
  transfers between devices with their start and end apart: 12 -> 30, of which waited for: 12 -> 12; matrix products, arithmetic and copies ran while one was open for 6% -> 21% of each run, Pallas kernels for 0% -> 0%
where the time goes in v1:
time: 129 us; the launch traced here: 128 us
  waiting for transfers between devices  41.1 us (32%)
  starting transfers between devices  38 us (29%)
  other arithmetic  19.2 us (15%)
  matrix products  13.9 us (11%)
  local copies, waits for them, and re-layouts  13.4 us (10%)
  between operations  2.78 us (2%)
    ppermute x30, waiting for transfers between devices, rotate(): lax.ppermute(block, axis, [(i, (i + distance) % count) for i in range(cou...  41.1 us
    ppermute x30, starting transfers between devices, rotate(): lax.ppermute(block, axis, [(i, (i + distance) % count) for i in range(cou...  38 us
    dot_general x2, matrix products, contract_first(): lax.dot_general(left_rows, right_rows, (((0,), (0,)), ((), ())), preferre...  7.05 us
    unnamed x99, local copies, waits for them, and re-layouts  6.67 us
    dot_general x3, matrix products, contract_last(): lax.dot_general(left_rows, right_rows, (((1,), (1,)), ((), ())), preferre...  4.69 us
    concatenate x1, other arithmetic, low_rank(): here_rows = jnp.concatenate([here_two, swap(here_two, 'tensor')])  4.22 us
  transfers between devices with their start and end apart: 30, of which 12 were waited for; matrix products, arithmetic and copies ran while one was open for 21% of the time, Pallas kernels for 0%

profile of v1, /device:TPU:0, one launch (start us, length us, event | category | flops | bytes accessed | tf_op | source)
XLA Modules:
  0.0 128.4 jit_solution(290680805594622595)
XLA Ops:
  0.7 1.4 %copy.53 = bf16[1,1280,256]{1,2,0:T(8,128)(2,1)S(1)} copy(bf16[1,1280,256]{2,1,0:T(8,128)(2,1)} %param.13) | data formatting | bytes 1310720 | tf_op args[2]
  2.1 2.2 %broadcast_select_fusion.1 = (bf16[256,1280]{1,0:T(8,128)(2,1)}, bf16[256,1280]{1,0:T(8,128)(2,1)S(1)}) fusion(pred[]{:T(512)S(6)} %eq.27, bf16[1,256,1280]{2,1,0:T(8,128)(2,1)} %param.14, f32[1280]{0:T(1024)S(1)} %fusion.53, bf16[1,1280,256]{1,2,0:T(8,128)(2,1)S(1)} %copy.53), kind=kLoop, calls=%fused_computation.40 | loop fusion | flops 1310720 | bytes 2626561 | tf_op jit(solution)/shard_map/jit(_where)/select_n | solution.py:226
  4.3 1.1 pad_maximum_fusion.2
  6.0 2.6 %collective-permute-start.6 = (bf16[256,1280]{1,0:T(8,128)(2,1)}, bf16[256,1280]{1,0:T(8,128)(2,1)}, u32[]{:S(2)}, u32[]{:S(2)}) collective-permute-start(bf16[256,1280]{1,0:T(8,128)(2,1)} %get-tuple-element.16), channel_id=1, source_target_pairs={{0,2},{2,0},{1,3},{3,1},{4,6},{6,4},{5,7},{7,5},{8,10},{10,8},{9,1... | collective-permute-start | bytes 1966088 | tf_op jit(solution)/shard_map/ppermute | solution.py:180
  8.6 1.4 %select_bitcast_fusion = bf16[64,5120]{1,0:T(8,128)(2,1)S(1)} fusion(pred[]{:T(512)S(6)} %eq.27, bf16[16,8,5120]{2,1,0:T(8,128)(2,1)} %param.12, s32[]{:T(128)S(6)} %select_n.223, bf16[16,8,5120]{2,1,0:T(8,128)(2,1)} %param.11), kind=kLoop, calls=%fused_computation.39 | loop fusion | flops 327680 | bytes 1966085 | tf_op jit(solution)/shard_map/jit(_where)/select_n | solution.py:222
  10.7 1.6 %collective-permute-start = (bf16[64,1280]{1,0:T(8,128)(2,1)}, bf16[64,1280]{1,0:T(8,128)(2,1)S(1)}, u32[]{:S(2)}, u32[]{:S(2)}) collective-permute-start(bf16[64,1280]{1,0:T(8,128)(2,1)} %get-tuple-element.33), channel_id=1, source_target_pairs={{0,4},{4,8},{8,12},{12,0},{1,5},{5,9},{9,13},{13,1},{2,6},{6,10},{... | collective-permute-start | bytes 491528 | tf_op jit(solution)/shard_map/ppermute | solution.py:180
  12.3 2.6 %collective-permute-start.1 = (bf16[64,1280]{1,0:T(8,128)(2,1)}, bf16[64,1280]{1,0:T(8,128)(2,1)S(1)}, u32[]{:S(2)}, u32[]{:S(2)}) collective-permute-start(bf16[64,1280]{1,0:T(8,128)(2,1)} %get-tuple-element.32), channel_id=1, source_target_pairs={{0,8},{4,12},{8,0},{12,4},{1,9},{5,13},{9,1},{13,5},{2,10},{6,14},... | collective-permute-start | bytes 491528 | tf_op jit(solution)/shard_map/ppermute | solution.py:180
  14.9 1.3 %collective-permute-start.2 = (bf16[64,1280]{1,0:T(8,128)(2,1)S(1)}, bf16[64,1280]{1,0:T(8,128)(2,1)S(1)}, u32[]{:S(2)}, u32[]{:S(2)}) collective-permute-start(bf16[64,1280]{1,0:T(8,128)(2,1)S(1)} %get-tuple-element.31), channel_id=1, source_target_pairs={{0,12},{4,0},{8,4},{12,8},{1,13},{5,1},{9,5},{13,9},{2,14},{6,2},{... | collective-permute-start | bytes 491528 | tf_op jit(solution)/shard_map/ppermute | solution.py:180
  17.2 1.6 %fusion.11 = (f32[8,8]{1,0:T(8,128)S(1)}, f32[8,8]{1,0:T(8,128)S(1)}) fusion(bf16[16,8,5120]{2,1,0:T(8,128)(2,1)} %param.12, s32[]{:T(128)S(6)} %select_n.223, bf16[16,8,5120]{2,1,0:T(8,128)(2,1)} %param.11), kind=kLoop, calls=%fused_computation.19 | loop fusion | flops 1965952 | bytes 1311236 | tf_op jit(solution)/shard_map/reduce_sum | solution.py:300
  23.7 2.5 %collective-permute-done.1 = bf16[64,1280]{1,0:T(8,128)(2,1)S(1)} collective-permute-done((bf16[64,1280]{1,0:T(8,128)(2,1)}, bf16[64,1280]{1,0:T(8,128)(2,1)S(1)}, u32[]{:S(2)}, u32[]{:S(2)}) %collective-permute-start.1) | collective-permute-done | bytes 163872 | tf_op jit(solution)/shard_map/ppermute | solution.py:180
  27.7 1.8 %fusion.8 = f32[128,512]{1,0:T(8,128)S(1)} fusion(bf16[256,1280]{1,0:T(8,128)(2,1)S(1)} %get-tuple-element.17, bf16[256,1280]{1,0:T(8,128)(2,1)S(1)} %get-tuple-element.18, pred[]{:T(512)S(6)} %eq.27, bf16[256,1280]{1,0:T(8,128)(2,1)S(1)} %get-tuple-element.20, bf16[256,1280]{1,0:T(8,128)(2,1)S(1)} %bitcast.53, ...), kind=kOutput, calls=%fused_computation.17 | convolution fusion | flops 173834240 | bytes 3540480 | tf_op jit(solution)/shard_map/dot_general | solution.py:37
  29.6 3.9 %collective-permute-start.17 = (bf16[32,512]{1,0:T(8,128)(2,1)S(1)}, bf16[32,512]{1,0:T(8,128)(2,1)S(1)}, u32[]{:S(2)}, u32[]{:S(2)}) collective-permute-start(bf16[32,512]{1,0:T(8,128)(2,1)S(1)} %get-tuple-element.44), channel_id=1, source_target_pairs={{0,4},{4,8},{8,12},{12,0},{1,5},{5,9},{9,13},{13,1},{2,6},{6,10},{... | collective-permute-start | bytes 98312 | tf_op jit(solution)/shard_map/ppermute | solution.py:180
  33.5 1.7 %collective-permute-start.18 = (bf16[32,512]{1,0:T(8,128)(2,1)S(1)}, bf16[32,512]{1,0:T(8,128)(2,1)S(1)}, u32[]{:S(2)}, u32[]{:S(2)}) collective-permute-start(bf16[32,512]{1,0:T(8,128)(2,1)S(1)} %get-tuple-element.46), channel_id=1, source_target_pairs={{0,8},{4,12},{8,0},{12,4},{1,9},{5,13},{9,1},{13,5},{2,10},{6,14},... | collective-permute-start | bytes 98312 | tf_op jit(solution)/shard_map/ppermute | solution.py:180
  36.1 1.2 constant_dynamic-update-slice_fusion.7
  37.4 1.1 copy-done.25
  38.5 1.2 fusion.77
  39.8 1.3 %collective-permute-start.20 = (bf16[32,512]{1,0:T(8,128)(2,1)S(1)}, bf16[32,512]{1,0:T(8,128)(2,1)S(1)}, u32[]{:S(2)}, u32[]{:S(2)}) collective-permute-start(bf16[32,512]{1,0:T(8,128)(2,1)S(1)} %get-tuple-element.13), channel_id=1, source_target_pairs={{0,4},{4,8},{8,12},{12,0},{1,5},{5,9},{9,13},{13,1},{2,6},{6,10},{... | collective-permute-start | bytes 98312 | tf_op jit(solution)/shard_map/ppermute | solution.py:180
  41.3 3.7 %collective-permute-start.8 = (bf16[64,1536]{1,0:T(8,128)(2,1)S(1)}, bf16[64,1536]{1,0:T(8,128)(2,1)S(1)}, u32[]{:S(2)}, u32[]{:S(2)}) collective-permute-start(bf16[64,1536]{1,0:T(8,128)(2,1)S(1)} %get-tuple-element.23), channel_id=1, source_target_pairs={{0,12},{4,0},{8,4},{12,8},{1,13},{5,1},{9,5},{13,9},{2,14},{6,2},{... | collective-permute-start | bytes 589832 | tf_op jit(solution)/shard_map/ppermute | solution.py:180
  45.1 0.9 collective-permute-done.20
  46.0 2.0 %collective-permute-start.21 = (bf16[32,512]{1,0:T(8,128)(2,1)S(1)}, bf16[32,512]{1,0:T(8,128)(2,1)S(1)}, u32[]{:S(2)}, u32[]{:S(2)}) collective-permute-start(bf16[32,512]{1,0:T(8,128)(2,1)S(1)} %get-tuple-element.13), channel_id=1, source_target_pairs={{0,8},{4,12},{8,0},{12,4},{1,9},{5,13},{9,1},{13,5},{2,10},{6,14},... | collective-permute-start | bytes 98312 | tf_op jit(solution)/shard_map/ppermute | solution.py:180
  48.0 15.2 %collective-permute-done.21 = bf16[32,512]{1,0:T(8,128)(2,1)S(1)} collective-permute-done((bf16[32,512]{1,0:T(8,128)(2,1)S(1)}, bf16[32,512]{1,0:T(8,128)(2,1)S(1)}, u32[]{:S(2)}, u32[]{:S(2)}) %collective-permute-start.21) | collective-permute-done | bytes 32800 | tf_op jit(solution)/shard_map/ppermute | solution.py:180
  63.8 3.4 %collective-permute-done.22 = bf16[32,512]{1,0:T(8,128)(2,1)S(1)} collective-permute-done((bf16[32,512]{1,0:T(8,128)(2,1)S(1)}, bf16[32,512]{1,0:T(8,128)(2,1)S(1)}, u32[]{:S(2)}, u32[]{:S(2)}) %collective-permute-start.22) | collective-permute-done | bytes 32800 | tf_op jit(solution)/shard_map/ppermute | solution.py:180
  67.2 1.5 %collective-permute-start.23 = (bf16[128,512]{1,0:T(8,128)(2,1)S(1)}, bf16[128,512]{1,0:T(8,128)(2,1)S(1)}, u32[]{:S(2)}, u32[]{:S(2)}) collective-permute-start(bf16[128,512]{1,0:T(8,128)(2,1)S(1)} %constant_dynamic-update-slice_fusion.11), channel_id=1, source_target_pairs={{0,16},{16,0},{1,17},{17,1},{2,18},{18,2},{3,19},{19,3},{4,20},{20... | collective-permute-start | bytes 393224 | tf_op jit(solution)/shard_map/ppermute | solution.py:180
  68.8 1.6 %collective-permute-start.11 = (bf16[64,1536]{1,0:T(8,128)(2,1)S(1)}, bf16[64,1536]{1,0:T(8,128)(2,1)S(1)}, u32[]{:S(2)}, u32[]{:S(2)}) collective-permute-start(bf16[64,1536]{1,0:T(8,128)(2,1)S(1)} %fusion.29), channel_id=1, source_target_pairs={{0,2},{2,0},{1,3},{3,1},{4,6},{6,4},{5,7},{7,5},{8,10},{10,8},{9,1... | collective-permute-start | bytes 589832 | tf_op jit(solution)/shard_map/ppermute | solution.py:180
  70.4 1.7 %collective-permute-done.23 = bf16[128,512]{1,0:T(8,128)(2,1)S(1)} collective-permute-done((bf16[128,512]{1,0:T(8,128)(2,1)S(1)}, bf16[128,512]{1,0:T(8,128)(2,1)S(1)}, u32[]{:S(2)}, u32[]{:S(2)}) %collective-permute-start.23) | collective-permute-done | bytes 131104 | tf_op jit(solution)/shard_map/ppermute | solution.py:180
  72.1 1.6 %collective-permute-start.24 = (bf16[256,512]{1,0:T(8,128)(2,1)S(1)}, bf16[256,512]{1,0:T(8,128)(2,1)S(1)}, u32[]{:S(2)}, u32[]{:S(2)}) collective-permute-start(bf16[256,512]{1,0:T(8,128)(2,1)S(1)} %constant_dynamic-update-slice_fusion.9), channel_id=1, source_target_pairs={{0,2},{2,0},{1,3},{3,1},{4,6},{6,4},{5,7},{7,5},{8,10},{10,8},{9,1... | collective-permute-start | bytes 786440 | tf_op jit(solution)/shard_map/ppermute | solution.py:180
  73.7 2.9 %collective-permute-done.11 = bf16[64,1536]{1,0:T(8,128)(2,1)S(1)} collective-permute-done((bf16[64,1536]{1,0:T(8,128)(2,1)S(1)}, bf16[64,1536]{1,0:T(8,128)(2,1)S(1)}, u32[]{:S(2)}, u32[]{:S(2)}) %collective-permute-start.11) | collective-permute-done | bytes 196640 | tf_op jit(solution)/shard_map/ppermute | solution.py:180
  76.7 3.0 %collective-permute-done.24 = bf16[256,512]{1,0:T(8,128)(2,1)S(1)} collective-permute-done((bf16[256,512]{1,0:T(8,128)(2,1)S(1)}, bf16[256,512]{1,0:T(8,128)(2,1)S(1)}, u32[]{:S(2)}, u32[]{:S(2)}) %collective-permute-start.24) | collective-permute-done | bytes 262176 | tf_op jit(solution)/shard_map/ppermute | solution.py:180
  80.1 2.6 %collective-permute-start.13 = (bf16[64,512]{1,0:T(8,128)(2,1)S(1)}, bf16[64,512]{1,0:T(8,128)(2,1)S(1)}, u32[]{:S(2)}, u32[]{:S(2)}) collective-permute-start(bf16[64,512]{1,0:T(8,128)(2,1)S(1)} %get-tuple-element.14), channel_id=1, source_target_pairs={{0,8},{4,12},{8,0},{12,4},{1,9},{5,13},{9,1},{13,5},{2,10},{6,14},... | collective-permute-start | bytes 196616 | tf_op jit(solution)/shard_map/ppermute | solution.py:180
  82.7 1.2 collective-permute-start.14
  83.9 1.1 pad_maximum_fusion.3
  85.1 1.9 %collective-permute-done.12 = bf16[64,512]{1,0:T(8,128)(2,1)S(1)} collective-permute-done((bf16[64,512]{1,0:T(8,128)(2,1)S(1)}, bf16[64,512]{1,0:T(8,128)(2,1)S(1)}, u32[]{:S(2)}, u32[]{:S(2)}) %collective-permute-start.12) | collective-permute-done | bytes 65568 | tf_op jit(solution)/shard_map/ppermute | solution.py:180
  86.9 1.9 %collective-permute-done.13 = bf16[64,512]{1,0:T(8,128)(2,1)S(1)} collective-permute-done((bf16[64,512]{1,0:T(8,128)(2,1)S(1)}, bf16[64,512]{1,0:T(8,128)(2,1)S(1)}, u32[]{:S(2)}, u32[]{:S(2)}) %collective-permute-start.13) | collective-permute-done | bytes 65568 | tf_op jit(solution)/shard_map/ppermute | solution.py:180
  89.6 1.5 %collective-permute-start.15 = (bf16[256,512]{1,0:T(8,128)(2,1)}, bf16[256,512]{1,0:T(8,128)(2,1)}, u32[]{:S(2)}, u32[]{:S(2)}) collective-permute-start(bf16[256,512]{1,0:T(8,128)(2,1)} %pad_maximum_fusion.12), channel_id=1, source_target_pairs={{0,2},{2,0},{1,3},{3,1},{4,6},{6,4},{5,7},{7,5},{8,10},{10,8},{9,1... | collective-permute-start | bytes 786440 | tf_op jit(solution)/shard_map/ppermute | solution.py:180
  91.2 1.0 fusion.42
  94.2 1.7 %select_convert_fusion.2 = bf16[64,512]{1,0:T(8,128)(2,1)S(1)} fusion(f32[64,512]{1,0:T(8,128)} %get-tuple-element.58, f32[64,1536]{1,0:T(8,128)} %copy-done.9, f32[64,1536]{1,0:T(8,128)} %copy-done.13, f32[64]{0:T(128)S(1)} %multiply_multiply_fusion, f32[64]{0:T(128)S(1)} %exponential_multiply_fusion.1, f32[64]{0:T(128)} %copy-done.35, ...), kind=kOutput, calls=%fused_computation.88 | convolution fusion | flops 36372480 | bytes 1640961 | tf_op jit(solution)/shard_map/dot_general | solution.py:37
  95.9 1.2 collective-permute-done.15
  97.2 1.8 %pad_maximum_fusion.11 = bf16[256,1024]{1,0:T(8,128)(2,1)} fusion(bf16[256,512]{1,0:T(8,128)(2,1)} %collective-permute-done.15, bf16[64,512]{1,0:T(8,128)(2,1)S(1)} %copy-done.21, bf16[64,512]{1,0:T(8,128)(2,1)S(1)} %collective-permute-done.13, bf16[64,512]{1,0:T(8,128)(2,1)S(1)} %collective-permute-done.12, bf16[64,512]{1,0:T(8,128)(2,1)S(1)} %get-tuple-element.14), kind=kLoop, calls=%fused_computation.48 | loop fusion | flops 2621440 | bytes 1048576 | tf_op jit(solution)/shard_map/concatenate | solution.py:322
  99.0 2.1 %collective-permute-start.27 = (bf16[128,384]{1,0:T(8,128)(2,1)S(1)}, bf16[128,384]{1,0:T(8,128)(2,1)S(1)}, u32[]{:S(2)}, u32[]{:S(2)}) collective-permute-start(bf16[128,384]{1,0:T(8,128)(2,1)S(1)} %pad_maximum_fusion.13), channel_id=1, source_target_pairs={{0,4},{4,8},{8,12},{12,0},{1,5},{5,9},{9,13},{13,1},{2,6},{6,10},{... | collective-permute-start | bytes 294920 | tf_op jit(solution)/shard_map/ppermute | solution.py:180
  101.1 4.2 %pad_maximum_fusion = bf16[512,2560]{1,0:T(8,128)(2,1)} fusion(bf16[256,2560]{1,0:T(8,128)(2,1)S(1)} %collective-permute-done.4, bf16[256,1280]{1,0:T(8,128)(2,1)S(1)} %collective-permute-done.3, bf16[64,1280]{1,0:T(8,128)(2,1)S(1)} %copy-done.8, bf16[64,1280]{1,0:T(8,128)(2,1)S(1)} %copy-done.6, bf16[64,1280]{1,0:T(8,128)(2,1)S(1)} %copy-done.4, ...), kind=kLoop, calls=%fused_computation.11 | loop fusion | flops 15728640 | bytes 5242880 | tf_op jit(solution)/shard_map/concatenate | solution.py:329
  105.3 2.2 %collective-permute-start.28 = (bf16[128,384]{1,0:T(8,128)(2,1)S(1)}, bf16[128,384]{1,0:T(8,128)(2,1)S(1)}, u32[]{:S(2)}, u32[]{:S(2)}) collective-permute-start(bf16[128,384]{1,0:T(8,128)(2,1)S(1)} %pad_maximum_fusion.13), channel_id=1, source_target_pairs={{0,8},{4,12},{8,0},{12,4},{1,9},{5,13},{9,1},{13,5},{2,10},{6,14},... | collective-permute-start | bytes 294920 | tf_op jit(solution)/shard_map/ppermute | solution.py:180
  107.8 5.4 %collective-permute-done.28 = bf16[128,384]{1,0:T(8,128)(2,1)S(1)} collective-permute-done((bf16[128,384]{1,0:T(8,128)(2,1)S(1)}, bf16[128,384]{1,0:T(8,128)(2,1)S(1)}, u32[]{:S(2)}, u32[]{:S(2)}) %collective-permute-start.28) | collective-permute-done | bytes 98336 | tf_op jit(solution)/shard_map/ppermute | solution.py:180
  113.2 1.0 collective-permute-done.29
  117.1 1.2 fusion.75
  118.4 1.2 maximum_maximum_fusion
  120.4 0.9 convolution_add_fusion
  121.4 1.9 %fusion.4 = f32[1,1280,256]{2,1,0:T(8,128)} fusion(f32[512,1280]{1,0:T(8,128)S(1)} %convolution_add_fusion, pred[]{:T(512)S(6)} %eq.27, f32[1280]{0:T(1024)S(1)} %broadcast_divide_fusion, bf16[512,512]{1,0:T(8,128)(2,1)S(1)} %get-tuple-element.21, f32[512]{0:T(512)S(1)} %get-tuple-element.9, bf16[512,384]{1,0:T(8,128)(2,1)S(1)} %copy-done.29, ...), kind=kOutput, calls=%fused_computation.8 | convolution fusion | flops 338362368 | bytes 7089152 | tf_op jit(solution)/shard_map/dot_general | solution.py:43
  123.3 5.1 %fusion.5 = f32[1,256,1280]{2,1,0:T(8,128)} fusion(bf16[512,512]{1,0:T(8,128)(2,1)} %copy-done.22, bf16[512,1280]{1,0:T(8,128)(2,1)} %copy-done.25, f32[512,1280]{1,0:T(8,128)} %copy-done.43, f32[512]{0:T(512)S(1)} %get-tuple-element.8, f32[512]{0:T(512)S(1)} %get-tuple-element.7, f32[512]{0:T(512)S(1)} %get-tuple-element.6, pred[]{:T(512)S(6)} %eq.27, ...), kind=kOutput, calls=%fused_computation.9 | convolution fusion | flops 1012989952 | bytes 8920576 | tf_op jit(solution)/shard_map/dot_general | solution.py:43
  (194 shorter events, 16.3 us)
Async XLA Ops:
  0.6 3.6 %copy-start.1 = (bf16[1,256,1280]{2,1,0:T(8,128)(2,1)S(1)}, bf16[1,256,1280]{2,1,0:T(8,128)(2,1)}, u32[]{:S(2)}) copy-start(bf16[1,256,1280]{2,1,0:T(8,128)(2,1)} %param.14) | copy-start | bytes 1966084
  5.4 10.8 %copy-start.41 = (s32[16]{0:T(128)S(1)}, s32[16]{0:T(128)}, u32[]{:S(2)}) copy-start(s32[16]{0:T(128)} %param.18) | copy-start | bytes 196
  5.4 11.0 %copy-start.42 = (s32[16]{0:T(128)S(1)}, s32[16]{0:T(128)}, u32[]{:S(2)}) copy-start(s32[16]{0:T(128)} %param.17) | copy-start | bytes 196
  5.4 11.1 %copy-start.40 = (f32[16]{0:T(128)S(1)}, f32[16]{0:T(128)}, u32[]{:S(2)}) copy-start(f32[16]{0:T(128)} %param.19) | copy-start | bytes 196
  5.4 11.2 %copy-start.30 = (f32[16,8]{0,1:T(8,128)S(1)}, f32[16,8]{0,1:T(8,128)}, u32[]{:S(2)}) copy-start(f32[16,8]{0,1:T(8,128)} %param.20) | copy-start | bytes 1540
  5.4 11.2 %copy-start.31 = (f32[16,8]{0,1:T(8,128)S(1)}, f32[16,8]{0,1:T(8,128)}, u32[]{:S(2)}) copy-start(f32[16,8]{0,1:T(8,128)} %param.21) | copy-start | bytes 1540
  5.4 22.1 %collective-permute-start.5 = (bf16[512,1280]{1,0:T(8,128)(2,1)}, bf16[512,1280]{1,0:T(8,128)(2,1)S(1)}, u32[]{:S(2)}, u32[]{:S(2)}) collective-permute-start(bf16[512,1280]{1,0:T(8,128)(2,1)} %pad_maximum_fusion.2), channel_id=1, source_target_pairs={{0,1},{1,0},{2,3},{3,2},{4,5},{5,4},{6,7},{7,6},{8,9},{9,8},{10,11... | collective-permute-start | bytes 3932168 | tf_op jit(solution)/shard_map/ppermute | solution.py:180
  6.0 21.5 %collective-permute-start.6 = (bf16[256,1280]{1,0:T(8,128)(2,1)}, bf16[256,1280]{1,0:T(8,128)(2,1)}, u32[]{:S(2)}, u32[]{:S(2)}) collective-permute-start(bf16[256,1280]{1,0:T(8,128)(2,1)} %get-tuple-element.16), channel_id=1, source_target_pairs={{0,2},{2,0},{1,3},{3,1},{4,6},{6,4},{5,7},{7,5},{8,10},{10,8},{9,1... | collective-permute-start | bytes 1966088 | tf_op jit(solution)/shard_map/ppermute | solution.py:180
  10.7 13.0 %collective-permute-start = (bf16[64,1280]{1,0:T(8,128)(2,1)}, bf16[64,1280]{1,0:T(8,128)(2,1)S(1)}, u32[]{:S(2)}, u32[]{:S(2)}) collective-permute-start(bf16[64,1280]{1,0:T(8,128)(2,1)} %get-tuple-element.33), channel_id=1, source_target_pairs={{0,4},{4,8},{8,12},{12,0},{1,5},{5,9},{9,13},{13,1},{2,6},{6,10},{... | collective-permute-start | bytes 491528 | tf_op jit(solution)/shard_map/ppermute | solution.py:180
  12.3 13.9 %collective-permute-start.1 = (bf16[64,1280]{1,0:T(8,128)(2,1)}, bf16[64,1280]{1,0:T(8,128)(2,1)S(1)}, u32[]{:S(2)}, u32[]{:S(2)}) collective-permute-start(bf16[64,1280]{1,0:T(8,128)(2,1)} %get-tuple-element.32), channel_id=1, source_target_pairs={{0,8},{4,12},{8,0},{12,4},{1,9},{5,13},{9,1},{13,5},{2,10},{6,14},... | collective-permute-start | bytes 491528 | tf_op jit(solution)/shard_map/ppermute | solution.py:180
  14.9 11.3 %collective-permute-start.2 = (bf16[64,1280]{1,0:T(8,128)(2,1)S(1)}, bf16[64,1280]{1,0:T(8,128)(2,1)S(1)}, u32[]{:S(2)}, u32[]{:S(2)}) collective-permute-start(bf16[64,1280]{1,0:T(8,128)(2,1)S(1)} %get-tuple-element.31), channel_id=1, source_target_pairs={{0,12},{4,0},{8,4},{12,8},{1,13},{5,1},{9,5},{13,9},{2,14},{6,2},{... | collective-permute-start | bytes 491528 | tf_op jit(solution)/shard_map/ppermute | solution.py:180
  20.9 6.8 %copy-start.38 = (f32[64]{0:T(128)}, f32[64]{0:T(128)S(1)}, u32[]{:S(2)}) copy-start(f32[64]{0:T(128)S(1)} %reduce_sum.89) | copy-start | bytes 772
  23.6 56.3 %copy-start.34 = (f32[64]{0:T(128)}, f32[64]{0:T(128)S(1)}, u32[]{:S(2)}) copy-start(f32[64]{0:T(128)S(1)} %add_rsqrt_fusion.2) | copy-start | bytes 772
  26.9 57.0 %collective-permute-start.3 = (bf16[256,1280]{1,0:T(8,128)(2,1)S(1)}, bf16[256,1280]{1,0:T(8,128)(2,1)S(1)}, u32[]{:S(2)}, u32[]{:S(2)}) collective-permute-start(bf16[256,1280]{1,0:T(8,128)(2,1)S(1)} %pad_maximum_fusion.7), channel_id=1, source_target_pairs={{0,2},{2,0},{1,3},{3,1},{4,6},{6,4},{5,7},{7,5},{8,10},{10,8},{9,1... | collective-permute-start | bytes 1966088 | tf_op jit(solution)/shard_map/ppermute | solution.py:180
  27.5 9.8 %collective-permute-start.7 = (bf16[256,1280]{1,0:T(8,128)(2,1)}, bf16[256,1280]{1,0:T(8,128)(2,1)S(1)}, u32[]{:S(2)}, u32[]{:S(2)}) collective-permute-start(bf16[256,1280]{1,0:T(8,128)(2,1)} %collective-permute-done.6), channel_id=1, source_target_pairs={{0,1},{1,0},{2,3},{3,2},{4,5},{5,4},{6,7},{7,6},{8,9},{9,8},{10,11... | collective-permute-start | bytes 1966088 | tf_op jit(solution)/shard_map/ppermute | solution.py:180
  29.6 10.2 %collective-permute-start.17 = (bf16[32,512]{1,0:T(8,128)(2,1)S(1)}, bf16[32,512]{1,0:T(8,128)(2,1)S(1)}, u32[]{:S(2)}, u32[]{:S(2)}) collective-permute-start(bf16[32,512]{1,0:T(8,128)(2,1)S(1)} %get-tuple-element.44), channel_id=1, source_target_pairs={{0,4},{4,8},{8,12},{12,0},{1,5},{5,9},{9,13},{13,1},{2,6},{6,10},{... | collective-permute-start | bytes 98312 | tf_op jit(solution)/shard_map/ppermute | solution.py:180
  33.5 6.2 %collective-permute-start.18 = (bf16[32,512]{1,0:T(8,128)(2,1)S(1)}, bf16[32,512]{1,0:T(8,128)(2,1)S(1)}, u32[]{:S(2)}, u32[]{:S(2)}) collective-permute-start(bf16[32,512]{1,0:T(8,128)(2,1)S(1)} %get-tuple-element.46), channel_id=1, source_target_pairs={{0,8},{4,12},{8,0},{12,4},{1,9},{5,13},{9,1},{13,5},{2,10},{6,14},... | collective-permute-start | bytes 98312 | tf_op jit(solution)/shard_map/ppermute | solution.py:180
  35.2 4.5 %collective-permute-start.19 = (bf16[32,512]{1,0:T(8,128)(2,1)S(1)}, bf16[32,512]{1,0:T(8,128)(2,1)S(1)}, u32[]{:S(2)}, u32[]{:S(2)}) collective-permute-start(bf16[32,512]{1,0:T(8,128)(2,1)S(1)} %get-tuple-element.45), channel_id=1, source_target_pairs={{0,12},{4,0},{8,4},{12,8},{1,13},{5,1},{9,5},{13,9},{2,14},{6,2},{... | collective-permute-start | bytes 98312 | tf_op jit(solution)/shard_map/ppermute | solution.py:180
  39.8 6.2 %collective-permute-start.20 = (bf16[32,512]{1,0:T(8,128)(2,1)S(1)}, bf16[32,512]{1,0:T(8,128)(2,1)S(1)}, u32[]{:S(2)}, u32[]{:S(2)}) collective-permute-start(bf16[32,512]{1,0:T(8,128)(2,1)S(1)} %get-tuple-element.13), channel_id=1, source_target_pairs={{0,4},{4,8},{8,12},{12,0},{1,5},{5,9},{9,13},{13,1},{2,6},{6,10},{... | collective-permute-start | bytes 98312 | tf_op jit(solution)/shard_map/ppermute | solution.py:180
  41.2 27.5 %collective-permute-start.10 = (bf16[64,1536]{1,0:T(8,128)(2,1)S(1)}, bf16[64,1536]{1,0:T(8,128)(2,1)S(1)}, u32[]{:S(2)}, u32[]{:S(2)}) collective-permute-start(bf16[64,1536]{1,0:T(8,128)(2,1)S(1)} %get-tuple-element.24), channel_id=1, source_target_pairs={{0,4},{4,8},{8,12},{12,0},{1,5},{5,9},{9,13},{13,1},{2,6},{6,10},{... | collective-permute-start | bytes 589832 | tf_op jit(solution)/shard_map/ppermute | solution.py:180
  41.3 27.3 %collective-permute-start.8 = (bf16[64,1536]{1,0:T(8,128)(2,1)S(1)}, bf16[64,1536]{1,0:T(8,128)(2,1)S(1)}, u32[]{:S(2)}, u32[]{:S(2)}) collective-permute-start(bf16[64,1536]{1,0:T(8,128)(2,1)S(1)} %get-tuple-element.23), channel_id=1, source_target_pairs={{0,12},{4,0},{8,4},{12,8},{1,13},{5,1},{9,5},{13,9},{2,14},{6,2},{... | collective-permute-start | bytes 589832 | tf_op jit(solution)/shard_map/ppermute | solution.py:180
  45.1 23.6 %collective-permute-start.9 = (bf16[64,1536]{1,0:T(8,128)(2,1)S(1)}, bf16[64,1536]{1,0:T(8,128)(2,1)S(1)}, u32[]{:S(2)}, u32[]{:S(2)}) collective-permute-start(bf16[64,1536]{1,0:T(8,128)(2,1)S(1)} %get-tuple-element.25), channel_id=1, source_target_pairs={{0,8},{4,12},{8,0},{12,4},{1,9},{5,13},{9,1},{13,5},{2,10},{6,14},... | collective-permute-start | bytes 589832 | tf_op jit(solution)/shard_map/ppermute | solution.py:180
  46.0 17.2 %collective-permute-start.21 = (bf16[32,512]{1,0:T(8,128)(2,1)S(1)}, bf16[32,512]{1,0:T(8,128)(2,1)S(1)}, u32[]{:S(2)}, u32[]{:S(2)}) collective-permute-start(bf16[32,512]{1,0:T(8,128)(2,1)S(1)} %get-tuple-element.13), channel_id=1, source_target_pairs={{0,8},{4,12},{8,0},{12,4},{1,9},{5,13},{9,1},{13,5},{2,10},{6,14},... | collective-permute-start | bytes 98312 | tf_op jit(solution)/shard_map/ppermute | solution.py:180
  63.2 3.9 %collective-permute-start.22 = (bf16[32,512]{1,0:T(8,128)(2,1)S(1)}, bf16[32,512]{1,0:T(8,128)(2,1)S(1)}, u32[]{:S(2)}, u32[]{:S(2)}) collective-permute-start(bf16[32,512]{1,0:T(8,128)(2,1)S(1)} %get-tuple-element.13), channel_id=1, source_target_pairs={{0,12},{4,0},{8,4},{12,8},{1,13},{5,1},{9,5},{13,9},{2,14},{6,2},{... | collective-permute-start | bytes 98312 | tf_op jit(solution)/shard_map/ppermute | solution.py:180
  67.2 5.0 %collective-permute-start.23 = (bf16[128,512]{1,0:T(8,128)(2,1)S(1)}, bf16[128,512]{1,0:T(8,128)(2,1)S(1)}, u32[]{:S(2)}, u32[]{:S(2)}) collective-permute-start(bf16[128,512]{1,0:T(8,128)(2,1)S(1)} %constant_dynamic-update-slice_fusion.11), channel_id=1, source_target_pairs={{0,16},{16,0},{1,17},{17,1},{2,18},{18,2},{3,19},{19,3},{4,20},{20... | collective-permute-start | bytes 393224 | tf_op jit(solution)/shard_map/ppermute | solution.py:180
  68.8 7.8 %collective-permute-start.11 = (bf16[64,1536]{1,0:T(8,128)(2,1)S(1)}, bf16[64,1536]{1,0:T(8,128)(2,1)S(1)}, u32[]{:S(2)}, u32[]{:S(2)}) collective-permute-start(bf16[64,1536]{1,0:T(8,128)(2,1)S(1)} %fusion.29), channel_id=1, source_target_pairs={{0,2},{2,0},{1,3},{3,1},{4,6},{6,4},{5,7},{7,5},{8,10},{10,8},{9,1... | collective-permute-start | bytes 589832 | tf_op jit(solution)/shard_map/ppermute | solution.py:180
  72.1 7.6 %collective-permute-start.24 = (bf16[256,512]{1,0:T(8,128)(2,1)S(1)}, bf16[256,512]{1,0:T(8,128)(2,1)S(1)}, u32[]{:S(2)}, u32[]{:S(2)}) collective-permute-start(bf16[256,512]{1,0:T(8,128)(2,1)S(1)} %constant_dynamic-update-slice_fusion.9), channel_id=1, source_target_pairs={{0,2},{2,0},{1,3},{3,1},{4,6},{6,4},{5,7},{7,5},{8,10},{10,8},{9,1... | collective-permute-start | bytes 786440 | tf_op jit(solution)/shard_map/ppermute | solution.py:180
  76.7 15.9 %copy-start.9 = (f32[64,1536]{1,0:T(8,128)}, f32[64,1536]{1,0:T(8,128)S(1)}, u32[]{:S(2)}) copy-start(f32[64,1536]{1,0:T(8,128)S(1)} %get-tuple-element.43) | copy-start | bytes 1179652
  76.7 15.9 %copy-start.13 = (f32[64,1536]{1,0:T(8,128)}, f32[64,1536]{1,0:T(8,128)S(1)}, u32[]{:S(2)}) copy-start(f32[64,1536]{1,0:T(8,128)S(1)} %get-tuple-element.42) | copy-start | bytes 1179652
  79.8 12.4 %copy-start.12 = (bf16[256,512]{1,0:T(8,128)(2,1)}, bf16[256,512]{1,0:T(8,128)(2,1)S(1)}, u32[]{:S(2)}) copy-start(bf16[256,512]{1,0:T(8,128)(2,1)S(1)} %get-tuple-element.36) | copy-start | bytes 786436
  79.8 11.2 %collective-permute-start.25 = (bf16[512,512]{1,0:T(8,128)(2,1)S(1)}, bf16[512,512]{1,0:T(8,128)(2,1)S(1)}, u32[]{:S(2)}, u32[]{:S(2)}) collective-permute-start(bf16[512,512]{1,0:T(8,128)(2,1)S(1)} %pad_maximum_fusion.8), channel_id=1, source_target_pairs={{0,1},{1,0},{2,3},{3,2},{4,5},{5,4},{6,7},{7,6},{8,9},{9,8},{10,11... | collective-permute-start | bytes 1572872 | tf_op jit(solution)/shard_map/ppermute | solution.py:180
  80.0 6.9 %collective-permute-start.12 = (bf16[64,512]{1,0:T(8,128)(2,1)S(1)}, bf16[64,512]{1,0:T(8,128)(2,1)S(1)}, u32[]{:S(2)}, u32[]{:S(2)}) collective-permute-start(bf16[64,512]{1,0:T(8,128)(2,1)S(1)} %get-tuple-element.14), channel_id=1, source_target_pairs={{0,4},{4,8},{8,12},{12,0},{1,5},{5,9},{9,13},{13,1},{2,6},{6,10},{... | collective-permute-start | bytes 196616 | tf_op jit(solution)/shard_map/ppermute | solution.py:180
  80.1 8.7 %collective-permute-start.13 = (bf16[64,512]{1,0:T(8,128)(2,1)S(1)}, bf16[64,512]{1,0:T(8,128)(2,1)S(1)}, u32[]{:S(2)}, u32[]{:S(2)}) collective-permute-start(bf16[64,512]{1,0:T(8,128)(2,1)S(1)} %get-tuple-element.14), channel_id=1, source_target_pairs={{0,8},{4,12},{8,0},{12,4},{1,9},{5,13},{9,1},{13,5},{2,10},{6,14},... | collective-permute-start | bytes 196616 | tf_op jit(solution)/shard_map/ppermute | solution.py:180
  82.7 6.1 %collective-permute-start.14 = (bf16[64,512]{1,0:T(8,128)(2,1)S(1)}, bf16[64,512]{1,0:T(8,128)(2,1)S(1)}, u32[]{:S(2)}, u32[]{:S(2)}) collective-permute-start(bf16[64,512]{1,0:T(8,128)(2,1)S(1)} %get-tuple-element.14), channel_id=1, source_target_pairs={{0,12},{4,0},{8,4},{12,8},{1,13},{5,1},{9,5},{13,9},{2,14},{6,2},{... | collective-permute-start | bytes 196616 | tf_op jit(solution)/shard_map/ppermute | solution.py:180
  85.0 7.1 %copy-start.39 = (f32[64]{0:T(128)S(1)}, f32[64]{0:T(128)}, u32[]{:S(2)}) copy-start(f32[64]{0:T(128)} %copy-done.38) | copy-start | bytes 772
  85.0 16.0 %collective-permute-start.4 = (bf16[256,2560]{1,0:T(8,128)(2,1)}, bf16[256,2560]{1,0:T(8,128)(2,1)S(1)}, u32[]{:S(2)}, u32[]{:S(2)}) collective-permute-start(bf16[256,2560]{1,0:T(8,128)(2,1)} %pad_maximum_fusion.3), channel_id=1, source_target_pairs={{0,1},{1,0},{2,3},{3,2},{4,5},{5,4},{6,7},{7,6},{8,9},{9,8},{10,11... | collective-permute-start | bytes 3932168 | tf_op jit(solution)/shard_map/ppermute | solution.py:180
  86.9 10.2 %copy-start.16 = (bf16[64,512]{1,0:T(8,128)(2,1)}, bf16[64,512]{1,0:T(8,128)(2,1)S(1)}, u32[]{:S(2)}) copy-start(bf16[64,512]{1,0:T(8,128)(2,1)S(1)} %collective-permute-done.12) | copy-start | bytes 196612
  88.8 8.4 %copy-start.18 = (bf16[64,512]{1,0:T(8,128)(2,1)}, bf16[64,512]{1,0:T(8,128)(2,1)S(1)}, u32[]{:S(2)}) copy-start(bf16[64,512]{1,0:T(8,128)(2,1)S(1)} %collective-permute-done.13) | copy-start | bytes 196612
  88.8 3.7 %copy-start.20 = (bf16[64,512]{1,0:T(8,128)(2,1)}, bf16[64,512]{1,0:T(8,128)(2,1)S(1)}, u32[]{:S(2)}) copy-start(bf16[64,512]{1,0:T(8,128)(2,1)S(1)} %collective-permute-done.14) | copy-start | bytes 196612
  89.6 7.6 %collective-permute-start.15 = (bf16[256,512]{1,0:T(8,128)(2,1)}, bf16[256,512]{1,0:T(8,128)(2,1)}, u32[]{:S(2)}, u32[]{:S(2)}) collective-permute-start(bf16[256,512]{1,0:T(8,128)(2,1)} %pad_maximum_fusion.12), channel_id=1, source_target_pairs={{0,2},{2,0},{1,3},{3,1},{4,6},{6,4},{5,7},{7,5},{8,10},{10,8},{9,1... | collective-permute-start | bytes 786440 | tf_op jit(solution)/shard_map/ppermute | solution.py:180
  93.4 3.7 %copy-start.21 = (bf16[64,512]{1,0:T(8,128)(2,1)S(1)}, bf16[64,512]{1,0:T(8,128)(2,1)}, u32[]{:S(2)}) copy-start(bf16[64,512]{1,0:T(8,128)(2,1)} %copy-done.20) | copy-start | bytes 196612
  95.9 3.1 %collective-permute-start.26 = (bf16[64,384]{1,0:T(8,128)(2,1)S(1)}, bf16[64,384]{1,0:T(8,128)(2,1)S(1)}, u32[]{:S(2)}, u32[]{:S(2)}) collective-permute-start(bf16[64,384]{1,0:T(8,128)(2,1)S(1)} %get-tuple-element.49), channel_id=1, source_target_pairs={{0,1},{1,0},{2,3},{3,2},{4,5},{5,4},{6,7},{7,6},{8,9},{9,8},{10,11... | collective-permute-start | bytes 147464 | tf_op jit(solution)/shard_map/ppermute | solution.py:180
  99.0 18.1 %collective-permute-start.16 = (bf16[256,1024]{1,0:T(8,128)(2,1)}, bf16[256,1024]{1,0:T(8,128)(2,1)}, u32[]{:S(2)}, u32[]{:S(2)}) collective-permute-start(bf16[256,1024]{1,0:T(8,128)(2,1)} %pad_maximum_fusion.11), channel_id=1, source_target_pairs={{0,1},{1,0},{2,3},{3,2},{4,5},{5,4},{6,7},{7,6},{8,9},{9,8},{10,11... | collective-permute-start | bytes 1572872 | tf_op jit(solution)/shard_map/ppermute | solution.py:180
  99.0 8.8 %collective-permute-start.27 = (bf16[128,384]{1,0:T(8,128)(2,1)S(1)}, bf16[128,384]{1,0:T(8,128)(2,1)S(1)}, u32[]{:S(2)}, u32[]{:S(2)}) collective-permute-start(bf16[128,384]{1,0:T(8,128)(2,1)S(1)} %pad_maximum_fusion.13), channel_id=1, source_target_pairs={{0,4},{4,8},{8,12},{12,0},{1,5},{5,9},{9,13},{13,1},{2,6},{6,10},{... | collective-permute-start | bytes 294920 | tf_op jit(solution)/shard_map/ppermute | solution.py:180
  105.3 13.0 %copy-start.17 = (bf16[64,512]{1,0:T(8,128)(2,1)S(1)}, bf16[64,512]{1,0:T(8,128)(2,1)}, u32[]{:S(2)}) copy-start(bf16[64,512]{1,0:T(8,128)(2,1)} %copy-done.16) | copy-start | bytes 196612
  105.3 13.0 %copy-start.19 = (bf16[64,512]{1,0:T(8,128)(2,1)S(1)}, bf16[64,512]{1,0:T(8,128)(2,1)}, u32[]{:S(2)}) copy-start(bf16[64,512]{1,0:T(8,128)(2,1)} %copy-done.18) | copy-start | bytes 196612
  105.3 7.8 %collective-permute-start.28 = (bf16[128,384]{1,0:T(8,128)(2,1)S(1)}, bf16[128,384]{1,0:T(8,128)(2,1)S(1)}, u32[]{:S(2)}, u32[]{:S(2)}) collective-permute-start(bf16[128,384]{1,0:T(8,128)(2,1)S(1)} %pad_maximum_fusion.13), channel_id=1, source_target_pairs={{0,8},{4,12},{8,0},{12,4},{1,9},{5,13},{9,1},{13,5},{2,10},{6,14},... | collective-permute-start | bytes 294920 | tf_op jit(solution)/shard_map/ppermute | solution.py:180
  107.5 6.7 %collective-permute-start.29 = (bf16[128,384]{1,0:T(8,128)(2,1)S(1)}, bf16[128,384]{1,0:T(8,128)(2,1)S(1)}, u32[]{:S(2)}, u32[]{:S(2)}) collective-permute-start(bf16[128,384]{1,0:T(8,128)(2,1)S(1)} %pad_maximum_fusion.13), channel_id=1, source_target_pairs={{0,12},{4,0},{8,4},{12,8},{1,13},{5,1},{9,5},{13,9},{2,14},{6,2},{... | collective-permute-start | bytes 294920 | tf_op jit(solution)/shard_map/ppermute | solution.py:180
  (26 other events, 42.2 us)

commit v2 on v0

--- a/solution.py
+++ b/solution.py
@@ -1,9 +1,13 @@
+import functools
 import math
 
 import jax
 import jax.numpy as jnp
 from jax import lax
+from jax.experimental import pallas as pl
+from jax.experimental.pallas import tpu as pltpu
 from jax.sharding import PartitionSpec as P
+
 
 GROUP = 16
 MB_RESP = 8
@@ -56,7 +60,7 @@
     )
 
 
-def local(
+def general(
     hidden,
     unembed,
     value_proj,
@@ -145,7 +149,7 @@
         grad_projected = contract_last(upstream, w_second).astype(jnp.bfloat16)
         partial_norm = contract_last(grad_projected, w_first)
         grad_normed = lax.psum(partial_norm.astype(jnp.bfloat16), "tensor").astype(jnp.float32)
-        values, inverse, unused_normed = norm_forward(entering, norm_gain)
+        values, inverse, _ = norm_forward(entering, norm_gain)
         grad_entering = (
             upstream.astype(jnp.float32) + norm_backward(values, inverse, norm_gain, grad_normed)
         ).astype(jnp.bfloat16)
@@ -175,6 +179,548 @@
     return (grad_value, grad_output)
 
 
+def rotate(block, axis, distance):
+    count = lax.axis_size(axis)
+    return lax.ppermute(block, axis, [(i, (i + distance) % count) for i in range(count)])
+
+
+def swap(block, axis):
+    return rotate(block, axis, 1)
+
+
+PREP_LIMIT = 60 * 1024 * 1024
+VMEM = pl.BlockSpec(memory_space=pltpu.VMEM)
+SMEM = pl.BlockSpec(memory_space=pltpu.SMEM)
+HBM = pl.BlockSpec(memory_space=pltpu.HBM)
+
+
+def on_core(body, outs, operands, flops, moved, scratch=(), specs=None, limit=32 * 1024 * 1024):
+    return pl.pallas_call(
+        body,
+        out_shape=outs,
+        in_specs=[SMEM] + (specs or [VMEM] * (len(operands) - 1)),
+        out_specs=[VMEM] * len(outs),
+        scratch_shapes=list(scratch),
+        cost_estimate=pl.CostEstimate(flops=flops, bytes_accessed=moved, transcendentals=0),
+        compiler_params=pltpu.CompilerParams(vmem_limit_bytes=limit),
+    )(*operands)
+
+
+def shape_of(rows, cols, dtype=jnp.bfloat16):
+    return jax.ShapeDtypeStruct((rows, cols), dtype)
+
+
+def dot_nt(left, right):
+    return lax.dot_general(
+        left, right, (((1,), (1,)), ((), ())), preferred_element_type=jnp.float32
+    )
+
+
+def dot_nn(left, right):
+    return lax.dot_general(
+        left, right, (((1,), (0,)), ((), ())), preferred_element_type=jnp.float32
+    )
+
+
+def tile_at(index, size):
+    return pl.ds(pl.multiple_of(index * size, size), size)
+
+
+def fetch(pairs, sems):
+    copies = [pltpu.make_async_copy(src, dst, sems.at[i]) for i, (src, dst) in enumerate(pairs)]
+    for copy in copies:
+        copy.start()
+    return copies
+
+
+def prep_body(count, place, hidden, unembed, value_proj, output_proj, gains, *refs):
+    f32, bf16 = jnp.float32, jnp.bfloat16
+    pieces, (ab, across, gain_out) = refs[:count], refs[count : count + 3]
+    held, value_held, output_held, sems = refs[count + 3 :]
+    first, dp_index, tensor_index = place[0] == 1, place[1], place[2]
+    rows, width = pieces[0].shape
+    half = output_proj.shape[0]
+    at = tile_at(tensor_index, rows)
+
+    def rows_from(source):
+        pairs = []
+        for d in range(count):
+            col = tile_at(lax.rem(dp_index + d, count), width)
+            pairs.append((source.at[at, col], held.at[d]))
+        return [pltpu.make_async_copy(*pair, sems.at[i]) for i, pair in enumerate(pairs)]
+
+    def start_rows(source):
+        for copy in rows_from(source):
+            copy.start()
+
+    loads = [
+        pltpu.make_async_copy(value_proj, value_held, sems.at[count]),
+        pltpu.make_async_copy(output_proj, output_held, sems.at[count + 1]),
+    ]
+    for load in loads:
+        load.start()
+    pl.when(first)(lambda: start_rows(hidden))
+    pl.when(jnp.logical_not(first))(lambda: start_rows(unembed))
+    gain = gains[:, tile_at(dp_index, width)]
+    gain_out[...] = gain
+    loads[0].wait()
+    scaled = (value_held[...].astype(f32).T * gain).astype(bf16)
+    loads[1].wait()
+    ab[:half, :] = scaled
+    ab[half:, :] = output_held[...]
+    across[...] = jnp.where(first, output_held[...], scaled)
+    for d, copy in enumerate(rows_from(hidden)):
+        copy.wait()
+        pieces[d][...] = held[d]
+
+
+def column_body(
+    place, lengths, assign, survive, advantage, hidden, unembed, base, gap, cols, held, sems
+):
+    f32 = jnp.float32
+    tensor_index = place[2]
+    positions, resp_count = base.shape
+    half_resp = resp_count // 2
+    rows = half_resp * positions
+    at = tile_at(tensor_index, rows)
+    copies = fetch([(hidden.at[at], held.at[0]), (unembed.at[at], held.at[1])], sems)
+
+    def spread(scalars):
+        return jnp.concatenate([jnp.full((positions, 1), v, f32) for v in scalars], axis=0)
+
+    def tall(array):
+        both = array[...].T
+        mine = jnp.where(tensor_index == 0, both[:half_resp], both[half_resp:])
+        wide = jnp.concatenate(
+            [jnp.broadcast_to(mine[r : r + 1, :], (positions, positions)) for r in range(half_resp)],
+            axis=0,
+        )
+        row = lax.broadcasted_iota(jnp.int32, (rows, positions), 0)
+        lane = lax.broadcasted_iota(jnp.int32, (rows, positions), 1)
+        return jnp.sum(
+            jnp.where(lane == lax.rem(row, positions), wide, 0.0), axis=-1, keepdims=True
+        )
+
+    here = [tensor_index * half_resp + r for r in range(half_resp)]
+    listed = []
+    for r in here:
+        found = assign[0] == r
+        for k in range(1, resp_count):
+            found = found | (assign[k] == r)
+        listed.append(jnp.where(found, 1.0, 0.0))
+    group = resp_count // survive.shape[0]
+    tokens = jnp.float32(0.0)
+    for r in range(resp_count):
+        tokens = tokens + (survive[r // group] * lengths[r]).astype(f32)
+    listed = spread(listed)
+    length = spread([lengths[r].astype(f32) for r in here])
+    adv = spread([advantage[r] for r in here])
+    position = lax.broadcasted_iota(jnp.int32, (rows, 1), 0)
+    position = lax.rem(position, positions).astype(f32)
+    gap_rows = tall(gap)
+    clipped = (adv > 0) & (gap_rows > clip_high) | (adv < 0) & (gap_rows < clip_low)
+    used = (position < length) & (listed > 0) & jnp.logical_not(clipped)
+    weight = jnp.where(used, -loss_scale * adv, 0.0)
+    for copy in copies:
+        copy.wait()
+    hid, un = held[0].astype(f32), held[1].astype(f32)
+    square0 = jnp.sum(hid * hid, axis=-1, keepdims=True)
+    dot0 = jnp.sum(hid * un, axis=-1, keepdims=True)
+    lane = lax.broadcasted_iota(jnp.int32, cols.shape, 1)
+    out = jnp.zeros(cols.shape, f32)
+    for k, value in enumerate((square0, dot0, weight, tall(base), listed, spread([tokens] * half_resp))):
+        out = jnp.where(lane == k, value, out)
+    cols[...] = out
+
+
+def product_body(count, place, ab, ab_other, c_own, *refs):
+    first, dp_index, group_index = place[0] == 1, place[1], place[3]
+    own_out, sends, scratch = refs[0], refs[1:-1], refs[-1]
+    half = c_own.shape[0]
+    rows = scratch.shape[0]
+    at = tile_at(group_index, rows)
+    low = pl.ds(half + pl.multiple_of(group_index * rows, rows), rows)
+    left = jnp.where(first, ab[low, :], c_own[at, :])
+    for k, source in enumerate((ab, ab_other)):
+        right = jnp.where(first, source[half:, :], source[:half, :])
+        scratch[:, k * half : (k + 1) * half] = dot_nt(left, right)
+    step = rows // count
+    own_out[...] = scratch[tile_at(dp_index, step), :]
+    for d, send in enumerate(sends):
+        send[...] = scratch[tile_at(lax.rem(dp_index + d + 1, count), step), :].astype(jnp.bfloat16)
+
+
+def total_body(place, own, *refs):
+    total = own[...]
+    for ref in refs[:-1]:
+        total = total + ref[...].astype(jnp.float32)
+    refs[-1][...] = total.astype(jnp.bfloat16)
+
+
+def order_body(count, place, *refs):
+    dp_index, out = place[1], refs[-1]
+    step = refs[0].shape[0]
+    for d in range(count):
+        out[tile_at(lax.rem(dp_index + count - d, count), step), :] = refs[d][...]
+
+
+def group_body(count, place, *refs):
+    group_index, out = place[3], refs[-1]
+    step = refs[0].shape[0]
+    for d in range(count):
+        out[tile_at(lax.rem(group_index + count - d, count), step), :] = refs[d][...]
+
+
+def sum_body(width, place, cols, own, *refs):
+    backs, (mine, early) = refs[:-2], refs[-2:]
+    total = own[...]
+    for ref in backs:
+        total = total + ref[...].astype(jnp.float32)
+    total = total.astype(jnp.bfloat16)
+    mine[...] = total
+    size = early.shape[1]
+    r0 = lax.rsqrt(cols[:, 0:1] / width + eps_norm)
+    scaled = (r0 * total[:, :size].astype(jnp.float32)).astype(jnp.bfloat16)
+    early[...] = jnp.where(place[0] == 1, scaled, total[:, size : 2 * size])
+
+
+def stage_body(count, flag, *refs):
+    pieces, (ab, ab_other, c_own, c_other) = refs[:count], refs[count : count + 4]
+    rows_out, own_out = refs[count + 4 : count + 6]
+    back_out = refs[count + 6 :]
+    rows, half = pieces[0].shape[0], c_own.shape[0]
+    for i, piece in enumerate(pieces):
+        rows_out[i * rows : (i + 1) * rows, :] = piece[...]
+    blocks = [
+        (ab, 0),
+        (ab_other, 0),
+        (ab, half),
+        (ab_other, half),
+        (c_own, 0),
+        (c_other, 0),
+    ]
+    for k, (block, start) in enumerate(blocks):
+        product = dot_nt(rows_out[...], block[start : start + half, :])
+        cols = slice(k * half, (k + 1) * half)
+        own_out[:, cols] = product[:rows]
+        for i, back in enumerate(back_out):
+            back[:, cols] = product[(i + 1) * rows : (i + 2) * rows].astype(jnp.bfloat16)
+
+
+def value_body(
+    width, flag, mine, theirs, grown, across, grown_other, across_other, cols, late_out
+):
+    f32, bf16 = jnp.float32, jnp.bfloat16
+    half = grown.shape[0]
+    first = flag[0] == 1
+
+    def part(own, other, index):
+        at = slice(index * half, (index + 1) * half)
+        return jnp.where(first, own[:, at].astype(f32), other[:, at].astype(f32))
+
+    a0 = [part(mine, theirs, i) for i in (0, 1)]
+    b0 = [part(mine, theirs, i) for i in (2, 3)]
+    a1 = [part(mine, theirs, i) for i in (4, 5)]
+    t1 = [part(theirs, mine, i) for i in (2, 3)]
+    t0 = [part(theirs, mine, i) for i in (4, 5)]
+    square0, dot0, weight = cols[:, 0:1], cols[:, 1:2], cols[:, 2:3]
+    base, listed, tokens = cols[:, 3:4], cols[:, 4:5], cols[:, 5:6]
+
+    def row_sum(pair):
+        return jnp.sum(pair[0] + pair[1], axis=-1, keepdims=True)
+
+    def square(own, other):
+        return ((own[:, :half], own[:, half:]), (other[:, half:], other[:, :half]))
+
+    gram = square(
+        jnp.where(first, grown[...], across[...]), jnp.where(first, grown_other[...], across_other[...])
+    )
+    link = square(
+        jnp.where(first, across[...], grown[...]), jnp.where(first, across_other[...], grown_other[...])
+    )
+    r0 = lax.rsqrt(square0 / width + eps_norm)
+    p0b = [(r0 * v).astype(bf16) for v in a0]
+    p0 = [v.astype(f32) for v in p0b]
+    linked = [dot_nn(p0b[0], link[0][i]) + dot_nn(p0b[1], link[1][i]) for i in (0, 1)]
+    low = [b0[i] + dot_nn(p0b[0], gram[0][i]) + dot_nn(p0b[1], gram[1][i]) for i in (0, 1)]
+    square1 = square0 + row_sum([p0[i] * (b0[i] + low[i]) for i in (0, 1)])
+    r1 = lax.rsqrt(jnp.maximum(square1, 0.0) / width + eps_norm)
+    p1 = [r1 * (a1[i] + linked[i]) for i in (0, 1)]
+    logit = dot0 + row_sum([p0[i] * t0[i] + p1[i] * t1[i] for i in (0, 1)])
+    seed = weight * jnp.exp(jnp.where(listed > 0.0, logit - base, 0.0))
+    gp1 = [seed * v for v in t1]
+    c1 = r1 * r1 * row_sum([gp1[i] * p1[i] for i in (0, 1)]) / width
+    gp1b = [v.astype(bf16) for v in gp1]
+    back = [dot_nt(gp1b[0], link[i][0]) + dot_nt(gp1b[1], link[i][1]) for i in (0, 1)]
+    gp0 = [seed * t0[i] + r1 * back[i] - c1 * low[i] for i in (0, 1)]
+    late = [jnp.where(first, r0 * gp0[i], seed * p1[i]).astype(bf16) for i in (0, 1)]
+    lane = lax.broadcasted_iota(jnp.int32, (mine.shape[0], 128), 1)
+    extra = jnp.zeros((mine.shape[0], 128), f32)
+    for k, value in enumerate((seed, r1, c1, tokens)):
+        high = value.astype(bf16).astype(f32)
+        extra = jnp.where(lane == k, high, jnp.where(lane == k + 4, value - high, extra))
+    late_out[:, :half] = late[0]
+    late_out[:, half : 2 * half] = late[1]
+    late_out[:, 2 * half :] = extra.astype(bf16)
+
+
+def chunk_of(width):
+    return 256 if width % 256 == 0 else width
+
+
+def middle_body(
+    flag,
+    own,
+    cross,
+    own_other,
+    cross_other,
+    early,
+    early_cross,
+    early_other,
+    early_cross_other,
+    ab,
+    ab_other,
+    c_own,
+    c_other,
+    gain,
+    x1_out,
+    n1_out,
+    right_out,
+):
+    f32, bf16 = jnp.float32, jnp.bfloat16
+    first = flag[0] == 1
+    half, width = c_own.shape
+    rows = own.shape[0]
+    step = chunk_of(width)
+    halves = ((own, cross, early, early_cross, 0), (own_other, cross_other, early_other, early_cross_other, 1))
+    for h, (here, there, e_here, e_there, flipped) in enumerate(halves):
+        p0 = jnp.where(first, e_here[...], e_there[...])
+        t1 = jnp.where(first, e_there[...], e_here[...])
+        mine, other = (slice(half, 2 * half), slice(0, half))[:: 1 if flipped else -1]
+        at = slice(h * rows, (h + 1) * rows)
+        for k in range(0, width, step):
+            col = slice(k, k + step)
+            wo_own = jnp.where(first, ab[half:, col], c_own[:, col])
+            wo_other = jnp.where(first, ab_other[half:, col], c_other[:, col])
+            hid = jnp.where(first, here[:, col], there[:, col]).astype(f32)
+            x1 = hid + dot_nn(p0[:, mine], wo_own) + dot_nn(p0[:, other], wo_other)
+            x1_out[at, col] = x1.astype(bf16)
+            n1 = dot_nn(t1[:, mine], c_own[:, col]) + dot_nn(t1[:, other], c_other[:, col])
+            n1_out[at, col] = n1.astype(bf16)
+            right = jnp.where(first, hid, x1) * gain[:, col]
+            right_out[col, at] = right.astype(bf16).T
+
+
+def last_body(
+    count,
+    flag,
+    *refs,
+):
+    f32, bf16 = jnp.float32, jnp.bfloat16
+    pieces, pieces_other = refs[:count], refs[count : 2 * count]
+    (own, cross, own_other, cross_other, early, early_cross, early_other, early_cross_other) = refs[
+        2 * count : 2 * count + 8
+    ]
+    x1, n1, right, value_out, output_out, left_scr = refs[2 * count + 8 :]
+    first = flag[0] == 1
+    half = value_out.shape[1]
+    width = right.shape[0]
+    rows = own.shape[0]
+    h = rows // count
+    step = chunk_of(width)
+    both = [*pieces, *pieces_other]
+    ext = jnp.concatenate([p[:, 2 * half :] for p in both], axis=0).astype(f32)
+    ext = ext[:, 0:4] + ext[:, 4:8]
+    seed, r1, c1 = ext[:, 0:1], ext[:, 1:2], ext[:, 2:3]
+    tokens = jnp.sum(ext[:, 3:4]) / (2.0 * h)
+    scale = 1.0 / tokens
+    late = jnp.concatenate(
+        [p[:, :half] for p in pieces] + [p[:, half : 2 * half] for p in pieces_other], axis=0
+    )
+    e_here = jnp.concatenate([early[:, :half], early_other[:, half:]], axis=0)
+    e_there = jnp.concatenate([early_cross[:, :half], early_cross_other[:, half:]], axis=0)
+    value_left = jnp.where(first, late, (seed * r1 * e_here.astype(f32)).astype(bf16))
+    left_scr[...] = jnp.where(first, e_here, late).T
+    value_out[...] = dot_nn(right[...], value_left) * scale
+    factor = seed * r1
+    for k in range(0, width, step):
+        col = slice(k, k + step)
+        here = jnp.concatenate([own[:, col], own_other[:, col]], axis=0)
+        there = jnp.concatenate([cross[:, col], cross_other[:, col]], axis=0)
+        grad = (
+            seed * there.astype(f32)
+            + factor * n1[:, col].astype(f32)
+            - c1 * x1[:, col].astype(f32)
+        ).astype(bf16)
+        output_out[:, col] = dot_nn(left_scr[...], jnp.where(first, grad, here)) * scale
+
+
+def low_rank(
+    hidden,
+    unembed,
+    value_proj,
+    output_proj,
+    norm_gains,
+    survive,
+    lengths,
+    assign,
+    advantage,
+    reference_logit,
+    recorded_gap,
+):
+    f32 = jnp.float32
+    resp_count, positions, model_width = hidden.shape
+    _, own_width, half_value = value_proj.shape
+    value_width = 2 * half_value
+    dp_count, group_count = lax.axis_size("dp"), lax.axis_size("groups")
+    names = ("dp", "tensor", "groups")
+    place = jnp.stack(
+        [(lax.axis_index("section") == 0).astype(jnp.int32)] + [lax.axis_index(a) for a in names]
+    )
+    half_rows = resp_count // 2 * positions
+    all_rows = dp_count * half_rows
+    shifts = range(1, dp_count)
+    hidden = hidden.reshape(resp_count * positions, model_width)
+    unembed = unembed.reshape(resp_count * positions, model_width)
+
+    def across_dp(block):
+        return [block] + [rotate(block, "dp", d) for d in shifts]
+
+    *pieces, ab, payload, gain = on_core(
+        functools.partial(prep_body, dp_count),
+        [shape_of(half_rows, own_width)] * dp_count
+        + [
+            shape_of(value_width, own_width),
+            shape_of(half_value, own_width),
+            shape_of(1, own_width, f32),
+        ],
+        [place, hidden, unembed, value_proj[0], output_proj[0], norm_gains],
+        half_rows * model_width,
+        8 * half_rows * model_width,
+        [
+            pltpu.VMEM((dp_count, half_rows, own_width), jnp.bfloat16),
+            pltpu.VMEM((own_width, half_value), jnp.bfloat16),
+            pltpu.VMEM((half_value, own_width), jnp.bfloat16),
+            pltpu.SemaphoreType.DMA((dp_count + 2,)),
+        ],
+        [HBM, HBM, HBM, HBM, VMEM],
+        limit=PREP_LIMIT,
+    )
+    c_own = swap(payload, "section")
+    arrived = [pieces[0]] + [rotate(pieces[d], "dp", d) for d in shifts]
+    ab_other = swap(ab, "tensor")
+    c_other = swap(c_own, "tensor")
+    (cols,) = on_core(
+        column_body,
+        [shape_of(half_rows, 128, f32)],
+        [place, lengths, assign, survive, advantage, hidden, unembed, reference_logit.T, recorded_gap.T],
+        half_rows * model_width,
+        4 * half_rows * model_width,
+        [
+            pltpu.VMEM((2, half_rows, model_width), jnp.bfloat16),
+            pltpu.SemaphoreType.DMA((2,)),
+        ],
+        [SMEM] * 4 + [HBM] * 2 + [VMEM] * 2,
+        limit=PREP_LIMIT,
+    )
+
+    rows_here, summed, *backs = on_core(
+        functools.partial(stage_body, dp_count),
+        [shape_of(all_rows, own_width), shape_of(half_rows, 3 * value_width, f32)]
+        + [shape_of(half_rows, 3 * value_width) for d in shifts],
+        [place, *arrived, ab, ab_other, c_own, c_other],
+        6 * all_rows * own_width * value_width,
+        2 * (4 * value_width + 2 * all_rows) * own_width,
+    )
+    backs = [rotate(backs[d - 1], "dp", -d) for d in shifts]
+    mine, early = on_core(
+        functools.partial(sum_body, model_width),
+        [shape_of(half_rows, 3 * value_width), shape_of(half_rows, value_width)],
+        [place, cols, summed, *backs],
+        9 * half_rows * value_width,
+        24 * half_rows * value_width,
+    )
+    theirs = swap(mine, "section")
+
+    part_rows = half_value // group_count
+    block_rows = part_rows // dp_count
+    own_part, *parts = on_core(
+        functools.partial(product_body, dp_count),
+        [shape_of(block_rows, value_width, f32)]
+        + [shape_of(block_rows, value_width) for d in shifts],
+        [place, ab, ab_other, c_own],
+        2 * part_rows * own_width * value_width,
+        4 * value_width * own_width,
+        [pltpu.VMEM((part_rows, value_width), f32)],
+    )
+    parts = [rotate(parts[d - 1], "dp", d) for d in shifts]
+    (total,) = on_core(
+        total_body,
+        [shape_of(block_rows, value_width)],
+        [place, own_part, *parts],
+        dp_count * block_rows * value_width,
+        4 * dp_count * block_rows * value_width,
+    )
+    (product,) = on_core(
+        functools.partial(order_body, dp_count),
+        [shape_of(part_rows, value_width)],
+        [place, *across_dp(total)],
+        part_rows * value_width,
+        4 * part_rows * value_width,
+    )
+    (grown,) = on_core(
+        functools.partial(group_body, group_count),
+        [shape_of(half_value, value_width)],
+        [place, product]
+        + [rotate(product, "groups", d) for d in range(1, group_count)],
+        half_value * value_width,
+        4 * half_value * value_width,
+    )
+    across = swap(grown, "section")
+    grown_other = swap(grown, "tensor")
+    across_other = swap(across, "tensor")
+
+    early = jnp.concatenate(across_dp(early))
+    early_cross = swap(early, "section")
+    early_other = swap(early, "tensor")
+    early_cross_other = swap(early_cross, "tensor")
+    cross = swap(rows_here, "section")
+    rows_other = swap(rows_here, "tensor")
+    cross_other = swap(cross, "tensor")
+    known = [rows_here, cross, rows_other, cross_other]
+    known += [early, early_cross, early_other, early_cross_other]
+    x1_rows, n1_rows, value_right = on_core(
+        middle_body,
+        [shape_of(2 * all_rows, own_width)] * 2 + [shape_of(own_width, 2 * all_rows)],
+        [place, *known, ab, ab_other, c_own, c_other, gain],
+        8 * all_rows * own_width * value_width,
+        16 * all_rows * own_width,
+    )
+
+    (late,) = on_core(
+        functools.partial(value_body, model_width),
+        [shape_of(half_rows, value_width + 128)],
+        [place, mine, theirs, grown, across, grown_other, across_other, cols],
+        6 * half_rows * value_width * value_width,
+        4 * value_width * value_width,
+    )
+    late = across_dp(late)
+    late_other = [swap(piece, "tensor") for piece in late]
+    grad_value, grad_output = on_core(
+        functools.partial(last_body, dp_count),
+        [shape_of(own_width, half_value, f32), shape_of(half_value, own_width, f32)],
+        [place, *late, *late_other, *known, x1_rows, n1_rows, value_right],
+        8 * all_rows * own_width * half_value,
+        24 * all_rows * own_width,
+        [pltpu.VMEM((half_value, 2 * all_rows), jnp.bfloat16)],
+    )
+    return (grad_value[None], grad_output[None])
+
+
+def named(*arrays):
+    return low_rank(*arrays)
+
+
 def solution(mesh):
     placed = (
         P(("groups", "dp"), None, None),
@@ -189,8 +735,9 @@
         P(("groups", "dp"), None),
         P(("groups", "dp"), None),
     )
+    two_by_two = mesh.shape["section"] == 2 and mesh.shape["tensor"] == 2
     return jax.shard_map(
-        local,
+        named if two_by_two else general,
         mesh=mesh,
         in_specs=placed,
         out_specs=(

time: 450 us -> 139 us (0.31)
  waiting for transfers between devices: 326 us -> 69.8 us
  other arithmetic: 32.2 us -> 0.66 us
  starting transfers between devices: 10.5 us -> 39.7 us
  local copies, waits for them, and re-layouts: 32.9 us -> 4.26 us
  Pallas kernels: 0 us -> 22.6 us
  matrix products: 19.3 us -> 0 us
  between operations: 15.3 us -> 1.57 us
  blocking collectives: 12.9 us -> 0 us
    all_gather x2 -> x0, waiting for transfers between devices: 101 us -> none  [the longest x1 52.5 us: local(): lax.all_gather(output_proj, 'dp', axis=2, tiled=True)]
    psum x5 -> x0, waiting for transfers between devices: 85.4 us -> none  [the longest x3 48.4 us: local(): lax.psum(partial_out.astype(jnp.bfloat16), 'tensor').astype(jnp.float32)]
    reduce_scatter x1 -> x0, waiting for transfers between devices: 80.2 us -> none  [local(): lax.psum_scatter(jnp.concatenate([contract_first(flat_normed, flat_grad_v...]
    ppermute x4 -> x36, starting transfers between devices: 10.2 us -> 39.7 us  [rotate(): lax.ppermute(block, axis, [(i, (i + distance) % count) for i in range(cou...]
    pallas_call x0 -> x11, Pallas kernels: none -> 22.6 us  [on_core(): pl.pallas_call(body, out_shape=outs, in_specs=[SMEM] + (specs or [VMEM] *...]
    dot_general x13 -> x0, matrix products: 19.3 us -> none  [the longest x5 6.28 us: contract_last(): lax.dot_general(left_rows, right_rows, (((1,), (1,)), ((), ())), preferre...]
    dynamic_update_slice x10 -> x0, other arithmetic: 14.3 us -> none  [put_slot(): lax.dynamic_update_index_in_dim(slot_store, jnp.where(active, new_value,...]
    psum x1 -> x0, blocking collectives: 12.9 us -> none  [local(): token_total = lax.psum(local_count, 'dp')]
  transfers between devices with their start and end apart: 12 -> 36, of which waited for: 12 -> 15; matrix products, arithmetic and copies ran while one was open for 6% -> 0% of each run, Pallas kernels for 0% -> 9%
where the time goes in v2:
time: 139 us
  waiting for transfers between devices  69.8 us (50%)
  starting transfers between devices  39.7 us (29%)
  Pallas kernels  22.6 us (16%)
  local copies, waits for them, and re-layouts  4.26 us (3%)
  between operations  1.57 us (1%)
    ppermute x36, waiting for transfers between devices, rotate(): lax.ppermute(block, axis, [(i, (i + distance) % count) for i in range(cou...  69.8 us
    ppermute x36, starting transfers between devices, rotate(): lax.ppermute(block, axis, [(i, (i + distance) % count) for i in range(cou...  39.7 us
    pallas_call x11, Pallas kernels, on_core(): pl.pallas_call(body, out_shape=outs, in_specs=[SMEM] + (specs or [VMEM] *...  22.6 us
    unnamed x25, local copies, waits for them, and re-layouts  4.26 us
  transfers between devices with their start and end apart: 36, of which 15 were waited for; matrix products, arithmetic and copies ran while one was open for 0% of the time, Pallas kernels for 9%

profile of v2, /device:TPU:0, one launch (start us, length us, event | category | flops | bytes accessed | tf_op | source)
XLA Modules:
  0.0 138.7 jit_solution(18117835338785832481)
XLA Ops:
  0.6 0.7 pad_add_fusion.place.flag
  1.3 3.8 %shard_map.123 = (bf16[64,1280]{1,0:T(8,128)(2,1)}, bf16[64,1280]{1,0:T(8,128)(2,1)}, bf16[64,1280]{1,0:T(8,128)(2,1)}, bf16[64,1280]{1,0:T(8,128)(2,1)}, bf16[5...) custom-call(s32[4]{0:T(128)} %pad_add_fusion.place.flag, bf16[128,5120]{1,0:T(8,128)(2,1)} %bitcast.12, ...), custom_call_target="tpu_custom_call" | custom-call | flops 327680 | bytes 2621440 | tf_op jit(solution)/shard_map/pallas_call | solution.py:198
  5.1 0.6 collective-permute-start.3
  5.7 2.6 %collective-permute-start.4 = (bf16[256,1280]{1,0:T(8,128)(2,1)}, bf16[256,1280]{1,0:T(8,128)(2,1)S(1)}, u32[]{:S(2)}, u32[]{:S(2)}) collective-permute-start(bf16[256,1280]{1,0:T(8,128)(2,1)} %get-tuple-element.30), channel_id=1, source_target_pairs={{0,2},{2,0},{1,3},{3,1},{4,6},{6,4},{5,7},{7,5},{8,10},{10,8},{9,1... | collective-permute-start | bytes 1966088 | tf_op jit(solution)/shard_map/ppermute | solution.py:184
  8.2 15.5 %collective-permute-done.4.refs_6_.c_own = bf16[256,1280]{1,0:T(8,128)(2,1)S(1)} collective-permute-done((bf16[256,1280]{1,0:T(8,128)(2,1)}, bf16[256,1280]{1,0:T(8,128)(2,1)S(1)}, u32[]{:S(2)}, u32[]{:S(2)}) %collective-permute-start.4) | collective-permute-done | bytes 655392 | tf_op jit(solution)/shard_map/ppermute | solution.py:184
  23.8 1.8 %collective-permute-start = (bf16[64,1280]{1,0:T(8,128)(2,1)}, bf16[64,1280]{1,0:T(8,128)(2,1)S(1)}, u32[]{:S(2)}, u32[]{:S(2)}) collective-permute-start(bf16[64,1280]{1,0:T(8,128)(2,1)} %get-tuple-element.26), channel_id=1, source_target_pairs={{0,4},{4,8},{8,12},{12,0},{1,5},{5,9},{9,13},{13,1},{2,6},{6,10},{... | collective-permute-start | bytes 491528 | tf_op jit(solution)/shard_map/ppermute | solution.py:184
  25.6 2.6 %collective-permute-start.1 = (bf16[64,1280]{1,0:T(8,128)(2,1)}, bf16[64,1280]{1,0:T(8,128)(2,1)S(1)}, u32[]{:S(2)}, u32[]{:S(2)}) collective-permute-start(bf16[64,1280]{1,0:T(8,128)(2,1)} %get-tuple-element.27), channel_id=1, source_target_pairs={{0,8},{4,12},{8,0},{12,4},{1,9},{5,13},{9,1},{13,5},{2,10},{6,14},... | collective-permute-start | bytes 491528 | tf_op jit(solution)/shard_map/ppermute | solution.py:184
  28.2 1.3 collective-permute-start.2
  29.5 3.5 %collective-permute-done.refs_1_ = bf16[64,1280]{1,0:T(8,128)(2,1)S(1)} collective-permute-done((bf16[64,1280]{1,0:T(8,128)(2,1)}, bf16[64,1280]{1,0:T(8,128)(2,1)S(1)}, u32[]{:S(2)}, u32[]{:S(2)}) %collective-permute-start) | collective-permute-done | bytes 163872 | tf_op jit(solution)/shard_map/ppermute | solution.py:184
  33.0 6.8 %collective-permute-done.1.refs_2_ = bf16[64,1280]{1,0:T(8,128)(2,1)S(1)} collective-permute-done((bf16[64,1280]{1,0:T(8,128)(2,1)}, bf16[64,1280]{1,0:T(8,128)(2,1)S(1)}, u32[]{:S(2)}, u32[]{:S(2)}) %collective-permute-start.1) | collective-permute-done | bytes 163872 | tf_op jit(solution)/shard_map/ppermute | solution.py:184
  39.9 1.5 %copy-done = bf16[512,1280]{1,0:T(8,128)(2,1)S(1)} copy-done((bf16[512,1280]{1,0:T(8,128)(2,1)S(1)}, bf16[512,1280]{1,0:T(8,128)(2,1)}, u32[]{:S(2)}) %copy-start) | copy-done | bytes 1310744
  41.4 0.9 copy-done.7
  42.3 2.5 %shard_map.124 = (bf16[256,1280]{1,0:T(8,128)(2,1)S(1)}, f32[64,1536]{1,0:T(8,128)S(1)}, bf16[64,1536]{1,0:T(8,128)(2,1)}, bf16[64,1536]{1,0:T(8,128)(2,1)}, bf16[64,1536]{1,0:T(8,128)(2,1)}) custom-call(s32[4]{0:T(128)S(1)} %copy-done.8, bf16[64,1280]{1,0:T(8,128)(2,1)S(1)} %copy-done.7, bf16[64,1280]{1,0:T(8,128)(2,1)S(1)} %collective-permute-done.refs_1_, ...), custom_call_target="tpu_custom_call" | custom-call | flops 1006632960 | bytes 6553600 | tf_op jit(solution)/shard_map/pallas_call | solution.py:198
  44.9 1.5 %collective-permute-start.27 = (bf16[256,1280]{1,0:T(8,128)(2,1)S(1)}, bf16[256,1280]{1,0:T(8,128)(2,1)}, u32[]{:S(2)}, u32[]{:S(2)}) collective-permute-start(bf16[256,1280]{1,0:T(8,128)(2,1)S(1)} %get-tuple-element.40.own.refs_8_), channel_id=1, source_target_pairs={{0,2},{2,0},{1,3},{3,1},{4,6},{6,4},{5,7},{7,5},{8,10},{10,8},{9,1... | collective-permute-start | bytes 1966088 | tf_op jit(solution)/shard_map/ppermute | solution.py:184
  46.3 1.1 shard_map.126
  47.5 4.0 %collective-permute-start.10 = (bf16[32,512]{1,0:T(8,128)(2,1)S(1)}, bf16[32,512]{1,0:T(8,128)(2,1)S(1)}, u32[]{:S(2)}, u32[]{:S(2)}) collective-permute-start(bf16[32,512]{1,0:T(8,128)(2,1)S(1)} %get-tuple-element.37), channel_id=1, source_target_pairs={{0,4},{4,8},{8,12},{12,0},{1,5},{5,9},{9,13},{13,1},{2,6},{6,10},{... | collective-permute-start | bytes 98312 | tf_op jit(solution)/shard_map/ppermute | solution.py:184
  51.5 1.6 %collective-permute-start.11 = (bf16[32,512]{1,0:T(8,128)(2,1)S(1)}, bf16[32,512]{1,0:T(8,128)(2,1)S(1)}, u32[]{:S(2)}, u32[]{:S(2)}) collective-permute-start(bf16[32,512]{1,0:T(8,128)(2,1)S(1)} %get-tuple-element.38), channel_id=1, source_target_pairs={{0,8},{4,12},{8,0},{12,4},{1,9},{5,13},{9,1},{13,5},{2,10},{6,14},... | collective-permute-start | bytes 98312 | tf_op jit(solution)/shard_map/ppermute | solution.py:184
  53.2 0.8 collective-permute-start.12
  54.0 0.8 collective-permute-done.10.refs_0_
  54.8 1.6 %collective-permute-done.11.refs_1_ = bf16[32,512]{1,0:T(8,128)(2,1)S(1)} collective-permute-done((bf16[32,512]{1,0:T(8,128)(2,1)S(1)}, bf16[32,512]{1,0:T(8,128)(2,1)S(1)}, u32[]{:S(2)}, u32[]{:S(2)}) %collective-permute-start.11) | collective-permute-done | bytes 32800 | tf_op jit(solution)/shard_map/ppermute | solution.py:184
  56.4 0.7 collective-permute-done.12.refs_2_
  57.9 3.6 %collective-permute-start.6 = (bf16[64,1536]{1,0:T(8,128)(2,1)}, bf16[64,1536]{1,0:T(8,128)(2,1)}, u32[]{:S(2)}, u32[]{:S(2)}) collective-permute-start(bf16[64,1536]{1,0:T(8,128)(2,1)} %get-tuple-element.32), channel_id=1, source_target_pairs={{0,12},{4,0},{8,4},{12,8},{1,13},{5,1},{9,5},{13,9},{2,14},{6,2},{... | collective-permute-start | bytes 589832 | tf_op jit(solution)/shard_map/ppermute | solution.py:184
  61.6 1.4 collective-permute-start.8
  62.9 1.0 collective-permute-done.13.refs_1_
  63.9 1.2 collective-permute-start.14
  65.1 14.2 %collective-permute-done.14.refs_2_ = bf16[32,512]{1,0:T(8,128)(2,1)S(1)} collective-permute-done((bf16[32,512]{1,0:T(8,128)(2,1)S(1)}, bf16[32,512]{1,0:T(8,128)(2,1)S(1)}, u32[]{:S(2)}, u32[]{:S(2)}) %collective-permute-start.14) | collective-permute-done | bytes 32800 | tf_op jit(solution)/shard_map/ppermute | solution.py:184
  79.3 2.9 %collective-permute-start.15 = (bf16[32,512]{1,0:T(8,128)(2,1)S(1)}, bf16[32,512]{1,0:T(8,128)(2,1)S(1)}, u32[]{:S(2)}, u32[]{:S(2)}) collective-permute-start(bf16[32,512]{1,0:T(8,128)(2,1)S(1)} %shard_map.127.refs_0_), channel_id=1, source_target_pairs={{0,12},{4,0},{8,4},{12,8},{1,13},{5,1},{9,5},{13,9},{2,14},{6,2},{... | collective-permute-start | bytes 98312 | tf_op jit(solution)/shard_map/ppermute | solution.py:184
  82.2 1.6 %collective-permute-done.15.refs_3_ = bf16[32,512]{1,0:T(8,128)(2,1)S(1)} collective-permute-done((bf16[32,512]{1,0:T(8,128)(2,1)S(1)}, bf16[32,512]{1,0:T(8,128)(2,1)S(1)}, u32[]{:S(2)}, u32[]{:S(2)}) %collective-permute-start.15) | collective-permute-done | bytes 32800 | tf_op jit(solution)/shard_map/ppermute | solution.py:184
  84.3 1.6 %collective-permute-start.16 = (bf16[128,512]{1,0:T(8,128)(2,1)S(1)}, bf16[128,512]{1,0:T(8,128)(2,1)}, u32[]{:S(2)}, u32[]{:S(2)}) collective-permute-start(bf16[128,512]{1,0:T(8,128)(2,1)S(1)} %shard_map.128.refs_0_), channel_id=1, source_target_pairs={{0,16},{16,0},{1,17},{17,1},{2,18},{18,2},{3,19},{19,3},{4,20},{20... | collective-permute-start | bytes 393224 | tf_op jit(solution)/shard_map/ppermute | solution.py:184
  86.6 3.1 %shard_map.122.cols = f32[64,128]{1,0:T(8,128)} custom-call(s32[4]{0:T(128)} %pad_add_fusion.place.flag, s32[16]{0:T(128)} %lengths.1, s32[16]{0:T(128)} %assign.1, s32[1]{0:T(128)S(6)} %copy.16.survive, f32[16]{0:T(128)} %advantage.1, bf16[128,5120]{1,0:T(8,128)(2,1)} %bitcast.13, bf16[128,5120]{1,0:T(8,128)(2,1)} %bitcast.15, f32[8,16]{1,0:T(8,128)} %bitcast.18, ...), custom_call_target="tpu_custom_call" | custom-call | flops 327680 | bytes 1310720 | tf_op jit(solution)/shard_map/pallas_call | solution.py:198
  89.9 1.0 copy-done.5
  90.8 0.8 copy-done.6
  91.6 1.2 shard_map.125
  92.9 4.7 %collective-permute-start.31 = (bf16[64,512]{1,0:T(8,128)(2,1)S(1)}, bf16[64,512]{1,0:T(8,128)(2,1)S(1)}, u32[]{:S(2)}, u32[]{:S(2)}) collective-permute-start(bf16[64,512]{1,0:T(8,128)(2,1)S(1)} %get-tuple-element.41), channel_id=1, source_target_pairs={{0,8},{4,12},{8,0},{12,4},{1,9},{5,13},{9,1},{13,5},{2,10},{6,14},... | collective-permute-start | bytes 196616 | tf_op jit(solution)/shard_map/ppermute | solution.py:184
  97.6 0.9 shard_map.129.grown
  98.6 1.5 %collective-permute-done.30 = bf16[64,512]{1,0:T(8,128)(2,1)S(1)} collective-permute-done((bf16[64,512]{1,0:T(8,128)(2,1)S(1)}, bf16[64,512]{1,0:T(8,128)(2,1)S(1)}, u32[]{:S(2)}, u32[]{:S(2)}) %collective-permute-start.30) | collective-permute-done | bytes 65568 | tf_op jit(solution)/shard_map/ppermute | solution.py:184
  100.6 2.1 %collective-permute-done.31 = bf16[64,512]{1,0:T(8,128)(2,1)S(1)} collective-permute-done((bf16[64,512]{1,0:T(8,128)(2,1)S(1)}, bf16[64,512]{1,0:T(8,128)(2,1)S(1)}, u32[]{:S(2)}, u32[]{:S(2)}) %collective-permute-start.31) | collective-permute-done | bytes 65568 | tf_op jit(solution)/shard_map/ppermute | solution.py:184
  103.2 0.6 collective-permute-start.18
  103.8 8.3 %collective-permute-done.9.theirs = bf16[64,1536]{1,0:T(8,128)(2,1)S(1)} collective-permute-done((bf16[64,1536]{1,0:T(8,128)(2,1)S(1)}, bf16[64,1536]{1,0:T(8,128)(2,1)S(1)}, u32[]{:S(2)}, u32[]{:S(2)}) %collective-permute-start.9) | collective-permute-done | bytes 196640 | tf_op jit(solution)/shard_map/ppermute | solution.py:184
  113.1 5.9 %collective-permute-done.33.early_cross.refs_13_ = bf16[256,512]{1,0:T(8,128)(2,1)S(1)} collective-permute-done((bf16[256,512]{1,0:T(8,128)(2,1)S(1)}, bf16[256,512]{1,0:T(8,128)(2,1)S(1)}, u32[]{:S(2)}, u32[]{:S(2)}) %collective-permute-start.33) | collective-permute-done | bytes 262176 | tf_op jit(solution)/shard_map/ppermute | solution.py:184
  119.1 1.7 %shard_map.130.refs_0_ = bf16[64,640]{1,0:T(8,128)(2,1)S(1)} custom-call(s32[4]{0:T(128)S(1)} %copy-done.9, bf16[64,1536]{1,0:T(8,128)(2,1)S(1)} %get-tuple-element.35.mine, bf16[64,1536]{1,0:T(8,128)(2,1)S(1)} %collective-permute-done.9.theirs, bf16[256,512]{1,0:T(8,128)(2,1)S(1)} %shard_map.129.grown, bf16[256,512]{1,0:T(8,128)(2,1)S(1)} %collective-permute-done.17.across, ...), custom_call_target="tpu_custom_call" | custom-call | flops 100663296 | bytes 1048576 | tf_op jit(solution)/shard_map/pallas_call | solution.py:198
  120.7 0.7 collective-permute-start.20
  121.5 0.8 collective-permute-start.21
  122.2 2.4 %collective-permute-start.22 = (bf16[64,640]{1,0:T(8,128)(2,1)S(1)}, bf16[64,640]{1,0:T(8,128)(2,1)S(1)}, u32[]{:S(2)}, u32[]{:S(2)}) collective-permute-start(bf16[64,640]{1,0:T(8,128)(2,1)S(1)} %shard_map.130.refs_0_), channel_id=1, source_target_pairs={{0,12},{4,0},{8,4},{12,8},{1,13},{5,1},{9,5},{13,9},{2,14},{6,2},{... | collective-permute-start | bytes 245768 | tf_op jit(solution)/shard_map/ppermute | solution.py:184
  124.7 3.3 %collective-permute-done.20.refs_1_ = bf16[64,640]{1,0:T(8,128)(2,1)S(1)} collective-permute-done((bf16[64,640]{1,0:T(8,128)(2,1)S(1)}, bf16[64,640]{1,0:T(8,128)(2,1)S(1)}, u32[]{:S(2)}, u32[]{:S(2)}) %collective-permute-start.20) | collective-permute-done | bytes 81952 | tf_op jit(solution)/shard_map/ppermute | solution.py:184
  128.0 3.0 %collective-permute-done.21.refs_2_ = bf16[64,640]{1,0:T(8,128)(2,1)S(1)} collective-permute-done((bf16[64,640]{1,0:T(8,128)(2,1)S(1)}, bf16[64,640]{1,0:T(8,128)(2,1)S(1)}, u32[]{:S(2)}, u32[]{:S(2)}) %collective-permute-start.21) | collective-permute-done | bytes 81952 | tf_op jit(solution)/shard_map/ppermute | solution.py:184
  131.6 2.9 %shard_map.131 = (bf16[512,1280]{1,0:T(8,128)(2,1)S(1)}, bf16[512,1280]{1,0:T(8,128)(2,1)S(1)}, bf16[1280,512]{1,0:T(8,128)(2,1)S(1)}) custom-call(s32[4]{0:T(128)S(1)} %copy-done.9, bf16[256,1280]{1,0:T(8,128)(2,1)S(1)} %get-tuple-element.40.own.refs_8_, bf16[256,1280]{1,0:T(8,128)(2,1)} %collective-permute-done.27.cross.refs_9_, ...), custom_call_target="tpu_custom_call" | custom-call | flops 1342177280 | bytes 5242880 | tf_op jit(solution)/shard_map/pallas_call | solution.py:198
  134.5 4.2 %shard_map.132 = (f32[1280,256]{1,0:T(8,128)}, f32[256,1280]{1,0:T(8,128)}) custom-call(s32[4]{0:T(128)S(1)} %copy-done.9, bf16[64,640]{1,0:T(8,128)(2,1)S(1)} %shard_map.130.refs_0_, bf16[64,640]{1,0:T(8,128)(2,1)S(1)} %collective-permute-done.20.refs_1_, bf16[64,640]{1,0:T(8,128)(2,1)S(1)} %collective-permute-done.21.refs_2_, ...), custom_call_target="tpu_custom_call" | custom-call | flops 671088640 | bytes 7864320 | tf_op jit(solution)/shard_map/pallas_call | solution.py:198
  (62 shorter events, 4.2 us)
Async XLA Ops:
  1.3 38.5 %copy-start.8 = (s32[4]{0:T(128)S(1)}, s32[4]{0:T(128)}, u32[]{:S(2)}) copy-start(s32[4]{0:T(128)} %pad_add_fusion.place.flag) | copy-start | bytes 52
  5.1 34.7 %collective-permute-start.3 = (bf16[512,1280]{1,0:T(8,128)(2,1)}, bf16[512,1280]{1,0:T(8,128)(2,1)S(1)}, u32[]{:S(2)}, u32[]{:S(2)}) collective-permute-start(bf16[512,1280]{1,0:T(8,128)(2,1)} %get-tuple-element.29.refs_4_.ab), channel_id=1, source_target_pairs={{0,1},{1,0},{2,3},{3,2},{4,5},{5,4},{6,7},{7,6},{8,9},{9,8},{10,11... | collective-permute-start | bytes 3932168 | tf_op jit(solution)/shard_map/ppermute | solution.py:184
  5.7 18.1 %collective-permute-start.4 = (bf16[256,1280]{1,0:T(8,128)(2,1)}, bf16[256,1280]{1,0:T(8,128)(2,1)S(1)}, u32[]{:S(2)}, u32[]{:S(2)}) collective-permute-start(bf16[256,1280]{1,0:T(8,128)(2,1)} %get-tuple-element.30), channel_id=1, source_target_pairs={{0,2},{2,0},{1,3},{3,1},{4,6},{6,4},{5,7},{7,5},{8,10},{10,8},{9,1... | collective-permute-start | bytes 1966088 | tf_op jit(solution)/shard_map/ppermute | solution.py:184
  23.8 16.1 %collective-permute-start.5 = (bf16[256,1280]{1,0:T(8,128)(2,1)S(1)}, bf16[256,1280]{1,0:T(8,128)(2,1)S(1)}, u32[]{:S(2)}, u32[]{:S(2)}) collective-permute-start(bf16[256,1280]{1,0:T(8,128)(2,1)S(1)} %collective-permute-done.4.refs_6_.c_own), channel_id=1, source_target_pairs={{0,1},{1,0},{2,3},{3,2},{4,5},{5,4},{6,7},{7,6},{8,9},{9,8},{10,11... | collective-permute-start | bytes 1966088 | tf_op jit(solution)/shard_map/ppermute | solution.py:184
  23.8 9.2 %collective-permute-start = (bf16[64,1280]{1,0:T(8,128)(2,1)}, bf16[64,1280]{1,0:T(8,128)(2,1)S(1)}, u32[]{:S(2)}, u32[]{:S(2)}) collective-permute-start(bf16[64,1280]{1,0:T(8,128)(2,1)} %get-tuple-element.26), channel_id=1, source_target_pairs={{0,4},{4,8},{8,12},{12,0},{1,5},{5,9},{9,13},{13,1},{2,6},{6,10},{... | collective-permute-start | bytes 491528 | tf_op jit(solution)/shard_map/ppermute | solution.py:184
  25.6 14.2 %collective-permute-start.1 = (bf16[64,1280]{1,0:T(8,128)(2,1)}, bf16[64,1280]{1,0:T(8,128)(2,1)S(1)}, u32[]{:S(2)}, u32[]{:S(2)}) collective-permute-start(bf16[64,1280]{1,0:T(8,128)(2,1)} %get-tuple-element.27), channel_id=1, source_target_pairs={{0,8},{4,12},{8,0},{12,4},{1,9},{5,13},{9,1},{13,5},{2,10},{6,14},... | collective-permute-start | bytes 491528 | tf_op jit(solution)/shard_map/ppermute | solution.py:184
  28.2 11.6 %collective-permute-start.2 = (bf16[64,1280]{1,0:T(8,128)(2,1)}, bf16[64,1280]{1,0:T(8,128)(2,1)S(1)}, u32[]{:S(2)}, u32[]{:S(2)}) collective-permute-start(bf16[64,1280]{1,0:T(8,128)(2,1)} %get-tuple-element.28), channel_id=1, source_target_pairs={{0,12},{4,0},{8,4},{12,8},{1,13},{5,1},{9,5},{13,9},{2,14},{6,2},{... | collective-permute-start | bytes 491528 | tf_op jit(solution)/shard_map/ppermute | solution.py:184
  39.8 5.0 %copy-start.2 = (bf16[256,1280]{1,0:T(8,128)(2,1)}, bf16[256,1280]{1,0:T(8,128)(2,1)S(1)}, u32[]{:S(2)}) copy-start(bf16[256,1280]{1,0:T(8,128)(2,1)S(1)} %collective-permute-done.5.refs_7_.c_other) | copy-start | bytes 1966084
  39.8 1.6 %copy-start = (bf16[512,1280]{1,0:T(8,128)(2,1)S(1)}, bf16[512,1280]{1,0:T(8,128)(2,1)}, u32[]{:S(2)}) copy-start(bf16[512,1280]{1,0:T(8,128)(2,1)} %get-tuple-element.29.refs_4_.ab) | copy-start | bytes 3932164
  41.4 0.9 copy-start.7
  42.3 4.0 %copy-start.1 = (bf16[512,1280]{1,0:T(8,128)(2,1)S(1)}, bf16[512,1280]{1,0:T(8,128)(2,1)}, u32[]{:S(2)}) copy-start(bf16[512,1280]{1,0:T(8,128)(2,1)} %get-tuple-element.29.refs_4_.ab) | copy-start | bytes 3932164
  44.9 2.6 %copy-start.4 = (f32[64,1536]{1,0:T(8,128)}, f32[64,1536]{1,0:T(8,128)S(1)}, u32[]{:S(2)}) copy-start(f32[64,1536]{1,0:T(8,128)S(1)} %get-tuple-element.31.own) | copy-start | bytes 1179652
  44.9 58.3 %collective-permute-start.27 = (bf16[256,1280]{1,0:T(8,128)(2,1)S(1)}, bf16[256,1280]{1,0:T(8,128)(2,1)}, u32[]{:S(2)}, u32[]{:S(2)}) collective-permute-start(bf16[256,1280]{1,0:T(8,128)(2,1)S(1)} %get-tuple-element.40.own.refs_8_), channel_id=1, source_target_pairs={{0,2},{2,0},{1,3},{3,1},{4,6},{6,4},{5,7},{7,5},{8,10},{10,8},{9,1... | collective-permute-start | bytes 1966088 | tf_op jit(solution)/shard_map/ppermute | solution.py:184
  47.5 7.3 %collective-permute-start.10 = (bf16[32,512]{1,0:T(8,128)(2,1)S(1)}, bf16[32,512]{1,0:T(8,128)(2,1)S(1)}, u32[]{:S(2)}, u32[]{:S(2)}) collective-permute-start(bf16[32,512]{1,0:T(8,128)(2,1)S(1)} %get-tuple-element.37), channel_id=1, source_target_pairs={{0,4},{4,8},{8,12},{12,0},{1,5},{5,9},{9,13},{13,1},{2,6},{6,10},{... | collective-permute-start | bytes 98312 | tf_op jit(solution)/shard_map/ppermute | solution.py:184
  51.5 4.8 %collective-permute-start.11 = (bf16[32,512]{1,0:T(8,128)(2,1)S(1)}, bf16[32,512]{1,0:T(8,128)(2,1)S(1)}, u32[]{:S(2)}, u32[]{:S(2)}) collective-permute-start(bf16[32,512]{1,0:T(8,128)(2,1)S(1)} %get-tuple-element.38), channel_id=1, source_target_pairs={{0,8},{4,12},{8,0},{12,4},{1,9},{5,13},{9,1},{13,5},{2,10},{6,14},... | collective-permute-start | bytes 98312 | tf_op jit(solution)/shard_map/ppermute | solution.py:184
  53.2 3.9 %collective-permute-start.12 = (bf16[32,512]{1,0:T(8,128)(2,1)S(1)}, bf16[32,512]{1,0:T(8,128)(2,1)S(1)}, u32[]{:S(2)}, u32[]{:S(2)}) collective-permute-start(bf16[32,512]{1,0:T(8,128)(2,1)S(1)} %get-tuple-element.39), channel_id=1, source_target_pairs={{0,12},{4,0},{8,4},{12,8},{1,13},{5,1},{9,5},{13,9},{2,14},{6,2},{... | collective-permute-start | bytes 98312 | tf_op jit(solution)/shard_map/ppermute | solution.py:184
  57.7 6.2 %collective-permute-start.13 = (bf16[32,512]{1,0:T(8,128)(2,1)S(1)}, bf16[32,512]{1,0:T(8,128)(2,1)S(1)}, u32[]{:S(2)}, u32[]{:S(2)}) collective-permute-start(bf16[32,512]{1,0:T(8,128)(2,1)S(1)} %shard_map.127.refs_0_), channel_id=1, source_target_pairs={{0,4},{4,8},{8,12},{12,0},{1,5},{5,9},{9,13},{13,1},{2,6},{6,10},{... | collective-permute-start | bytes 98312 | tf_op jit(solution)/shard_map/ppermute | solution.py:184
  57.9 31.8 %collective-permute-start.6 = (bf16[64,1536]{1,0:T(8,128)(2,1)}, bf16[64,1536]{1,0:T(8,128)(2,1)}, u32[]{:S(2)}, u32[]{:S(2)}) collective-permute-start(bf16[64,1536]{1,0:T(8,128)(2,1)} %get-tuple-element.32), channel_id=1, source_target_pairs={{0,12},{4,0},{8,4},{12,8},{1,13},{5,1},{9,5},{13,9},{2,14},{6,2},{... | collective-permute-start | bytes 589832 | tf_op jit(solution)/shard_map/ppermute | solution.py:184
  61.5 28.3 %collective-permute-start.7 = (bf16[64,1536]{1,0:T(8,128)(2,1)}, bf16[64,1536]{1,0:T(8,128)(2,1)}, u32[]{:S(2)}, u32[]{:S(2)}) collective-permute-start(bf16[64,1536]{1,0:T(8,128)(2,1)} %get-tuple-element.33), channel_id=1, source_target_pairs={{0,8},{4,12},{8,0},{12,4},{1,9},{5,13},{9,1},{13,5},{2,10},{6,14},... | collective-permute-start | bytes 589832 | tf_op jit(solution)/shard_map/ppermute | solution.py:184
  61.6 28.3 %collective-permute-start.8 = (bf16[64,1536]{1,0:T(8,128)(2,1)}, bf16[64,1536]{1,0:T(8,128)(2,1)}, u32[]{:S(2)}, u32[]{:S(2)}) collective-permute-start(bf16[64,1536]{1,0:T(8,128)(2,1)} %get-tuple-element.34), channel_id=1, source_target_pairs={{0,4},{4,8},{8,12},{12,0},{1,5},{5,9},{9,13},{13,1},{2,6},{6,10},{... | collective-permute-start | bytes 589832 | tf_op jit(solution)/shard_map/ppermute | solution.py:184
  63.9 15.4 %collective-permute-start.14 = (bf16[32,512]{1,0:T(8,128)(2,1)S(1)}, bf16[32,512]{1,0:T(8,128)(2,1)S(1)}, u32[]{:S(2)}, u32[]{:S(2)}) collective-permute-start(bf16[32,512]{1,0:T(8,128)(2,1)S(1)} %shard_map.127.refs_0_), channel_id=1, source_target_pairs={{0,8},{4,12},{8,0},{12,4},{1,9},{5,13},{9,1},{13,5},{2,10},{6,14},... | collective-permute-start | bytes 98312 | tf_op jit(solution)/shard_map/ppermute | solution.py:184
  79.3 4.5 %collective-permute-start.15 = (bf16[32,512]{1,0:T(8,128)(2,1)S(1)}, bf16[32,512]{1,0:T(8,128)(2,1)S(1)}, u32[]{:S(2)}, u32[]{:S(2)}) collective-permute-start(bf16[32,512]{1,0:T(8,128)(2,1)S(1)} %shard_map.127.refs_0_), channel_id=1, source_target_pairs={{0,12},{4,0},{8,4},{12,8},{1,13},{5,1},{9,5},{13,9},{2,14},{6,2},{... | collective-permute-start | bytes 98312 | tf_op jit(solution)/shard_map/ppermute | solution.py:184
  84.3 13.3 %collective-permute-start.16 = (bf16[128,512]{1,0:T(8,128)(2,1)S(1)}, bf16[128,512]{1,0:T(8,128)(2,1)}, u32[]{:S(2)}, u32[]{:S(2)}) collective-permute-start(bf16[128,512]{1,0:T(8,128)(2,1)S(1)} %shard_map.128.refs_0_), channel_id=1, source_target_pairs={{0,16},{16,0},{1,17},{17,1},{2,18},{18,2},{3,19},{19,3},{4,20},{20... | collective-permute-start | bytes 393224 | tf_op jit(solution)/shard_map/ppermute | solution.py:184
  86.6 3.3 %copy-start.9 = (s32[4]{0:T(128)S(1)}, s32[4]{0:T(128)}, u32[]{:S(2)}) copy-start(s32[4]{0:T(128)} %pad_add_fusion.place.flag) | copy-start | bytes 52
  89.7 32.5 %collective-permute-start.28 = (bf16[256,1280]{1,0:T(8,128)(2,1)S(1)}, bf16[256,1280]{1,0:T(8,128)(2,1)S(1)}, u32[]{:S(2)}, u32[]{:S(2)}) collective-permute-start(bf16[256,1280]{1,0:T(8,128)(2,1)S(1)} %get-tuple-element.40.own.refs_8_), channel_id=1, source_target_pairs={{0,1},{1,0},{2,3},{3,2},{4,5},{5,4},{6,7},{7,6},{8,9},{9,8},{10,11... | collective-permute-start | bytes 1966088 | tf_op jit(solution)/shard_map/ppermute | solution.py:184
  89.8 1.0 copy-start.5
  90.8 0.8 copy-start.6
  92.8 38.7 %copy-start.3 = (bf16[256,1280]{1,0:T(8,128)(2,1)S(1)}, bf16[256,1280]{1,0:T(8,128)(2,1)}, u32[]{:S(2)}) copy-start(bf16[256,1280]{1,0:T(8,128)(2,1)} %copy-done.2) | copy-start | bytes 1966084
  92.9 38.7 %copy-start.10 = (f32[1,1280]{1,0:T(1,128)S(1)}, f32[1,1280]{1,0:T(1,128)}, u32[]{:S(2)}) copy-start(f32[1,1280]{1,0:T(1,128)} %get-tuple-element.42.gain) | copy-start | bytes 15364
  92.9 7.2 %collective-permute-start.30 = (bf16[64,512]{1,0:T(8,128)(2,1)S(1)}, bf16[64,512]{1,0:T(8,128)(2,1)S(1)}, u32[]{:S(2)}, u32[]{:S(2)}) collective-permute-start(bf16[64,512]{1,0:T(8,128)(2,1)S(1)} %get-tuple-element.41), channel_id=1, source_target_pairs={{0,4},{4,8},{8,12},{12,0},{1,5},{5,9},{9,13},{13,1},{2,6},{6,10},{... | collective-permute-start | bytes 196616 | tf_op jit(solution)/shard_map/ppermute | solution.py:184
  92.9 9.7 %collective-permute-start.31 = (bf16[64,512]{1,0:T(8,128)(2,1)S(1)}, bf16[64,512]{1,0:T(8,128)(2,1)S(1)}, u32[]{:S(2)}, u32[]{:S(2)}) collective-permute-start(bf16[64,512]{1,0:T(8,128)(2,1)S(1)} %get-tuple-element.41), channel_id=1, source_target_pairs={{0,8},{4,12},{8,0},{12,4},{1,9},{5,13},{9,1},{13,5},{2,10},{6,14},... | collective-permute-start | bytes 196616 | tf_op jit(solution)/shard_map/ppermute | solution.py:184
  97.6 5.6 %collective-permute-start.32 = (bf16[64,512]{1,0:T(8,128)(2,1)S(1)}, bf16[64,512]{1,0:T(8,128)(2,1)S(1)}, u32[]{:S(2)}, u32[]{:S(2)}) collective-permute-start(bf16[64,512]{1,0:T(8,128)(2,1)S(1)} %get-tuple-element.41), channel_id=1, source_target_pairs={{0,12},{4,0},{8,4},{12,8},{1,13},{5,1},{9,5},{13,9},{2,14},{6,2},{... | collective-permute-start | bytes 196616 | tf_op jit(solution)/shard_map/ppermute | solution.py:184
  100.1 12.6 %collective-permute-start.17 = (bf16[256,512]{1,0:T(8,128)(2,1)S(1)}, bf16[256,512]{1,0:T(8,128)(2,1)S(1)}, u32[]{:S(2)}, u32[]{:S(2)}) collective-permute-start(bf16[256,512]{1,0:T(8,128)(2,1)S(1)} %shard_map.129.grown), channel_id=1, source_target_pairs={{0,2},{2,0},{1,3},{3,1},{4,6},{6,4},{5,7},{7,5},{8,10},{10,8},{9,1... | collective-permute-start | bytes 786440 | tf_op jit(solution)/shard_map/ppermute | solution.py:184
  102.7 9.4 %collective-permute-start.9 = (bf16[64,1536]{1,0:T(8,128)(2,1)S(1)}, bf16[64,1536]{1,0:T(8,128)(2,1)S(1)}, u32[]{:S(2)}, u32[]{:S(2)}) collective-permute-start(bf16[64,1536]{1,0:T(8,128)(2,1)S(1)} %get-tuple-element.35.mine), channel_id=1, source_target_pairs={{0,2},{2,0},{1,3},{3,1},{4,6},{6,4},{5,7},{7,5},{8,10},{10,8},{9,1... | collective-permute-start | bytes 589832 | tf_op jit(solution)/shard_map/ppermute | solution.py:184
  103.2 28.3 %collective-permute-start.29 = (bf16[256,1280]{1,0:T(8,128)(2,1)}, bf16[256,1280]{1,0:T(8,128)(2,1)S(1)}, u32[]{:S(2)}, u32[]{:S(2)}) collective-permute-start(bf16[256,1280]{1,0:T(8,128)(2,1)} %collective-permute-done.27.cross.refs_9_), channel_id=1, source_target_pairs={{0,1},{1,0},{2,3},{3,2},{4,5},{5,4},{6,7},{7,6},{8,9},{9,8},{10,11... | collective-permute-start | bytes 1966088 | tf_op jit(solution)/shard_map/ppermute | solution.py:184
  103.2 9.4 %collective-permute-start.18 = (bf16[256,512]{1,0:T(8,128)(2,1)S(1)}, bf16[256,512]{1,0:T(8,128)(2,1)S(1)}, u32[]{:S(2)}, u32[]{:S(2)}) collective-permute-start(bf16[256,512]{1,0:T(8,128)(2,1)S(1)} %shard_map.129.grown), channel_id=1, source_target_pairs={{0,1},{1,0},{2,3},{3,2},{4,5},{5,4},{6,7},{7,6},{8,9},{9,8},{10,11... | collective-permute-start | bytes 786440 | tf_op jit(solution)/shard_map/ppermute | solution.py:184
  112.1 6.9 %collective-permute-start.33 = (bf16[256,512]{1,0:T(8,128)(2,1)S(1)}, bf16[256,512]{1,0:T(8,128)(2,1)S(1)}, u32[]{:S(2)}, u32[]{:S(2)}) collective-permute-start(bf16[256,512]{1,0:T(8,128)(2,1)S(1)} %constant_dynamic-update-slice_fusion.early.refs_12_), channel_id=1, source_target_pairs={{0,2},{2,0},{1,3},{3,1},{4,6},{6,4},{5,7},{7,5},{8,10},{10,8},{9,1... | collective-permute-start | bytes 786440 | tf_op jit(solution)/shard_map/ppermute | solution.py:184
  112.6 6.4 %collective-permute-start.19 = (bf16[256,512]{1,0:T(8,128)(2,1)S(1)}, bf16[256,512]{1,0:T(8,128)(2,1)S(1)}, u32[]{:S(2)}, u32[]{:S(2)}) collective-permute-start(bf16[256,512]{1,0:T(8,128)(2,1)S(1)} %collective-permute-done.17.across), channel_id=1, source_target_pairs={{0,1},{1,0},{2,3},{3,2},{4,5},{5,4},{6,7},{7,6},{8,9},{9,8},{10,11... | collective-permute-start | bytes 786440 | tf_op jit(solution)/shard_map/ppermute | solution.py:184
  112.6 8.8 %collective-permute-start.34 = (bf16[256,512]{1,0:T(8,128)(2,1)S(1)}, bf16[256,512]{1,0:T(8,128)(2,1)S(1)}, u32[]{:S(2)}, u32[]{:S(2)}) collective-permute-start(bf16[256,512]{1,0:T(8,128)(2,1)S(1)} %constant_dynamic-update-slice_fusion.early.refs_12_), channel_id=1, source_target_pairs={{0,1},{1,0},{2,3},{3,2},{4,5},{5,4},{6,7},{7,6},{8,9},{9,8},{10,11... | collective-permute-start | bytes 786440 | tf_op jit(solution)/shard_map/ppermute | solution.py:184
  119.0 5.6 %collective-permute-start.35 = (bf16[256,512]{1,0:T(8,128)(2,1)S(1)}, bf16[256,512]{1,0:T(8,128)(2,1)S(1)}, u32[]{:S(2)}, u32[]{:S(2)}) collective-permute-start(bf16[256,512]{1,0:T(8,128)(2,1)S(1)} %collective-permute-done.33.early_cross.refs_13_), channel_id=1, source_target_pairs={{0,1},{1,0},{2,3},{3,2},{4,5},{5,4},{6,7},{7,6},{8,9},{9,8},{10,11... | collective-permute-start | bytes 786440 | tf_op jit(solution)/shard_map/ppermute | solution.py:184
  120.7 7.3 %collective-permute-start.20 = (bf16[64,640]{1,0:T(8,128)(2,1)S(1)}, bf16[64,640]{1,0:T(8,128)(2,1)S(1)}, u32[]{:S(2)}, u32[]{:S(2)}) collective-permute-start(bf16[64,640]{1,0:T(8,128)(2,1)S(1)} %shard_map.130.refs_0_), channel_id=1, source_target_pairs={{0,4},{4,8},{8,12},{12,0},{1,5},{5,9},{9,13},{13,1},{2,6},{6,10},{... | collective-permute-start | bytes 245768 | tf_op jit(solution)/shard_map/ppermute | solution.py:184
  121.5 9.6 %collective-permute-start.21 = (bf16[64,640]{1,0:T(8,128)(2,1)S(1)}, bf16[64,640]{1,0:T(8,128)(2,1)S(1)}, u32[]{:S(2)}, u32[]{:S(2)}) collective-permute-start(bf16[64,640]{1,0:T(8,128)(2,1)S(1)} %shard_map.130.refs_0_), channel_id=1, source_target_pairs={{0,8},{4,12},{8,0},{12,4},{1,9},{5,13},{9,1},{13,5},{2,10},{6,14},... | collective-permute-start | bytes 245768 | tf_op jit(solution)/shard_map/ppermute | solution.py:184
  122.2 8.8 %collective-permute-start.22 = (bf16[64,640]{1,0:T(8,128)(2,1)S(1)}, bf16[64,640]{1,0:T(8,128)(2,1)S(1)}, u32[]{:S(2)}, u32[]{:S(2)}) collective-permute-start(bf16[64,640]{1,0:T(8,128)(2,1)S(1)} %shard_map.130.refs_0_), channel_id=1, source_target_pairs={{0,12},{4,0},{8,4},{12,8},{1,13},{5,1},{9,5},{13,9},{2,14},{6,2},{... | collective-permute-start | bytes 245768 | tf_op jit(solution)/shard_map/ppermute | solution.py:184
  124.7 9.8 %collective-permute-start.23 = (bf16[64,640]{1,0:T(8,128)(2,1)S(1)}, bf16[64,640]{1,0:T(8,128)(2,1)S(1)}, u32[]{:S(2)}, u32[]{:S(2)}) collective-permute-start(bf16[64,640]{1,0:T(8,128)(2,1)S(1)} %shard_map.130.refs_0_), channel_id=1, source_target_pairs={{0,1},{1,0},{2,3},{3,2},{4,5},{5,4},{6,7},{7,6},{8,9},{9,8},{10,11... | collective-permute-start | bytes 245768 | tf_op jit(solution)/shard_map/ppermute | solution.py:184
  128.0 6.5 %collective-permute-start.24 = (bf16[64,640]{1,0:T(8,128)(2,1)S(1)}, bf16[64,640]{1,0:T(8,128)(2,1)S(1)}, u32[]{:S(2)}, u32[]{:S(2)}) collective-permute-start(bf16[64,640]{1,0:T(8,128)(2,1)S(1)} %collective-permute-done.20.refs_1_), channel_id=1, source_target_pairs={{0,1},{1,0},{2,3},{3,2},{4,5},{5,4},{6,7},{7,6},{8,9},{9,8},{10,11... | collective-permute-start | bytes 245768 | tf_op jit(solution)/shard_map/ppermute | solution.py:184
  131.0 3.4 %collective-permute-start.25 = (bf16[64,640]{1,0:T(8,128)(2,1)S(1)}, bf16[64,640]{1,0:T(8,128)(2,1)S(1)}, u32[]{:S(2)}, u32[]{:S(2)}) collective-permute-start(bf16[64,640]{1,0:T(8,128)(2,1)S(1)} %collective-permute-done.21.refs_2_), channel_id=1, source_target_pairs={{0,1},{1,0},{2,3},{3,2},{4,5},{5,4},{6,7},{7,6},{8,9},{9,8},{10,11... | collective-permute-start | bytes 245768 | tf_op jit(solution)/shard_map/ppermute | solution.py:184
  131.0 3.4 %collective-permute-start.26 = (bf16[64,640]{1,0:T(8,128)(2,1)S(1)}, bf16[64,640]{1,0:T(8,128)(2,1)S(1)}, u32[]{:S(2)}, u32[]{:S(2)}) collective-permute-start(bf16[64,640]{1,0:T(8,128)(2,1)S(1)} %collective-permute-done.22.refs_3_), channel_id=1, source_target_pairs={{0,1},{1,0},{2,3},{3,2},{4,5},{5,4},{6,7},{7,6},{8,9},{9,8},{10,11... | collective-permute-start | bytes 245768 | tf_op jit(solution)/shard_map/ppermute | solution.py:184

commit v3 on v2

--- a/solution.py
+++ b/solution.py
@@ -184,11 +184,23 @@
     return lax.ppermute(block, axis, [(i, (i + distance) % count) for i in range(count)])
 
 
+def flip(block, bit):
+    count = lax.axis_size("dp")
+    return lax.ppermute(block, "dp", [(i, i ^ bit) for i in range(count)])
+
+
+def low_bit(index):
+    return index & -index
+
+
+def sum_order(count):
+    return sorted(range(1, count), key=lambda r: (low_bit(r), -r))
+
+
 def swap(block, axis):
     return rotate(block, axis, 1)
 
 
-PREP_LIMIT = 60 * 1024 * 1024
 VMEM = pl.BlockSpec(memory_space=pltpu.VMEM)
 SMEM = pl.BlockSpec(memory_space=pltpu.SMEM)
 HBM = pl.BlockSpec(memory_space=pltpu.HBM)
@@ -233,45 +245,18 @@
     return copies
 
 
-def prep_body(count, place, hidden, unembed, value_proj, output_proj, gains, *refs):
-    f32, bf16 = jnp.float32, jnp.bfloat16
-    pieces, (ab, across, gain_out) = refs[:count], refs[count : count + 3]
-    held, value_held, output_held, sems = refs[count + 3 :]
-    first, dp_index, tensor_index = place[0] == 1, place[1], place[2]
-    rows, width = pieces[0].shape
-    half = output_proj.shape[0]
-    at = tile_at(tensor_index, rows)
-
-    def rows_from(source):
-        pairs = []
-        for d in range(count):
-            col = tile_at(lax.rem(dp_index + d, count), width)
-            pairs.append((source.at[at, col], held.at[d]))
-        return [pltpu.make_async_copy(*pair, sems.at[i]) for i, pair in enumerate(pairs)]
-
-    def start_rows(source):
-        for copy in rows_from(source):
-            copy.start()
-
-    loads = [
-        pltpu.make_async_copy(value_proj, value_held, sems.at[count]),
-        pltpu.make_async_copy(output_proj, output_held, sems.at[count + 1]),
-    ]
-    for load in loads:
-        load.start()
-    pl.when(first)(lambda: start_rows(hidden))
-    pl.when(jnp.logical_not(first))(lambda: start_rows(unembed))
-    gain = gains[:, tile_at(dp_index, width)]
-    gain_out[...] = gain
-    loads[0].wait()
-    scaled = (value_held[...].astype(f32).T * gain).astype(bf16)
-    loads[1].wait()
-    ab[:half, :] = scaled
-    ab[half:, :] = output_held[...]
-    across[...] = jnp.where(first, output_held[...], scaled)
-    for d, copy in enumerate(rows_from(hidden)):
-        copy.wait()
-        pieces[d][...] = held[d]
+def scaled_to(out, held, gain):
+    _, width = out.shape
+    step = width // 2 if width % 256 == 0 else width
+    for k in range(0, width, step):
+        block = held[k : k + step, :].astype(jnp.float32).T
+        out[:, k : k + step] = (block * gain[:, k : k + step]).astype(jnp.bfloat16)
+
+
+def own_body(place, value_proj, output_proj, gain, ab):
+    half, _ = output_proj.shape
+    scaled_to(ab.at[:half], value_proj, gain)
+    ab[half:, :] = output_proj[...]
 
 
 def column_body(
@@ -333,35 +318,30 @@
     cols[...] = out
 
 
-def product_body(count, place, ab, ab_other, c_own, *refs):
-    first, dp_index, group_index = place[0] == 1, place[1], place[3]
-    own_out, sends, scratch = refs[0], refs[1:-1], refs[-1]
+def product_body(place, ab, ab_other, c_own, own_out, send_out):
+    first, group_index = place[0] == 1, place[3]
     half = c_own.shape[0]
-    rows = scratch.shape[0]
-    at = tile_at(group_index, rows)
+    rows = own_out.shape[0]
     low = pl.ds(half + pl.multiple_of(group_index * rows, rows), rows)
-    left = jnp.where(first, ab[low, :], c_own[at, :])
+    left = jnp.where(first, ab[low, :], c_own[tile_at(group_index, rows), :])
     for k, source in enumerate((ab, ab_other)):
         right = jnp.where(first, source[half:, :], source[:half, :])
-        scratch[:, k * half : (k + 1) * half] = dot_nt(left, right)
-    step = rows // count
-    own_out[...] = scratch[tile_at(dp_index, step), :]
-    for d, send in enumerate(sends):
-        send[...] = scratch[tile_at(lax.rem(dp_index + d + 1, count), step), :].astype(jnp.bfloat16)
-
-
-def total_body(place, own, *refs):
+        product = dot_nt(left, right)
+        own_out[:, k * half : (k + 1) * half] = product
+        send_out[:, k * half : (k + 1) * half] = product.astype(jnp.bfloat16)
+
+
+def add_body(place, own, *refs):
     total = own[...]
     for ref in refs[:-1]:
         total = total + ref[...].astype(jnp.float32)
     refs[-1][...] = total.astype(jnp.bfloat16)
 
 
-def order_body(count, place, *refs):
-    dp_index, out = place[1], refs[-1]
-    step = refs[0].shape[0]
-    for d in range(count):
-        out[tile_at(lax.rem(dp_index + count - d, count), step), :] = refs[d][...]
+def total_body(place, own, other, total_out, send_out):
+    total = own[...] + other[...].astype(jnp.float32)
+    total_out[...] = total
+    send_out[...] = total.astype(jnp.bfloat16)
 
 
 def group_body(count, place, *refs):
@@ -386,8 +366,7 @@
 
 def stage_body(count, flag, *refs):
     pieces, (ab, ab_other, c_own, c_other) = refs[:count], refs[count : count + 4]
-    rows_out, own_out = refs[count + 4 : count + 6]
-    back_out = refs[count + 6 :]
+    rows_out, back_out = refs[count + 4], refs[count + 5 :]
     rows, half = pieces[0].shape[0], c_own.shape[0]
     for i, piece in enumerate(pieces):
         rows_out[i * rows : (i + 1) * rows, :] = piece[...]
@@ -402,9 +381,8 @@
     for k, (block, start) in enumerate(blocks):
         product = dot_nt(rows_out[...], block[start : start + half, :])
         cols = slice(k * half, (k + 1) * half)
-        own_out[:, cols] = product[:rows]
         for i, back in enumerate(back_out):
-            back[:, cols] = product[(i + 1) * rows : (i + 2) * rows].astype(jnp.bfloat16)
+            back[:, cols] = product[i * rows : (i + 1) * rows].astype(back.dtype)
 
 
 def value_body(
@@ -584,30 +562,41 @@
     unembed = unembed.reshape(resp_count * positions, model_width)
 
     def across_dp(block):
-        return [block] + [rotate(block, "dp", d) for d in shifts]
-
-    *pieces, ab, payload, gain = on_core(
-        functools.partial(prep_body, dp_count),
-        [shape_of(half_rows, own_width)] * dp_count
-        + [
-            shape_of(value_width, own_width),
-            shape_of(half_value, own_width),
-            shape_of(1, own_width, f32),
-        ],
-        [place, hidden, unembed, value_proj[0], output_proj[0], norm_gains],
-        half_rows * model_width,
-        8 * half_rows * model_width,
-        [
-            pltpu.VMEM((dp_count, half_rows, own_width), jnp.bfloat16),
-            pltpu.VMEM((own_width, half_value), jnp.bfloat16),
-            pltpu.VMEM((half_value, own_width), jnp.bfloat16),
-            pltpu.SemaphoreType.DMA((dp_count + 2,)),
-        ],
-        [HBM, HBM, HBM, HBM, VMEM],
-        limit=PREP_LIMIT,
+        held, bit = {0: block}, dp_count // 2
+        while bit:
+            for r in sorted(held):
+                held[r ^ bit] = flip(held[r], bit)
+            bit //= 2
+        return [held[r] for r in range(dp_count)]
+
+    first = lax.axis_index("section") == 0
+    dp_index = lax.axis_index("dp")
+    gain = lax.dynamic_slice_in_dim(norm_gains, dp_index * own_width, own_width, 1)
+    held = lax.optimization_barrier(value_proj)
+    payload = jnp.where(
+        first,
+        output_proj[0],
+        (held[0].astype(f32) * gain[0][:, None]).astype(jnp.bfloat16).T,
+    )
+
+    def piece(r):
+        at = (lax.axis_index("tensor") * half_rows, (dp_index ^ r) * own_width)
+        taken = [lax.dynamic_slice(a, at, (half_rows, own_width)) for a in (hidden, unembed)]
+        return jnp.where(first, *taken)
+
+    pieces = [piece(r) for r in range(dp_count)]
+    pieces, hidden, unembed, value_proj, output_proj = lax.optimization_barrier(
+        (pieces, hidden, unembed, value_proj, output_proj)
     )
     c_own = swap(payload, "section")
-    arrived = [pieces[0]] + [rotate(pieces[d], "dp", d) for d in shifts]
+    arrived = [pieces[0]] + [flip(pieces[r], r) for r in shifts]
+    (ab,) = on_core(
+        own_body,
+        [shape_of(value_width, own_width)],
+        [place, value_proj[0], output_proj[0], gain],
+        half_value * own_width,
+        8 * half_value * own_width,
+    )
     ab_other = swap(ab, "tensor")
     c_other = swap(c_own, "tensor")
     (cols,) = on_core(
@@ -621,53 +610,62 @@
             pltpu.SemaphoreType.DMA((2,)),
         ],
         [SMEM] * 4 + [HBM] * 2 + [VMEM] * 2,
-        limit=PREP_LIMIT,
-    )
-
-    rows_here, summed, *backs = on_core(
+    )
+
+    rows_here, *sums = on_core(
         functools.partial(stage_body, dp_count),
-        [shape_of(all_rows, own_width), shape_of(half_rows, 3 * value_width, f32)]
-        + [shape_of(half_rows, 3 * value_width) for d in shifts],
+        [shape_of(all_rows, own_width)]
+        + [
+            shape_of(half_rows, 3 * value_width, jnp.bfloat16 if r % 2 else f32)
+            for r in range(dp_count)
+        ],
         [place, *arrived, ab, ab_other, c_own, c_other],
         6 * all_rows * own_width * value_width,
         2 * (4 * value_width + 2 * all_rows) * own_width,
     )
-    backs = [rotate(backs[d - 1], "dp", -d) for d in shifts]
+    got = {r: [] for r in range(dp_count)}
+    for r in sum_order(dp_count):
+        sent = sums[r]
+        if got[r]:
+            (sent,) = on_core(
+                add_body,
+                [shape_of(half_rows, 3 * value_width)],
+                [place, sent, *got[r]],
+                3 * half_rows * value_width,
+                24 * half_rows * value_width,
+            )
+        got[r ^ low_bit(r)].append(flip(sent, low_bit(r)))
     mine, early = on_core(
         functools.partial(sum_body, model_width),
         [shape_of(half_rows, 3 * value_width), shape_of(half_rows, value_width)],
-        [place, cols, summed, *backs],
+        [place, cols, sums[0], *got[0]],
         9 * half_rows * value_width,
         24 * half_rows * value_width,
     )
     theirs = swap(mine, "section")
 
     part_rows = half_value // group_count
-    block_rows = part_rows // dp_count
-    own_part, *parts = on_core(
-        functools.partial(product_body, dp_count),
-        [shape_of(block_rows, value_width, f32)]
-        + [shape_of(block_rows, value_width) for d in shifts],
+    part_shapes = [shape_of(part_rows, value_width, f32), shape_of(part_rows, value_width)]
+    part, product = on_core(
+        product_body,
+        part_shapes,
         [place, ab, ab_other, c_own],
         2 * part_rows * own_width * value_width,
         4 * value_width * own_width,
-        [pltpu.VMEM((part_rows, value_width), f32)],
-    )
-    parts = [rotate(parts[d - 1], "dp", d) for d in shifts]
-    (total,) = on_core(
-        total_body,
-        [shape_of(block_rows, value_width)],
-        [place, own_part, *parts],
-        dp_count * block_rows * value_width,
-        4 * dp_count * block_rows * value_width,
-    )
-    (product,) = on_core(
-        functools.partial(order_body, dp_count),
-        [shape_of(part_rows, value_width)],
-        [place, *across_dp(total)],
-        part_rows * value_width,
-        4 * part_rows * value_width,
-    )
+    )
+    step = 1
+    while step < dp_count:
+        other = flip(product, step)
+        last = 2 * step >= dp_count
+        *kept, product = on_core(
+            add_body if last else total_body,
+            part_shapes[1:] if last else part_shapes,
+            [place, part, other],
+            part_rows * value_width,
+            12 * part_rows * value_width,
+        )
+        part = None if last else kept[0]
+        step *= 2
     (grown,) = on_core(
         functools.partial(group_body, group_count),
         [shape_of(half_value, value_width)],
@@ -735,7 +733,9 @@
         P(("groups", "dp"), None),
         P(("groups", "dp"), None),
     )
+    count = mesh.shape["dp"]
     two_by_two = mesh.shape["section"] == 2 and mesh.shape["tensor"] == 2
+    two_by_two = two_by_two and count & (count - 1) == 0
     return jax.shard_map(
         named if two_by_two else general,
         mesh=mesh,

time: 139 us -> 115 us (0.83)
  starting transfers between devices: 39.7 us -> 29.2 us
  waiting for transfers between devices: 69.8 us -> 61.9 us
  Pallas kernels: 22.6 us -> 15.8 us
  other arithmetic: 0.66 us -> 3.98 us
  local copies, waits for them, and re-layouts: 4.26 us -> 1.87 us
    ppermute x36 -> x18, waiting for transfers between devices: 69.8 us -> 25.4 us  [rotate(): lax.ppermute(block, axis, [(i, (i + distance) % count) for i in range(cou...]
    ppermute x0 -> x14, waiting for transfers between devices: none -> 36.5 us  [flip(): return lax.ppermute(block, 'dp', [(i, i ^ bit) for i in range(count)])]
    ppermute x36 -> x18, starting transfers between devices: 39.7 us -> 10.1 us  [rotate(): lax.ppermute(block, axis, [(i, (i + distance) % count) for i in range(cou...]
    ppermute x0 -> x14, starting transfers between devices: none -> 19.1 us  [flip(): return lax.ppermute(block, 'dp', [(i, i ^ bit) for i in range(count)])]
    pallas_call x11 -> x12, Pallas kernels: 22.6 us -> 15.8 us  [on_core(): pl.pallas_call(body, out_shape=outs, in_specs=[SMEM] + (specs or [VMEM] *...]
    unnamed x25 -> x27, local copies, waits for them, and re-layouts: 4.26 us -> 0.08 us
    select_n x0 -> x2, other arithmetic: none -> 3.9 us  [the longest x1 2.36 us: piece(): return jnp.where(first, *taken)]
  transfers between devices with their start and end apart: 36 -> 32, of which waited for: 15 -> 11; matrix products, arithmetic and copies ran while one was open for 0% -> 2% of each run, Pallas kernels for 9% -> 8%
where the time goes in v3:
time: 115 us; the launch traced here: 114 us
  waiting for transfers between devices  61.9 us (54%)
  starting transfers between devices  29.2 us (25%)
  Pallas kernels  15.8 us (14%)
  other arithmetic  3.98 us (3%)
  local copies, waits for them, and re-layouts  1.87 us (2%)
  between operations  1.63 us (1%)
    ppermute x14, waiting for transfers between devices, flip(): return lax.ppermute(block, 'dp', [(i, i ^ bit) for i in range(count)])  36.5 us
    ppermute x18, waiting for transfers between devices, rotate(): lax.ppermute(block, axis, [(i, (i + distance) % count) for i in range(cou...  25.4 us
    ppermute x14, starting transfers between devices, flip(): return lax.ppermute(block, 'dp', [(i, i ^ bit) for i in range(count)])  19.1 us
    pallas_call x12, Pallas kernels, on_core(): pl.pallas_call(body, out_shape=outs, in_specs=[SMEM] + (specs or [VMEM] *...  15.8 us
    ppermute x18, starting transfers between devices, rotate(): lax.ppermute(block, axis, [(i, (i + distance) % count) for i in range(cou...  10.1 us
    select_n x1, other arithmetic, piece(): return jnp.where(first, *taken)  2.36 us
  transfers between devices with their start and end apart: 32, of which 11 were waited for; matrix products, arithmetic and copies ran while one was open for 2% of the time, Pallas kernels for 8%

profile of v3, /device:TPU:0, one launch (start us, length us, event | category | flops | bytes accessed | tf_op | source)
XLA Modules:
  0.0 114.4 jit_solution(16112004392414303695)
XLA Ops:
  0.7 2.4 %dynamic-slice_select_fusion = (bf16[64,1280]{1,0:T(8,128)(2,1)}, bf16[64,1280]{1,0:T(8,128)(2,1)}, bf16[64,1280]{1,0:T(8,128)(2,1)}, bf16[64,1280]{1,0:T(8,128)(2,1)S(1)}) fusion(bf16[128,5120]{1,0:T(8,128)(2,1)} %bitcast.23, s32[]{:T(128)S(6)} %select_n.56, s32[]{:T(128)S(6)} %select_n.63, bf16[128,5120]{1,0:T(8,128)(2,1)} %bitcast.21, pred[]{:T(512)S(6)} %eq.4, ...), kind=kLoop, calls=%fused_computation.4 | loop fusion | flops 327680 | bytes 1966101 | tf_op jit(solution)/shard_map/jit(_where)/select_n | solution.py:585
  3.0 0.7 fusion.3
  3.8 0.1 pad_add_fusion.place.flag
  3.8 0.8 shard_map.123.refs_4_.ab
  4.6 0.6 collective-permute-start.3
  5.2 1.1 copy.13
  6.3 1.5 %fusion.2 = bf16[256,1280]{1,0:T(8,128)(2,1)S(1)} fusion(bf16[1,1280,256]{1,2,0:T(8,128)(2,1)} %copy.13, bf16[1,256,1280]{2,1,0:T(8,128)(2,1)} %param.14, f32[1280]{0:T(1024)S(1)} %get-tuple-element.50, pred[]{:T(512)S(6)} %eq.4), kind=kLoop, calls=%fused_computation.3 | loop fusion | flops 1310720 | bytes 1971201 | tf_op jit(solution)/shard_map/jit(_where)/select_n | solution.py:576
  7.8 2.6 %collective-permute-start.4 = (bf16[256,1280]{1,0:T(8,128)(2,1)S(1)}, bf16[256,1280]{1,0:T(8,128)(2,1)S(1)}, u32[]{:S(2)}, u32[]{:S(2)}) collective-permute-start(bf16[256,1280]{1,0:T(8,128)(2,1)S(1)} %fusion.2), channel_id=1, source_target_pairs={{0,2},{2,0},{1,3},{3,1},{4,6},{6,4},{5,7},{7,5},{8,10},{10,8},{9,1... | collective-permute-start | bytes 1966088 | tf_op jit(solution)/shard_map/ppermute | solution.py:184
  10.4 15.4 %collective-permute-done.4.refs_6_.c_own = bf16[256,1280]{1,0:T(8,128)(2,1)S(1)} collective-permute-done((bf16[256,1280]{1,0:T(8,128)(2,1)S(1)}, bf16[256,1280]{1,0:T(8,128)(2,1)S(1)}, u32[]{:S(2)}, u32[]{:S(2)}) %collective-permute-start.4) | collective-permute-done | bytes 655392 | tf_op jit(solution)/shard_map/ppermute | solution.py:184
  25.8 1.8 %collective-permute-start = (bf16[64,1280]{1,0:T(8,128)(2,1)S(1)}, bf16[64,1280]{1,0:T(8,128)(2,1)S(1)}, u32[]{:S(2)}, u32[]{:S(2)}) collective-permute-start(bf16[64,1280]{1,0:T(8,128)(2,1)S(1)} %copy-done.11), channel_id=1, source_target_pairs={{0,4},{4,0},{8,12},{12,8},{1,5},{5,1},{9,13},{13,9},{2,6},{6,2},{1... | collective-permute-start | bytes 491528 | tf_op jit(solution)/shard_map/ppermute | solution.py:189
  27.6 2.6 %collective-permute-start.1 = (bf16[64,1280]{1,0:T(8,128)(2,1)S(1)}, bf16[64,1280]{1,0:T(8,128)(2,1)S(1)}, u32[]{:S(2)}, u32[]{:S(2)}) collective-permute-start(bf16[64,1280]{1,0:T(8,128)(2,1)S(1)} %copy-done.10), channel_id=1, source_target_pairs={{0,8},{4,12},{8,0},{12,4},{1,9},{5,13},{9,1},{13,5},{2,10},{6,14},... | collective-permute-start | bytes 491528 | tf_op jit(solution)/shard_map/ppermute | solution.py:189
  30.2 5.3 %collective-permute-done.refs_1_ = bf16[64,1280]{1,0:T(8,128)(2,1)S(1)} collective-permute-done((bf16[64,1280]{1,0:T(8,128)(2,1)S(1)}, bf16[64,1280]{1,0:T(8,128)(2,1)S(1)}, u32[]{:S(2)}, u32[]{:S(2)}) %collective-permute-start) | collective-permute-done | bytes 163872 | tf_op jit(solution)/shard_map/ppermute | solution.py:189
  35.5 7.1 %collective-permute-done.1.refs_2_ = bf16[64,1280]{1,0:T(8,128)(2,1)S(1)} collective-permute-done((bf16[64,1280]{1,0:T(8,128)(2,1)S(1)}, bf16[64,1280]{1,0:T(8,128)(2,1)S(1)}, u32[]{:S(2)}, u32[]{:S(2)}) %collective-permute-start.1) | collective-permute-done | bytes 163872 | tf_op jit(solution)/shard_map/ppermute | solution.py:189
  42.7 1.8 %shard_map.124 = (bf16[256,1280]{1,0:T(8,128)(2,1)S(1)}, f32[64,1536]{1,0:T(8,128)S(1)}, bf16[64,1536]{1,0:T(8,128)(2,1)S(1)}, f32[64,1536]{1,0:T(8,128)S(1)}, bf16[64,1536]{1,0:T(8,128)(2,1)S(1)}) custom-call(s32[4]{0:T(128)S(1)} %pad_add_fusion.place.flag, bf16[64,1280]{1,0:T(8,128)(2,1)S(1)} %get-tuple-element.28.refs_0_, ...), custom_call_target="tpu_custom_call" | custom-call | flops 1006632960 | bytes 6553600 | tf_op jit(solution)/shard_map/pallas_call | solution.py:210
  44.4 1.6 %collective-permute-start.23 = (bf16[256,1280]{1,0:T(8,128)(2,1)S(1)}, bf16[256,1280]{1,0:T(8,128)(2,1)S(1)}, u32[]{:S(2)}, u32[]{:S(2)}) collective-permute-start(bf16[256,1280]{1,0:T(8,128)(2,1)S(1)} %get-tuple-element.43.own.refs_8_), channel_id=1, source_target_pairs={{0,2},{2,0},{1,3},{3,1},{4,6},{6,4},{5,7},{7,5},{8,10},{10,8},{9,1... | collective-permute-start | bytes 1966088 | tf_op jit(solution)/shard_map/ppermute | solution.py:184
  46.0 3.3 %collective-permute-start.7 = (bf16[64,1536]{1,0:T(8,128)(2,1)S(1)}, bf16[64,1536]{1,0:T(8,128)(2,1)S(1)}, u32[]{:S(2)}, u32[]{:S(2)}) collective-permute-start(bf16[64,1536]{1,0:T(8,128)(2,1)S(1)} %get-tuple-element.37), channel_id=1, source_target_pairs={{0,4},{4,0},{8,12},{12,8},{1,5},{5,1},{9,13},{13,9},{2,6},{6,2},{1... | collective-permute-start | bytes 589832 | tf_op jit(solution)/shard_map/ppermute | solution.py:189
  49.3 1.1 shard_map.127
  50.6 5.7 %collective-permute-done.10.other = bf16[128,512]{1,0:T(8,128)(2,1)S(1)} collective-permute-done((bf16[128,512]{1,0:T(8,128)(2,1)S(1)}, bf16[128,512]{1,0:T(8,128)(2,1)S(1)}, u32[]{:S(2)}, u32[]{:S(2)}) %collective-permute-start.10) | collective-permute-done | bytes 131104 | tf_op jit(solution)/shard_map/ppermute | solution.py:189
  56.3 0.6 shard_map.128
  56.9 2.8 %collective-permute-start.11 = (bf16[128,512]{1,0:T(8,128)(2,1)S(1)}, bf16[128,512]{1,0:T(8,128)(2,1)S(1)}, u32[]{:S(2)}, u32[]{:S(2)}) collective-permute-start(bf16[128,512]{1,0:T(8,128)(2,1)S(1)} %get-tuple-element.42), channel_id=1, source_target_pairs={{0,8},{4,12},{8,0},{12,4},{1,9},{5,13},{9,1},{13,5},{2,10},{6,14},... | collective-permute-start | bytes 393224 | tf_op jit(solution)/shard_map/ppermute | solution.py:189
  59.7 0.3 collective-permute-start.6
  60.0 0.6 shard_map.125
  60.5 1.7 %collective-permute-start.8 = (bf16[64,1536]{1,0:T(8,128)(2,1)S(1)}, bf16[64,1536]{1,0:T(8,128)(2,1)S(1)}, u32[]{:S(2)}, u32[]{:S(2)}) collective-permute-start(bf16[64,1536]{1,0:T(8,128)(2,1)S(1)} %shard_map.125), channel_id=1, source_target_pairs={{0,8},{4,12},{8,0},{12,4},{1,9},{5,13},{9,1},{13,5},{2,10},{6,14},... | collective-permute-start | bytes 589832 | tf_op jit(solution)/shard_map/ppermute | solution.py:189
  62.2 4.8 %collective-permute-done.11.refs_0_ = bf16[128,512]{1,0:T(8,128)(2,1)S(1)} collective-permute-done((bf16[128,512]{1,0:T(8,128)(2,1)S(1)}, bf16[128,512]{1,0:T(8,128)(2,1)S(1)}, u32[]{:S(2)}, u32[]{:S(2)}) %collective-permute-start.11) | collective-permute-done | bytes 131104 | tf_op jit(solution)/shard_map/ppermute | solution.py:189
  67.0 0.6 shard_map.129.refs_0_
  67.6 1.6 %collective-permute-start.12 = (bf16[128,512]{1,0:T(8,128)(2,1)S(1)}, bf16[128,512]{1,0:T(8,128)(2,1)S(1)}, u32[]{:S(2)}, u32[]{:S(2)}) collective-permute-start(bf16[128,512]{1,0:T(8,128)(2,1)S(1)} %shard_map.129.refs_0_), channel_id=1, source_target_pairs={{0,16},{16,0},{1,17},{17,1},{2,18},{18,2},{3,19},{19,3},{4,20},{20... | collective-permute-start | bytes 393224 | tf_op jit(solution)/shard_map/ppermute | solution.py:184
  69.9 1.6 %shard_map.122.cols = f32[64,128]{1,0:T(8,128)S(1)} custom-call(s32[4]{0:T(128)S(1)} %pad_add_fusion.place.flag, s32[16]{0:T(128)S(1)} %copy-done.6, s32[16]{0:T(128)S(1)} %copy-done.7, s32[1]{0:T(128)S(6)} %copy.17.survive, f32[16]{0:T(128)S(1)} %copy-done.8, bf16[128,5120]{1,0:T(8,128)(2,1)S(1)} %bitcast.22, bf16[128,5120]{1,0:T(8,128)(2,1)S(1)} %bitcast.24, ...), custom_call_target="tpu_custom_call" | custom-call | flops 327680 | bytes 1310720 | tf_op jit(solution)/shard_map/pallas_call | solution.py:210
  71.6 1.5 %collective-permute-done.8.refs_1_ = bf16[64,1536]{1,0:T(8,128)(2,1)S(1)} collective-permute-done((bf16[64,1536]{1,0:T(8,128)(2,1)S(1)}, bf16[64,1536]{1,0:T(8,128)(2,1)S(1)}, u32[]{:S(2)}, u32[]{:S(2)}) %collective-permute-start.8) | collective-permute-done | bytes 196640 | tf_op jit(solution)/shard_map/ppermute | solution.py:189
  73.1 0.6 shard_map.126
  73.8 3.0 %collective-permute-start.27 = (bf16[64,512]{1,0:T(8,128)(2,1)S(1)}, bf16[64,512]{1,0:T(8,128)(2,1)S(1)}, u32[]{:S(2)}, u32[]{:S(2)}) collective-permute-start(bf16[64,512]{1,0:T(8,128)(2,1)S(1)} %get-tuple-element.44), channel_id=1, source_target_pairs={{0,8},{4,12},{8,0},{12,4},{1,9},{5,13},{9,1},{13,5},{2,10},{6,14},... | collective-permute-start | bytes 196616 | tf_op jit(solution)/shard_map/ppermute | solution.py:189
  76.9 0.6 shard_map.130.grown
  77.4 0.6 collective-permute-start.13
  78.1 1.5 %collective-permute-start.9 = (bf16[64,1536]{1,0:T(8,128)(2,1)S(1)}, bf16[64,1536]{1,0:T(8,128)(2,1)S(1)}, u32[]{:S(2)}, u32[]{:S(2)}) collective-permute-start(bf16[64,1536]{1,0:T(8,128)(2,1)S(1)} %get-tuple-element.38.mine), channel_id=1, source_target_pairs={{0,2},{2,0},{1,3},{3,1},{4,6},{6,4},{5,7},{7,5},{8,10},{10,8},{9,1... | collective-permute-start | bytes 589832 | tf_op jit(solution)/shard_map/ppermute | solution.py:184
  79.6 1.4 %collective-permute-start.28 = (bf16[64,512]{1,0:T(8,128)(2,1)S(1)}, bf16[64,512]{1,0:T(8,128)(2,1)S(1)}, u32[]{:S(2)}, u32[]{:S(2)}) collective-permute-start(bf16[64,512]{1,0:T(8,128)(2,1)S(1)} %collective-permute-done.27), channel_id=1, source_target_pairs={{0,4},{4,0},{8,12},{12,8},{1,5},{5,1},{9,13},{13,9},{2,6},{6,2},{1... | collective-permute-start | bytes 196616 | tf_op jit(solution)/shard_map/ppermute | solution.py:189
  81.1 2.8 %collective-permute-done.28 = bf16[64,512]{1,0:T(8,128)(2,1)S(1)} collective-permute-done((bf16[64,512]{1,0:T(8,128)(2,1)S(1)}, bf16[64,512]{1,0:T(8,128)(2,1)S(1)}, u32[]{:S(2)}, u32[]{:S(2)}) %collective-permute-start.28) | collective-permute-done | bytes 65568 | tf_op jit(solution)/shard_map/ppermute | solution.py:189
  83.9 4.7 %collective-permute-done.9.theirs = bf16[64,1536]{1,0:T(8,128)(2,1)S(1)} collective-permute-done((bf16[64,1536]{1,0:T(8,128)(2,1)S(1)}, bf16[64,1536]{1,0:T(8,128)(2,1)S(1)}, u32[]{:S(2)}, u32[]{:S(2)}) %collective-permute-start.9) | collective-permute-done | bytes 196640 | tf_op jit(solution)/shard_map/ppermute | solution.py:184
  88.5 0.5 collective-permute-start.29
  89.1 0.5 collective-permute-start.30
  89.6 5.3 %collective-permute-done.29.early_cross.refs_13_ = bf16[256,512]{1,0:T(8,128)(2,1)S(1)} collective-permute-done((bf16[256,512]{1,0:T(8,128)(2,1)S(1)}, bf16[256,512]{1,0:T(8,128)(2,1)S(1)}, u32[]{:S(2)}, u32[]{:S(2)}) %collective-permute-start.29) | collective-permute-done | bytes 262176 | tf_op jit(solution)/shard_map/ppermute | solution.py:184
  94.9 1.7 %shard_map.131.refs_0_ = bf16[64,640]{1,0:T(8,128)(2,1)S(1)} custom-call(s32[4]{0:T(128)S(1)} %pad_add_fusion.place.flag, bf16[64,1536]{1,0:T(8,128)(2,1)S(1)} %get-tuple-element.38.mine, bf16[64,1536]{1,0:T(8,128)(2,1)S(1)} %collective-permute-done.9.theirs, bf16[256,512]{1,0:T(8,128)(2,1)S(1)} %shard_map.130.grown, ...), custom_call_target="tpu_custom_call" | custom-call | flops 100663296 | bytes 1048576 | tf_op jit(solution)/shard_map/pallas_call | solution.py:210
  96.6 0.3 collective-permute-start.17
  97.0 1.6 %collective-permute-start.16 = (bf16[64,640]{1,0:T(8,128)(2,1)S(1)}, bf16[64,640]{1,0:T(8,128)(2,1)S(1)}, u32[]{:S(2)}, u32[]{:S(2)}) collective-permute-start(bf16[64,640]{1,0:T(8,128)(2,1)S(1)} %shard_map.131.refs_0_), channel_id=1, source_target_pairs={{0,4},{4,0},{8,12},{12,8},{1,5},{5,1},{9,13},{13,9},{2,6},{6,2},{1... | collective-permute-start | bytes 245768 | tf_op jit(solution)/shard_map/ppermute | solution.py:189
  98.6 5.4 %collective-permute-done.17.refs_2_ = bf16[64,640]{1,0:T(8,128)(2,1)S(1)} collective-permute-done((bf16[64,640]{1,0:T(8,128)(2,1)S(1)}, bf16[64,640]{1,0:T(8,128)(2,1)S(1)}, u32[]{:S(2)}, u32[]{:S(2)}) %collective-permute-start.17) | collective-permute-done | bytes 81952 | tf_op jit(solution)/shard_map/ppermute | solution.py:189
  104.1 0.4 collective-permute-start.21
  104.5 0.1 collective-permute-start.20
  104.6 3.8 %collective-permute-done.18.refs_3_ = bf16[64,640]{1,0:T(8,128)(2,1)S(1)} collective-permute-done((bf16[64,640]{1,0:T(8,128)(2,1)S(1)}, bf16[64,640]{1,0:T(8,128)(2,1)S(1)}, u32[]{:S(2)}, u32[]{:S(2)}) %collective-permute-start.18) | collective-permute-done | bytes 81952 | tf_op jit(solution)/shard_map/ppermute | solution.py:189
  108.4 2.3 %shard_map.132 = (bf16[512,1280]{1,0:T(8,128)(2,1)S(1)}, bf16[512,1280]{1,0:T(8,128)(2,1)S(1)}, bf16[1280,512]{1,0:T(8,128)(2,1)S(1)}) custom-call(s32[4]{0:T(128)S(1)} %pad_add_fusion.place.flag, bf16[256,1280]{1,0:T(8,128)(2,1)S(1)} %get-tuple-element.43.own.refs_8_, bf16[256,1280]{1,0:T(8,128)(2,1)S(1)} %collective-permute-done.23.cross.refs_9_, ...), custom_call_target="tpu_custom_call" | custom-call | flops 1342177280 | bytes 5242880 | tf_op jit(solution)/shard_map/pallas_call | solution.py:210
  110.8 3.7 %shard_map.133 = (f32[1280,256]{1,0:T(8,128)}, f32[256,1280]{1,0:T(8,128)}) custom-call(s32[4]{0:T(128)S(1)} %pad_add_fusion.place.flag, bf16[64,640]{1,0:T(8,128)(2,1)S(1)} %shard_map.131.refs_0_, bf16[64,640]{1,0:T(8,128)(2,1)S(1)} %collective-permute-done.16.refs_1_, bf16[64,640]{1,0:T(8,128)(2,1)S(1)} %collective-permute-done.17.refs_2_, ...), custom_call_target="tpu_custom_call" | custom-call | flops 671088640 | bytes 7864320 | tf_op jit(solution)/shard_map/pallas_call | solution.py:210
  (61 shorter events, 0.6 us)
Async XLA Ops:
  0.6 3.2 %copy-start.2 = (bf16[1,1280,256]{2,1,0:T(8,128)(2,1)S(1)}, bf16[1,1280,256]{2,1,0:T(8,128)(2,1)}, u32[]{:S(2)}) copy-start(bf16[1,1280,256]{2,1,0:T(8,128)(2,1)} %param.13) | copy-start | bytes 1966084
  0.6 3.2 %copy-start.3 = (bf16[1,256,1280]{2,1,0:T(8,128)(2,1)S(1)}, bf16[1,256,1280]{2,1,0:T(8,128)(2,1)}, u32[]{:S(2)}) copy-start(bf16[1,256,1280]{2,1,0:T(8,128)(2,1)} %param.14) | copy-start | bytes 1966084
  4.6 38.0 %collective-permute-start.3 = (bf16[512,1280]{1,0:T(8,128)(2,1)S(1)}, bf16[512,1280]{1,0:T(8,128)(2,1)S(1)}, u32[]{:S(2)}, u32[]{:S(2)}) collective-permute-start(bf16[512,1280]{1,0:T(8,128)(2,1)S(1)} %shard_map.123.refs_4_.ab), channel_id=1, source_target_pairs={{0,1},{1,0},{2,3},{3,2},{4,5},{5,4},{6,7},{7,6},{8,9},{9,8},{10,11... | collective-permute-start | bytes 3932168 | tf_op jit(solution)/shard_map/ppermute | solution.py:184
  6.3 19.5 %copy-start.11 = (bf16[64,1280]{1,0:T(8,128)(2,1)S(1)}, bf16[64,1280]{1,0:T(8,128)(2,1)}, u32[]{:S(2)}) copy-start(bf16[64,1280]{1,0:T(8,128)(2,1)} %get-tuple-element.29) | copy-start | bytes 491524
  6.3 21.3 %copy-start.10 = (bf16[64,1280]{1,0:T(8,128)(2,1)S(1)}, bf16[64,1280]{1,0:T(8,128)(2,1)}, u32[]{:S(2)}) copy-start(bf16[64,1280]{1,0:T(8,128)(2,1)} %get-tuple-element.30) | copy-start | bytes 491524
  6.3 23.9 %copy-start.9 = (bf16[64,1280]{1,0:T(8,128)(2,1)S(1)}, bf16[64,1280]{1,0:T(8,128)(2,1)}, u32[]{:S(2)}) copy-start(bf16[64,1280]{1,0:T(8,128)(2,1)} %get-tuple-element.31) | copy-start | bytes 491524
  7.8 17.9 %collective-permute-start.4 = (bf16[256,1280]{1,0:T(8,128)(2,1)S(1)}, bf16[256,1280]{1,0:T(8,128)(2,1)S(1)}, u32[]{:S(2)}, u32[]{:S(2)}) collective-permute-start(bf16[256,1280]{1,0:T(8,128)(2,1)S(1)} %fusion.2), channel_id=1, source_target_pairs={{0,2},{2,0},{1,3},{3,1},{4,6},{6,4},{5,7},{7,5},{8,10},{10,8},{9,1... | collective-permute-start | bytes 1966088 | tf_op jit(solution)/shard_map/ppermute | solution.py:184
  25.8 16.9 %collective-permute-start.5 = (bf16[256,1280]{1,0:T(8,128)(2,1)S(1)}, bf16[256,1280]{1,0:T(8,128)(2,1)S(1)}, u32[]{:S(2)}, u32[]{:S(2)}) collective-permute-start(bf16[256,1280]{1,0:T(8,128)(2,1)S(1)} %collective-permute-done.4.refs_6_.c_own), channel_id=1, source_target_pairs={{0,1},{1,0},{2,3},{3,2},{4,5},{5,4},{6,7},{7,6},{8,9},{9,8},{10,11... | collective-permute-start | bytes 1966088 | tf_op jit(solution)/shard_map/ppermute | solution.py:184
  25.8 9.8 %collective-permute-start = (bf16[64,1280]{1,0:T(8,128)(2,1)S(1)}, bf16[64,1280]{1,0:T(8,128)(2,1)S(1)}, u32[]{:S(2)}, u32[]{:S(2)}) collective-permute-start(bf16[64,1280]{1,0:T(8,128)(2,1)S(1)} %copy-done.11), channel_id=1, source_target_pairs={{0,4},{4,0},{8,12},{12,8},{1,5},{5,1},{9,13},{13,9},{2,6},{6,2},{1... | collective-permute-start | bytes 491528 | tf_op jit(solution)/shard_map/ppermute | solution.py:189
  27.6 15.0 %collective-permute-start.1 = (bf16[64,1280]{1,0:T(8,128)(2,1)S(1)}, bf16[64,1280]{1,0:T(8,128)(2,1)S(1)}, u32[]{:S(2)}, u32[]{:S(2)}) collective-permute-start(bf16[64,1280]{1,0:T(8,128)(2,1)S(1)} %copy-done.10), channel_id=1, source_target_pairs={{0,8},{4,12},{8,0},{12,4},{1,9},{5,13},{9,1},{13,5},{2,10},{6,14},... | collective-permute-start | bytes 491528 | tf_op jit(solution)/shard_map/ppermute | solution.py:189
  30.2 12.5 %collective-permute-start.2 = (bf16[64,1280]{1,0:T(8,128)(2,1)S(1)}, bf16[64,1280]{1,0:T(8,128)(2,1)S(1)}, u32[]{:S(2)}, u32[]{:S(2)}) collective-permute-start(bf16[64,1280]{1,0:T(8,128)(2,1)S(1)} %copy-done.9), channel_id=1, source_target_pairs={{0,12},{4,8},{8,4},{12,0},{1,13},{5,9},{9,5},{13,1},{2,14},{6,10},... | collective-permute-start | bytes 491528 | tf_op jit(solution)/shard_map/ppermute | solution.py:189
  44.4 36.6 %collective-permute-start.23 = (bf16[256,1280]{1,0:T(8,128)(2,1)S(1)}, bf16[256,1280]{1,0:T(8,128)(2,1)S(1)}, u32[]{:S(2)}, u32[]{:S(2)}) collective-permute-start(bf16[256,1280]{1,0:T(8,128)(2,1)S(1)} %get-tuple-element.43.own.refs_8_), channel_id=1, source_target_pairs={{0,2},{2,0},{1,3},{3,1},{4,6},{6,4},{5,7},{7,5},{8,10},{10,8},{9,1... | collective-permute-start | bytes 1966088 | tf_op jit(solution)/shard_map/ppermute | solution.py:184
  46.0 14.0 %collective-permute-start.7 = (bf16[64,1536]{1,0:T(8,128)(2,1)S(1)}, bf16[64,1536]{1,0:T(8,128)(2,1)S(1)}, u32[]{:S(2)}, u32[]{:S(2)}) collective-permute-start(bf16[64,1536]{1,0:T(8,128)(2,1)S(1)} %get-tuple-element.37), channel_id=1, source_target_pairs={{0,4},{4,0},{8,12},{12,8},{1,5},{5,1},{9,13},{13,9},{2,6},{6,2},{1... | collective-permute-start | bytes 589832 | tf_op jit(solution)/shard_map/ppermute | solution.py:189
  49.3 20.5 %copy-start.1 = (bf16[16,8,5120]{2,1,0:T(8,128)(2,1)S(1)}, bf16[16,8,5120]{2,1,0:T(8,128)(2,1)}, u32[]{:S(2)}) copy-start(bf16[16,8,5120]{2,1,0:T(8,128)(2,1)} %param.12) | copy-start | bytes 3932164
  50.4 19.4 %copy-start = (bf16[16,8,5120]{2,1,0:T(8,128)(2,1)S(1)}, bf16[16,8,5120]{2,1,0:T(8,128)(2,1)}, u32[]{:S(2)}) copy-start(bf16[16,8,5120]{2,1,0:T(8,128)(2,1)} %param.11) | copy-start | bytes 3932164
  50.4 19.4 %copy-start.4 = (f32[16,8]{0,1:T(8,128)S(1)}, f32[16,8]{0,1:T(8,128)}, u32[]{:S(2)}) copy-start(f32[16,8]{0,1:T(8,128)} %param.20) | copy-start | bytes 1540
  50.4 19.4 %copy-start.5 = (f32[16,8]{0,1:T(8,128)S(1)}, f32[16,8]{0,1:T(8,128)}, u32[]{:S(2)}) copy-start(f32[16,8]{0,1:T(8,128)} %param.21) | copy-start | bytes 1540
  50.5 19.4 %copy-start.6 = (s32[16]{0:T(128)S(1)}, s32[16]{0:T(128)}, u32[]{:S(2)}) copy-start(s32[16]{0:T(128)} %lengths.1) | copy-start | bytes 196
  50.5 19.4 %copy-start.7 = (s32[16]{0:T(128)S(1)}, s32[16]{0:T(128)}, u32[]{:S(2)}) copy-start(s32[16]{0:T(128)} %assign.1) | copy-start | bytes 196
  50.5 19.4 %copy-start.8 = (f32[16]{0:T(128)S(1)}, f32[16]{0:T(128)}, u32[]{:S(2)}) copy-start(f32[16]{0:T(128)} %advantage.1) | copy-start | bytes 196
  50.5 5.8 %collective-permute-start.10 = (bf16[128,512]{1,0:T(8,128)(2,1)S(1)}, bf16[128,512]{1,0:T(8,128)(2,1)S(1)}, u32[]{:S(2)}, u32[]{:S(2)}) collective-permute-start(bf16[128,512]{1,0:T(8,128)(2,1)S(1)} %get-tuple-element.40), channel_id=1, source_target_pairs={{0,4},{4,0},{8,12},{12,8},{1,5},{5,1},{9,13},{13,9},{2,6},{6,2},{1... | collective-permute-start | bytes 393224 | tf_op jit(solution)/shard_map/ppermute | solution.py:189
  56.9 10.2 %collective-permute-start.11 = (bf16[128,512]{1,0:T(8,128)(2,1)S(1)}, bf16[128,512]{1,0:T(8,128)(2,1)S(1)}, u32[]{:S(2)}, u32[]{:S(2)}) collective-permute-start(bf16[128,512]{1,0:T(8,128)(2,1)S(1)} %get-tuple-element.42), channel_id=1, source_target_pairs={{0,8},{4,12},{8,0},{12,4},{1,9},{5,13},{9,1},{13,5},{2,10},{6,14},... | collective-permute-start | bytes 393224 | tf_op jit(solution)/shard_map/ppermute | solution.py:189
  59.7 11.9 %collective-permute-start.6 = (bf16[64,1536]{1,0:T(8,128)(2,1)S(1)}, bf16[64,1536]{1,0:T(8,128)(2,1)S(1)}, u32[]{:S(2)}, u32[]{:S(2)}) collective-permute-start(bf16[64,1536]{1,0:T(8,128)(2,1)S(1)} %get-tuple-element.35), channel_id=1, source_target_pairs={{0,4},{4,0},{8,12},{12,8},{1,5},{5,1},{9,13},{13,9},{2,6},{6,2},{1... | collective-permute-start | bytes 589832 | tf_op jit(solution)/shard_map/ppermute | solution.py:189
  60.5 12.6 %collective-permute-start.8 = (bf16[64,1536]{1,0:T(8,128)(2,1)S(1)}, bf16[64,1536]{1,0:T(8,128)(2,1)S(1)}, u32[]{:S(2)}, u32[]{:S(2)}) collective-permute-start(bf16[64,1536]{1,0:T(8,128)(2,1)S(1)} %shard_map.125), channel_id=1, source_target_pairs={{0,8},{4,12},{8,0},{12,4},{1,9},{5,13},{9,1},{13,5},{2,10},{6,14},... | collective-permute-start | bytes 589832 | tf_op jit(solution)/shard_map/ppermute | solution.py:189
  67.6 9.3 %collective-permute-start.12 = (bf16[128,512]{1,0:T(8,128)(2,1)S(1)}, bf16[128,512]{1,0:T(8,128)(2,1)S(1)}, u32[]{:S(2)}, u32[]{:S(2)}) collective-permute-start(bf16[128,512]{1,0:T(8,128)(2,1)S(1)} %shard_map.129.refs_0_), channel_id=1, source_target_pairs={{0,16},{16,0},{1,17},{17,1},{2,18},{18,2},{3,19},{19,3},{4,20},{20... | collective-permute-start | bytes 393224 | tf_op jit(solution)/shard_map/ppermute | solution.py:184
  71.5 25.5 %collective-permute-start.24 = (bf16[256,1280]{1,0:T(8,128)(2,1)S(1)}, bf16[256,1280]{1,0:T(8,128)(2,1)S(1)}, u32[]{:S(2)}, u32[]{:S(2)}) collective-permute-start(bf16[256,1280]{1,0:T(8,128)(2,1)S(1)} %get-tuple-element.43.own.refs_8_), channel_id=1, source_target_pairs={{0,1},{1,0},{2,3},{3,2},{4,5},{5,4},{6,7},{7,6},{8,9},{9,8},{10,11... | collective-permute-start | bytes 1966088 | tf_op jit(solution)/shard_map/ppermute | solution.py:184
  73.8 4.3 %collective-permute-start.26 = (bf16[64,512]{1,0:T(8,128)(2,1)S(1)}, bf16[64,512]{1,0:T(8,128)(2,1)S(1)}, u32[]{:S(2)}, u32[]{:S(2)}) collective-permute-start(bf16[64,512]{1,0:T(8,128)(2,1)S(1)} %get-tuple-element.44), channel_id=1, source_target_pairs={{0,4},{4,0},{8,12},{12,8},{1,5},{5,1},{9,13},{13,9},{2,6},{6,2},{1... | collective-permute-start | bytes 196616 | tf_op jit(solution)/shard_map/ppermute | solution.py:189
  73.8 5.8 %collective-permute-start.27 = (bf16[64,512]{1,0:T(8,128)(2,1)S(1)}, bf16[64,512]{1,0:T(8,128)(2,1)S(1)}, u32[]{:S(2)}, u32[]{:S(2)}) collective-permute-start(bf16[64,512]{1,0:T(8,128)(2,1)S(1)} %get-tuple-element.44), channel_id=1, source_target_pairs={{0,8},{4,12},{8,0},{12,4},{1,9},{5,13},{9,1},{13,5},{2,10},{6,14},... | collective-permute-start | bytes 196616 | tf_op jit(solution)/shard_map/ppermute | solution.py:189
  77.4 11.6 %collective-permute-start.13 = (bf16[256,512]{1,0:T(8,128)(2,1)S(1)}, bf16[256,512]{1,0:T(8,128)(2,1)S(1)}, u32[]{:S(2)}, u32[]{:S(2)}) collective-permute-start(bf16[256,512]{1,0:T(8,128)(2,1)S(1)} %shard_map.130.grown), channel_id=1, source_target_pairs={{0,2},{2,0},{1,3},{3,1},{4,6},{6,4},{5,7},{7,5},{8,10},{10,8},{9,1... | collective-permute-start | bytes 786440 | tf_op jit(solution)/shard_map/ppermute | solution.py:184
  78.1 10.5 %collective-permute-start.9 = (bf16[64,1536]{1,0:T(8,128)(2,1)S(1)}, bf16[64,1536]{1,0:T(8,128)(2,1)S(1)}, u32[]{:S(2)}, u32[]{:S(2)}) collective-permute-start(bf16[64,1536]{1,0:T(8,128)(2,1)S(1)} %get-tuple-element.38.mine), channel_id=1, source_target_pairs={{0,2},{2,0},{1,3},{3,1},{4,6},{6,4},{5,7},{7,5},{8,10},{10,8},{9,1... | collective-permute-start | bytes 589832 | tf_op jit(solution)/shard_map/ppermute | solution.py:184
  79.6 4.3 %collective-permute-start.28 = (bf16[64,512]{1,0:T(8,128)(2,1)S(1)}, bf16[64,512]{1,0:T(8,128)(2,1)S(1)}, u32[]{:S(2)}, u32[]{:S(2)}) collective-permute-start(bf16[64,512]{1,0:T(8,128)(2,1)S(1)} %collective-permute-done.27), channel_id=1, source_target_pairs={{0,4},{4,0},{8,12},{12,8},{1,5},{5,1},{9,13},{13,9},{2,6},{6,2},{1... | collective-permute-start | bytes 196616 | tf_op jit(solution)/shard_map/ppermute | solution.py:189
  81.0 27.4 %collective-permute-start.25 = (bf16[256,1280]{1,0:T(8,128)(2,1)S(1)}, bf16[256,1280]{1,0:T(8,128)(2,1)S(1)}, u32[]{:S(2)}, u32[]{:S(2)}) collective-permute-start(bf16[256,1280]{1,0:T(8,128)(2,1)S(1)} %collective-permute-done.23.cross.refs_9_), channel_id=1, source_target_pairs={{0,1},{1,0},{2,3},{3,2},{4,5},{5,4},{6,7},{7,6},{8,9},{9,8},{10,11... | collective-permute-start | bytes 1966088 | tf_op jit(solution)/shard_map/ppermute | solution.py:184
  83.9 5.2 %collective-permute-start.14 = (bf16[256,512]{1,0:T(8,128)(2,1)S(1)}, bf16[256,512]{1,0:T(8,128)(2,1)S(1)}, u32[]{:S(2)}, u32[]{:S(2)}) collective-permute-start(bf16[256,512]{1,0:T(8,128)(2,1)S(1)} %shard_map.130.grown), channel_id=1, source_target_pairs={{0,1},{1,0},{2,3},{3,2},{4,5},{5,4},{6,7},{7,6},{8,9},{9,8},{10,11... | collective-permute-start | bytes 786440 | tf_op jit(solution)/shard_map/ppermute | solution.py:184
  88.5 6.4 %collective-permute-start.29 = (bf16[256,512]{1,0:T(8,128)(2,1)S(1)}, bf16[256,512]{1,0:T(8,128)(2,1)S(1)}, u32[]{:S(2)}, u32[]{:S(2)}) collective-permute-start(bf16[256,512]{1,0:T(8,128)(2,1)S(1)} %constant_dynamic-update-slice_fusion.early.refs_12_), channel_id=1, source_target_pairs={{0,2},{2,0},{1,3},{3,1},{4,6},{6,4},{5,7},{7,5},{8,10},{10,8},{9,1... | collective-permute-start | bytes 786440 | tf_op jit(solution)/shard_map/ppermute | solution.py:184
  89.1 5.9 %collective-permute-start.15 = (bf16[256,512]{1,0:T(8,128)(2,1)S(1)}, bf16[256,512]{1,0:T(8,128)(2,1)S(1)}, u32[]{:S(2)}, u32[]{:S(2)}) collective-permute-start(bf16[256,512]{1,0:T(8,128)(2,1)S(1)} %collective-permute-done.13.across), channel_id=1, source_target_pairs={{0,1},{1,0},{2,3},{3,2},{4,5},{5,4},{6,7},{7,6},{8,9},{9,8},{10,11... | collective-permute-start | bytes 786440 | tf_op jit(solution)/shard_map/ppermute | solution.py:184
  89.1 14.9 %collective-permute-start.30 = (bf16[256,512]{1,0:T(8,128)(2,1)S(1)}, bf16[256,512]{1,0:T(8,128)(2,1)S(1)}, u32[]{:S(2)}, u32[]{:S(2)}) collective-permute-start(bf16[256,512]{1,0:T(8,128)(2,1)S(1)} %constant_dynamic-update-slice_fusion.early.refs_12_), channel_id=1, source_target_pairs={{0,1},{1,0},{2,3},{3,2},{4,5},{5,4},{6,7},{7,6},{8,9},{9,8},{10,11... | collective-permute-start | bytes 786440 | tf_op jit(solution)/shard_map/ppermute | solution.py:184
  94.9 9.6 %collective-permute-start.31 = (bf16[256,512]{1,0:T(8,128)(2,1)S(1)}, bf16[256,512]{1,0:T(8,128)(2,1)S(1)}, u32[]{:S(2)}, u32[]{:S(2)}) collective-permute-start(bf16[256,512]{1,0:T(8,128)(2,1)S(1)} %collective-permute-done.29.early_cross.refs_13_), channel_id=1, source_target_pairs={{0,1},{1,0},{2,3},{3,2},{4,5},{5,4},{6,7},{7,6},{8,9},{9,8},{10,11... | collective-permute-start | bytes 786440 | tf_op jit(solution)/shard_map/ppermute | solution.py:184
  96.6 7.4 %collective-permute-start.17 = (bf16[64,640]{1,0:T(8,128)(2,1)S(1)}, bf16[64,640]{1,0:T(8,128)(2,1)S(1)}, u32[]{:S(2)}, u32[]{:S(2)}) collective-permute-start(bf16[64,640]{1,0:T(8,128)(2,1)S(1)} %shard_map.131.refs_0_), channel_id=1, source_target_pairs={{0,8},{4,12},{8,0},{12,4},{1,9},{5,13},{9,1},{13,5},{2,10},{6,14},... | collective-permute-start | bytes 245768 | tf_op jit(solution)/shard_map/ppermute | solution.py:189
  97.0 7.1 %collective-permute-start.16 = (bf16[64,640]{1,0:T(8,128)(2,1)S(1)}, bf16[64,640]{1,0:T(8,128)(2,1)S(1)}, u32[]{:S(2)}, u32[]{:S(2)}) collective-permute-start(bf16[64,640]{1,0:T(8,128)(2,1)S(1)} %shard_map.131.refs_0_), channel_id=1, source_target_pairs={{0,4},{4,0},{8,12},{12,8},{1,5},{5,1},{9,13},{13,9},{2,6},{6,2},{1... | collective-permute-start | bytes 245768 | tf_op jit(solution)/shard_map/ppermute | solution.py:189
  104.0 4.4 %collective-permute-start.18 = (bf16[64,640]{1,0:T(8,128)(2,1)S(1)}, bf16[64,640]{1,0:T(8,128)(2,1)S(1)}, u32[]{:S(2)}, u32[]{:S(2)}) collective-permute-start(bf16[64,640]{1,0:T(8,128)(2,1)S(1)} %collective-permute-done.17.refs_2_), channel_id=1, source_target_pairs={{0,4},{4,0},{8,12},{12,8},{1,5},{5,1},{9,13},{13,9},{2,6},{6,2},{1... | collective-permute-start | bytes 245768 | tf_op jit(solution)/shard_map/ppermute | solution.py:189
  104.0 6.8 %collective-permute-start.19 = (bf16[64,640]{1,0:T(8,128)(2,1)S(1)}, bf16[64,640]{1,0:T(8,128)(2,1)S(1)}, u32[]{:S(2)}, u32[]{:S(2)}) collective-permute-start(bf16[64,640]{1,0:T(8,128)(2,1)S(1)} %shard_map.131.refs_0_), channel_id=1, source_target_pairs={{0,1},{1,0},{2,3},{3,2},{4,5},{5,4},{6,7},{7,6},{8,9},{9,8},{10,11... | collective-permute-start | bytes 245768 | tf_op jit(solution)/shard_map/ppermute | solution.py:184
  104.1 6.7 %collective-permute-start.21 = (bf16[64,640]{1,0:T(8,128)(2,1)S(1)}, bf16[64,640]{1,0:T(8,128)(2,1)S(1)}, u32[]{:S(2)}, u32[]{:S(2)}) collective-permute-start(bf16[64,640]{1,0:T(8,128)(2,1)S(1)} %collective-permute-done.17.refs_2_), channel_id=1, source_target_pairs={{0,1},{1,0},{2,3},{3,2},{4,5},{5,4},{6,7},{7,6},{8,9},{9,8},{10,11... | collective-permute-start | bytes 245768 | tf_op jit(solution)/shard_map/ppermute | solution.py:184
  104.5 6.2 %collective-permute-start.20 = (bf16[64,640]{1,0:T(8,128)(2,1)S(1)}, bf16[64,640]{1,0:T(8,128)(2,1)S(1)}, u32[]{:S(2)}, u32[]{:S(2)}) collective-permute-start(bf16[64,640]{1,0:T(8,128)(2,1)S(1)} %collective-permute-done.16.refs_1_), channel_id=1, source_target_pairs={{0,1},{1,0},{2,3},{3,2},{4,5},{5,4},{6,7},{7,6},{8,9},{9,8},{10,11... | collective-permute-start | bytes 245768 | tf_op jit(solution)/shard_map/ppermute | solution.py:184
  108.4 2.4 %collective-permute-start.22 = (bf16[64,640]{1,0:T(8,128)(2,1)S(1)}, bf16[64,640]{1,0:T(8,128)(2,1)S(1)}, u32[]{:S(2)}, u32[]{:S(2)}) collective-permute-start(bf16[64,640]{1,0:T(8,128)(2,1)S(1)} %collective-permute-done.18.refs_3_), channel_id=1, source_target_pairs={{0,1},{1,0},{2,3},{3,2},{4,5},{5,4},{6,7},{7,6},{8,9},{9,8},{10,11... | collective-permute-start | bytes 245768 | tf_op jit(solution)/shard_map/ppermute | solution.py:184
